TPU v7x, 32 devices: a whole 2x2x4 slice. The times are simulated.
32 devices in a mesh: groups: 1, section: 2 (over x), axial: 16 (over z, y, core).
Axes of the slice: x: 2, y: 2, z: 4, core: 2. Of those that a mesh axis runs over, the one named last changes fastest.
Arguments:
- pair_in: bfloat16 [4, 128, 128, 128], P('groups', 'axial'), may hold values from -6 to 6
- crop_mask: int32 [4, 128], P('groups'), may hold values 0 or 1
- proj_weights: bfloat16 [2, 5, 128, 128], P('section'), may hold values from -0.5 to 0.5
- out_weights: bfloat16 [2, 128, 128], P('section'), may hold values from -0.5 to 0.5
- up_weights: bfloat16 [2, 128, 512], P('section'), may hold values from -0.5 to 0.5
- down_weights: bfloat16 [2, 512, 128], P('section'), may hold values from -0.25 to 0.25
- norm_gains: bfloat16 [2, 3, 128], P('section'), may hold values from 0.099609375 to 1.8984375
Outputs:
- pair_out: bfloat16 [4, 128, 128, 128], P(('groups', 'section'), 'axial')
Inputs may be any that keep to these rules, and one draw needn't show every extreme that they name: `crop_mask`: 1 marks a residue inside the crop, 0 a padded one.
All inputs are finite; a program needn't handle non-finite values.
Results may differ from a plain program's by a relative error of at most 0.013.
Values may be sent and summed in bfloat16 or wider, within the bound.
No kernel may reach another device: no remote copies, remote signals or barrier semaphores. Data moves between devices by JAX's collectives and lax.ppermute only.
A program may use at most 64 MiB of HBM per device.

v0:
```python
import functools

import jax
import jax.numpy as jnp
from jax import lax
from jax.experimental import pallas as pl
from jax.experimental.pallas import tpu as pltpu
from jax.sharding import PartitionSpec as P


epsilon = 1e-05
LANES = 128
TOGETHER = 1024
VMEM_BYTES = 48 * 1024 * 1024


def sigmoid(x):
    return 0.5 * jnp.tanh(0.5 * x) + 0.5


def normalize(values):
    count = values.shape[0]
    center = values - jnp.sum(values, axis=0, keepdims=True) * (1.0 / count)
    spread = jnp.sum(center * center, axis=0, keepdims=True) * (1.0 / count)
    return center * lax.rsqrt(spread + epsilon)


def matmul(a, b):
    return jnp.dot(a, b, preferred_element_type=jnp.float32)


def side_by_side(pieces):
    return pieces[0] if len(pieces) == 1 else jnp.concatenate(pieces, axis=1)


def put_rows(scratch, first, rows, values):
    tiles = scratch.shape[0]
    for place in range(values.shape[1] // LANES):
        scratch[place % tiles, pl.ds(first + place // tiles, values.shape[0], stride=rows), :] = (
            values[:, place * LANES : (place + 1) * LANES]
        )


def take_rows(scratch, first, count, rows, channels):
    return side_by_side(
        [
            scratch[tile, pl.ds(first + row, channels, stride=rows), :]
            for row in range(count)
            for tile in range(scratch.shape[0])
        ]
    )


def read_rows(ref, first, count):
    return side_by_side([ref[first + row] for row in range(count)])


def write_rows(ref, first, values):
    columns = ref.shape[-1]
    for row in range(values.shape[1] // columns):
        ref[first + row] = values[:, row * columns : (row + 1) * columns]


def edges_of_rows(pair_f, row, rows, mask, proj, gain, left_scr, right_scr):
    channels = pair_f.shape[0]
    normed = (normalize(pair_f) * gain).astype(jnp.bfloat16)
    linear = matmul(proj[...], normed)
    p0, p1, p2, p3, p4 = [linear[e * channels : (e + 1) * channels] for e in range(5)]
    put_rows(left_scr, row, rows, sigmoid(p1) * p0 * mask)
    put_rows(right_scr, row, rows, sigmoid(p3) * p2 * mask)
    return sigmoid(p4)


def write_edges(left_scr, right_scr, here, edges):
    block = edges[0].shape[2]
    for which, scr in enumerate((left_scr, right_scr)):
        for m in range(2 * len(edges)):
            start = pl.multiple_of((here[0] ^ m) * block, block)
            for tile in range(scr.shape[0]):
                edges[m // 2][m % 2, which, :, tile * LANES : (tile + 1) * LANES] = scr[
                    tile, pl.ds(start, block), :
                ].astype(jnp.bfloat16)


def arrived(own, cross, m):
    return cross[m // 2][1] if m % 2 else own[m // 2][0]


def repeat(gains, count):
    return side_by_side([gains] * count)


def rows_together(rows, columns):
    return min(rows, max(1, TOGETHER // columns))


def first_kernel(half, here, pair, mask, proj, gains, *refs):
    edges, (pair_t, gate, left_scr, right_scr) = refs[:half], refs[half:]
    rows, columns = pair.shape[:2]
    count = rows_together(rows, columns)

    def step(i, carry):
        row = i * count
        pair_f = side_by_side([pair[row + k].astype(jnp.float32).T for k in range(count)])
        write_rows(pair_t, row, pair_f.astype(jnp.bfloat16))
        opened = edges_of_rows(
            pair_f, row, rows, read_rows(mask, row, count), proj, repeat(gains[0], count),
            left_scr, right_scr,
        )
        write_rows(gate, row, opened)
        return carry

    lax.fori_loop(0, rows // count, step, 0)
    write_edges(left_scr, right_scr, here, edges)


def triangle_kernel(half, chunks, here, *refs):
    groups = 2 * half
    sources = [refs[k * groups : (k + 1) * groups] for k in range(chunks)]
    refs = refs[chunks * groups :]
    products = [refs[k * half : (k + 1) * half] for k in range(chunks)]
    wide, sums = refs[chunks * half :]
    block, columns = sums.shape[1:]
    places = groups * chunks
    rows = columns // places

    def place_of(k, m):
        return lax.rem(here[1] + k, chunks) * groups + (here[0] ^ m)

    for k in range(chunks):
        for m in range(groups):
            values = arrived(sources[k][:half], sources[k][half:], m)
            for which in range(2):
                wide[which, place_of(k, m)] = values[which].astype(jnp.float32)

    def step(c, carry):
        at = pl.ds(pl.multiple_of(c * rows, rows), rows)
        left, right = [
            jnp.concatenate([wide[which, p, at, :] for p in range(places)], axis=0).astype(
                jnp.bfloat16
            )
            for which in range(2)
        ]
        total = lax.dot_general(
            left, right, (((1,), (1,)), ((), ())), preferred_element_type=jnp.float32
        )
        for p in range(places):
            sums[p, at, :] = total[p * rows : (p + 1) * rows]
        return carry

    lax.fori_loop(0, block // rows, step, 0, unroll=min(4, block // rows))
    for k in range(chunks):
        for m in range(groups):
            products[k][m // 2][m % 2] = sums[place_of(k, m)].astype(jnp.bfloat16)


def load_product(here, own, cross, prod_scr):
    block = own[0].shape[1]
    for m in range(2 * len(own)):
        values = arrived(own, cross, m).astype(jnp.float32)
        start = pl.multiple_of((here[0] ^ m) * block, block)
        for tile in range(prod_scr.shape[0]):
            prod_scr[tile, pl.ds(start, block), :] = values[:, tile * LANES : (tile + 1) * LANES]


def finish_rows(prod_scr, row, count, pair, gate, out_t, up_t, down_t, gains):
    rows, channels = pair.shape[:2]
    tri = take_rows(prod_scr, row, count, rows, channels)
    tri_norm = (normalize(tri) * repeat(gains[1], count)).astype(jnp.bfloat16)
    mid = read_rows(pair, row, count).astype(jnp.float32) + read_rows(gate, row, count) * matmul(
        out_t[...], tri_norm
    )
    trans_in = (normalize(mid) * repeat(gains[2], count)).astype(jnp.bfloat16)
    hidden = jnp.maximum(matmul(up_t[...], trans_in), 0.0).astype(jnp.bfloat16)
    return (mid + matmul(down_t[...], hidden)).astype(jnp.bfloat16)


def middle_kernel(half, here, *refs):
    own, cross, refs = refs[:half], refs[half : 2 * half], refs[2 * half :]
    pair, gate, out_t, up_t, down_t, gains, mask, proj, next_gains = refs[:9]
    edges, refs = refs[9 : 9 + half], refs[9 + half :]
    next_pair, next_gate, prod_scr, left_scr, right_scr = refs
    rows, _, columns = pair.shape
    count = rows_together(rows, columns)
    load_product(here, own, cross, prod_scr)

    def step(i, carry):
        row = i * count
        new = finish_rows(prod_scr, row, count, pair, gate, out_t, up_t, down_t, gains)
        write_rows(next_pair, row, new)
        opened = edges_of_rows(
            new.astype(jnp.float32), row, rows, read_rows(mask, row, count), proj,
            repeat(next_gains[0], count), left_scr, right_scr,
        )
        write_rows(next_gate, row, opened)
        return carry

    lax.fori_loop(0, rows // count, step, 0)
    write_edges(left_scr, right_scr, here, edges)


def last_kernel(half, here, *refs):
    own, cross, refs = refs[:half], refs[half : 2 * half], refs[2 * half :]
    pair, gate, out_t, up_t, down_t, gains, result, prod_scr = refs
    rows, _, columns = pair.shape
    count = rows_together(rows, columns)
    slot = here[1] if result.shape[0] > 1 else 0
    load_product(here, own, cross, prod_scr)

    def step(i, carry):
        row = i * count
        new = finish_rows(prod_scr, row, count, pair, gate, out_t, up_t, down_t, gains)
        for k in range(count):
            result[slot, row + k] = (
                new[:, k * columns : (k + 1) * columns].astype(jnp.float32).T.astype(jnp.bfloat16)
            )
        return carry

    lax.fori_loop(0, rows // count, step, 0)


def call(kernel, outs, scratch, flops, here, *operands):
    whole = pl.BlockSpec(memory_space=pltpu.VMEM)
    return pallas(kernel, outs, scratch, flops, whole, here, *operands)


def pallas(kernel, outs, scratch, flops, whole, here, *operands):
    return pl.pallas_call(
        kernel,
        out_shape=[jax.ShapeDtypeStruct(shape, dtype) for shape, dtype in outs],
        in_specs=[pl.BlockSpec(memory_space=pltpu.SMEM)] + [whole] * len(operands),
        out_specs=[whole] * len(outs),
        scratch_shapes=[pltpu.VMEM(shape, jnp.float32) for shape in scratch],
        compiler_params=pltpu.CompilerParams(vmem_limit_bytes=VMEM_BYTES),
        cost_estimate=pl.CostEstimate(flops=flops, bytes_accessed=0, transcendentals=0),
    )(here, *operands)


def exchange(blocks, width, groups):
    half = len(blocks)
    if not by_permutes(width):
        whole = lax.all_to_all(
            jnp.concatenate(blocks), "axial", 0, 0, tiled=True, axis_index_groups=groups
        )
        return [whole[2 * i : 2 * i + 2] for i in range(half)] * 2
    size = lax.axis_size("axial")
    own = list(blocks)
    for i in range(half - 1, 0, -1):
        own[i] = lax.ppermute(blocks[i], "axial", [(j, j ^ (2 * i)) for j in range(size)])
    return own + [lax.ppermute(pair, "axial", [(j, j ^ 1) for j in range(size)]) for pair in own]


def by_permutes(width):
    return width in (2, 4, 8)


def move_parts(values, distance, width):
    if distance == 0:
        return values
    size = lax.axis_size("axial")
    return lax.ppermute(
        values, "axial", [(j, (j + distance * width) % size) for j in range(size)]
    )


def from_sections(weight, sections):
    return [weight] + [
        lax.ppermute(weight, "section", [((i + shift) % sections, i) for i in range(sections)])
        for shift in range(1, sections)
    ]


def by_layer(slots, section):
    sections = len(slots)
    layers = []
    for layer in range(sections):
        chosen = slots[0]
        for shift in range(1, sections):
            chosen = jnp.where((section + shift) % sections == layer, slots[shift], chosen)
        layers.append(chosen)
    return layers


def per_device(pair_in, crop_mask, proj_weights, out_weights, up_weights, down_weights, norm_gains):
    section = lax.axis_index("section")
    sections = lax.axis_size("section")
    axial = lax.axis_size("axial")
    own_count = pair_in.shape[0] // sections
    rows, columns, channels = pair_in.shape[1:]
    parts = own_count
    width = axial // parts
    half = width // 2
    block = channels // width * rows
    part, place = lax.axis_index("axial") // width, lax.axis_index("axial") % width
    groups = [[p * width + i for i in range(width)] for p in range(parts)]
    here = jnp.stack((place if by_permutes(width) else 0 * place, part)).astype(jnp.int32)

    pairs = []
    for k in range(parts):
        crop = lax.dynamic_index_in_dim(
            pair_in, section * own_count + (part + parts - k) % parts, 0, keepdims=False
        )
        pairs.append(move_parts(crop, -k, width))
    projs, gains = [from_sections(w[0], sections) for w in (proj_weights, norm_gains)]
    others = (out_weights[0], up_weights[0], down_weights[0])
    *others, projs[-1] = lax.optimization_barrier((*others, projs[-1]))
    others = [from_sections(w, sections) for w in others]
    pairs[-1], others = lax.optimization_barrier((pairs[-1], others))
    projs = [w.transpose(0, 2, 1).reshape(-1, channels) for w in by_layer(projs, section)]
    outs, ups, downs = [[w.T for w in by_layer(slots, section)] for slots in others]
    gains = [
        jnp.broadcast_to(g.astype(jnp.float32)[:, :, None], g.shape + (columns,))
        for g in by_layer(gains, section)
    ]

    mask_all = lax.dynamic_index_in_dim(
        crop_mask, section * own_count + part, 0, keepdims=False
    ).astype(jnp.float32)
    masks = [
        (
            lax.dynamic_slice_in_dim(
                mask_all, ((part + k) % parts * width + place) * rows, rows
            )[:, None]
            * mask_all
        )[:, None, :]
        for k in range(parts)
    ]

    tiles = columns // LANES
    scratch = (tiles, channels * rows, LANES)
    edges_out = [((2, 2, block, columns), jnp.bfloat16)] * half
    state_out = [
        ((rows, channels, columns), jnp.bfloat16), ((rows, channels, columns), jnp.float32)
    ]
    hidden = ups[0].shape[0]
    points = rows * columns
    head_flops = 2 * points * 5 * channels * channels
    tail_flops = 2 * points * channels * (channels + 2 * hidden)
    edges, state = [None] * parts, [None] * parts
    for k in range(parts):
        *sent, pair, gate = call(
            functools.partial(first_kernel, half), edges_out + state_out, [scratch] * 2,
            head_flops, here, pairs[k], masks[k], projs[0], gains[0],
        )
        edges[k], state[k] = exchange(sent, width, groups), (pair, gate)
    finished = [None] * parts
    for layer in range(sections):
        places = (parts * width, block, columns)
        products = call(
            functools.partial(triangle_kernel, half, parts),
            [((2, block, columns), jnp.bfloat16)] * (half * parts), [(2,) + places, places],
            2 * channels // width * columns**3, here, *sum(edges, []),
        )
        last = layer == sections - 1
        order = range(parts - 1, -1, -1) if last else range(parts)
        tri = {k: exchange(products[k * half : (k + 1) * half], width, groups) for k in order}
        for k in order:
            operands = (*tri[k], *state[k], outs[layer], ups[layer], downs[layer], gains[layer])
            if not last:
                *sent, pair, gate = call(
                    functools.partial(middle_kernel, half), edges_out + state_out, [scratch] * 3,
                    head_flops + tail_flops, here, *operands, masks[k], projs[layer + 1],
                    gains[layer + 1],
                )
                edges[k] = exchange(sent, width, groups)
                state[k] = (pair, gate)
            else:
                slots = 1 if k else parts
                (done,) = call(
                    functools.partial(last_kernel, half),
                    [((slots, rows, columns, channels), jnp.bfloat16)],
                    [scratch], tail_flops, here, *operands,
                )
                finished[k] = move_parts(done, k, width)
    result = finished[0]
    for k in range(1, parts):
        result = lax.dynamic_update_slice_in_dim(result, finished[k], (part + parts - k) % parts, 0)
    return result


def solution(mesh):
    def step(pair_in, *operands):
        mapped = jax.shard_map(
            per_device,
            mesh=mesh,
            in_specs=(
                P("groups", "axial", None, None),
                P("groups", None),
                P("section", None, None, None),
                P("section", None, None),
                P("section", None, None),
                P("section", None, None),
                P("section", None, None),
            ),
            out_specs=P(("groups", "section"), "axial", None, None),
            check_vma=False,
        )
        return mapped(pair_in, *operands)

    return step
```

profile of v0, /device:TPU:0, one launch (start us, length us, event | category | flops | bytes accessed | tf_op | source)
XLA Modules:
  0.0 100.7 jit_solution(8262118426197903602)
XLA Ops:
  0.7 3.0 %collective-permute-start.1 = (bf16[3,128]{1,0:T(4,128)(2,1)S(1)}, bf16[3,128]{1,0:T(4,128)(2,1)S(1)}, u32[]{:S(2)}, u32[]{:S(2)}) collective-permute-start(bf16[3,128]{1,0:T(4,128)(2,1)S(1)} %bitcast.50), channel_id=1, source_target_pairs={{16,0},{0,16},{17,1},{1,17},{18,2},{2,18},{19,3},{3,19},{20,4},{4,... | collective-permute-start | bytes 2312 | tf_op jit(solution)/shard_map/ppermute | solution.py:268
  4.8 3.2 %collective-permute-start.9 = (bf16[8,128,128]{2,1,0:T(8,128)(2,1)S(1)}, bf16[8,128,128]{2,1,0:T(8,128)(2,1)S(1)}, u32[]{:S(2)}, u32[]{:S(2)}) collective-permute-start(bf16[8,128,128]{2,1,0:T(8,128)(2,1)S(1)} %get-tuple-element.107), channel_id=1, source_target_pairs={{0,8},{1,9},{2,10},{3,11},{4,12},{5,13},{6,14},{7,15},{8,0},{9,1},... | collective-permute-start | bytes 786440 | tf_op jit(solution)/shard_map/ppermute | solution.py:261
  9.5 1.5 %collective-permute-start.10 = (bf16[128,128]{0,1:T(8,128)(2,1)S(1)}, bf16[128,128]{0,1:T(8,128)(2,1)S(1)}, u32[]{:S(2)}, u32[]{:S(2)}) collective-permute-start(bf16[128,128]{0,1:T(8,128)(2,1)S(1)} %bitcast.48), channel_id=1, source_target_pairs={{16,0},{0,16},{17,1},{1,17},{18,2},{2,18},{19,3},{3,19},{20,4},{4,... | collective-permute-start | bytes 98312 | tf_op jit(solution)/shard_map/ppermute | solution.py:268
  11.6 1.5 %collective-permute-start.12 = (bf16[512,128]{0,1:T(8,128)(2,1)S(1)}, bf16[512,128]{0,1:T(8,128)(2,1)S(1)}, u32[]{:S(2)}, u32[]{:S(2)}) collective-permute-start(bf16[512,128]{0,1:T(8,128)(2,1)S(1)} %bitcast.43), channel_id=1, source_target_pairs={{16,0},{0,16},{17,1},{1,17},{18,2},{2,18},{19,3},{3,19},{20,4},{4,... | collective-permute-start | bytes 393224 | tf_op jit(solution)/shard_map/ppermute | solution.py:268
  13.4 1.4 %shard_map.73 = (bf16[2,2,128,128]{3,2,1,0:T(8,128)(2,1)S(1)}, bf16[2,2,128,128]{3,2,1,0:T(8,128)(2,1)S(1)}, bf16[2,2,128,128]{3,2,1,0:T(8,128)(2,1)S(1)}, bf16[...) custom-call(s32[2]{0:T(128)S(1)} %pad_add_fusion.here, ...), custom_call_target="tpu_custom_call" | custom-call | flops 167772160 | tf_op jit(solution)/shard_map/pallas_call | solution.py:228
  14.7 1.6 %collective-permute-start.2 = (bf16[2,2,128,128]{3,2,1,0:T(8,128)(2,1)S(1)}, bf16[2,2,128,128]{3,2,1,0:T(8,128)(2,1)S(1)}, u32[]{:S(2)}, u32[]{:S(2)}) collective-permute-start(bf16[2,2,128,128]{3,2,1,0:T(8,128)(2,1)S(1)} %get-tuple-element.58), channel_id=1, source_target_pairs={{0,2},{1,3},{2,0},{3,1},{4,6},{5,7},{6,4},{7,5},{8,10},{9,11},{10,... | collective-permute-start | bytes 393224 | tf_op jit(solution)/shard_map/ppermute | solution.py:249
  16.3 1.6 %collective-permute-start.3 = (bf16[2,2,128,128]{3,2,1,0:T(8,128)(2,1)S(1)}, bf16[2,2,128,128]{3,2,1,0:T(8,128)(2,1)S(1)}, u32[]{:S(2)}, u32[]{:S(2)}) collective-permute-start(bf16[2,2,128,128]{3,2,1,0:T(8,128)(2,1)S(1)} %get-tuple-element.59), channel_id=1, source_target_pairs={{0,4},{1,5},{2,6},{3,7},{4,0},{5,1},{6,2},{7,3},{8,12},{9,13},{10,... | collective-permute-start | bytes 393224 | tf_op jit(solution)/shard_map/ppermute | solution.py:249
  17.9 1.5 %collective-permute-done.9.pair = bf16[8,128,128]{2,1,0:T(8,128)(2,1)S(1)} collective-permute-done((bf16[8,128,128]{2,1,0:T(8,128)(2,1)S(1)}, bf16[8,128,128]{2,1,0:T(8,128)(2,1)S(1)}, u32[]{:S(2)}, u32[]{:S(2)}) %collective-permute-start.9) | collective-permute-done | bytes 262176 | tf_op jit(solution)/shard_map/ppermute | solution.py:261
  19.4 1.6 %collective-permute-start.4 = (bf16[2,2,128,128]{3,2,1,0:T(8,128)(2,1)S(1)}, bf16[2,2,128,128]{3,2,1,0:T(8,128)(2,1)S(1)}, u32[]{:S(2)}, u32[]{:S(2)}) collective-permute-start(bf16[2,2,128,128]{3,2,1,0:T(8,128)(2,1)S(1)} %get-tuple-element.60), channel_id=1, source_target_pairs={{0,6},{1,7},{2,4},{3,5},{4,2},{5,3},{6,0},{7,1},{8,14},{9,15},{10,... | collective-permute-start | bytes 393224 | tf_op jit(solution)/shard_map/ppermute | solution.py:249
  22.3 1.4 %shard_map.74 = (bf16[2,2,128,128]{3,2,1,0:T(8,128)(2,1)S(1)}, bf16[2,2,128,128]{3,2,1,0:T(8,128)(2,1)S(1)}, bf16[2,2,128,128]{3,2,1,0:T(8,128)(2,1)S(1)}, bf16[...) custom-call(s32[2]{0:T(128)S(1)} %pad_add_fusion.here, ...), custom_call_target="tpu_custom_call" | custom-call | flops 167772160 | tf_op jit(solution)/shard_map/pallas_call | solution.py:228
  24.3 1.4 %collective-permute-start.14 = (bf16[2,2,128,128]{3,2,1,0:T(8,128)(2,1)S(1)}, bf16[2,2,128,128]{3,2,1,0:T(8,128)(2,1)S(1)}, u32[]{:S(2)}, u32[]{:S(2)}) collective-permute-start(bf16[2,2,128,128]{3,2,1,0:T(8,128)(2,1)S(1)} %get-tuple-element.67), channel_id=1, source_target_pairs={{0,4},{1,5},{2,6},{3,7},{4,0},{5,1},{6,2},{7,3},{8,12},{9,13},{10,... | collective-permute-start | bytes 393224 | tf_op jit(solution)/shard_map/ppermute | solution.py:249
  25.6 1.6 %collective-permute-start.15 = (bf16[2,2,128,128]{3,2,1,0:T(8,128)(2,1)S(1)}, bf16[2,2,128,128]{3,2,1,0:T(8,128)(2,1)S(1)}, u32[]{:S(2)}, u32[]{:S(2)}) collective-permute-start(bf16[2,2,128,128]{3,2,1,0:T(8,128)(2,1)S(1)} %get-tuple-element.68), channel_id=1, source_target_pairs={{0,6},{1,7},{2,4},{3,5},{4,2},{5,3},{6,0},{7,1},{8,14},{9,15},{10,... | collective-permute-start | bytes 393224 | tf_op jit(solution)/shard_map/ppermute | solution.py:249
  27.8 1.4 %collective-permute-done.13.refs_9_ = bf16[2,2,128,128]{3,2,1,0:T(8,128)(2,1)S(1)} collective-permute-done((bf16[2,2,128,128]{3,2,1,0:T(8,128)(2,1)S(1)}, bf16[2,2,128,128]{3,2,1,0:T(8,128)(2,1)S(1)}, u32[]{:S(2)}, u32[]{:S(2)}) %collective-permute-start.13) | collective-permute-done | bytes 131104 | tf_op jit(solution)/shard_map/ppermute | solution.py:249
  30.0 3.0 %collective-permute-done.15.refs_11_ = bf16[2,2,128,128]{3,2,1,0:T(8,128)(2,1)S(1)} collective-permute-done((bf16[2,2,128,128]{3,2,1,0:T(8,128)(2,1)S(1)}, bf16[2,2,128,128]{3,2,1,0:T(8,128)(2,1)S(1)}, u32[]{:S(2)}, u32[]{:S(2)}) %collective-permute-start.15) | collective-permute-done | bytes 131104 | tf_op jit(solution)/shard_map/ppermute | solution.py:249
  36.6 2.4 %shard_map.75 = (bf16[2,128,128]{2,1,0:T(8,128)(2,1)S(1)}, bf16[2,128,128]{2,1,0:T(8,128)(2,1)S(1)}, bf16[2,128,128]{2,1,0:T(8,128)(2,1)S(1)}, bf16[2,128,128]{2...) custom-call(s32[2]{0:T(128)S(1)} %pad_add_fusion.here, ...), custom_call_target="tpu_custom_call" | custom-call | flops 67108864 | tf_op jit(solution)/shard_map/pallas_call | solution.py:228
  39.6 1.5 %collective-permute-start.34 = (bf16[2,128,128]{2,1,0:T(8,128)(2,1)S(1)}, bf16[2,128,128]{2,1,0:T(8,128)(2,1)S(1)}, u32[]{:S(2)}, u32[]{:S(2)}) collective-permute-start(bf16[2,128,128]{2,1,0:T(8,128)(2,1)S(1)} %get-tuple-element.86), channel_id=1, source_target_pairs={{0,2},{1,3},{2,0},{3,1},{4,6},{5,7},{6,4},{7,5},{8,10},{9,11},{10,... | collective-permute-start | bytes 196616 | tf_op jit(solution)/shard_map/ppermute | solution.py:249
  42.0 1.5 %collective-permute-start.21 = (bf16[2,128,128]{2,1,0:T(8,128)(2,1)S(1)}, bf16[2,128,128]{2,1,0:T(8,128)(2,1)S(1)}, u32[]{:S(2)}, u32[]{:S(2)}) collective-permute-start(bf16[2,128,128]{2,1,0:T(8,128)(2,1)S(1)} %get-tuple-element.71), channel_id=1, source_target_pairs={{0,4},{1,5},{2,6},{3,7},{4,0},{5,1},{6,2},{7,3},{8,12},{9,13},{10,... | collective-permute-start | bytes 196616 | tf_op jit(solution)/shard_map/ppermute | solution.py:249
  51.2 2.2 %shard_map.77 = (bf16[2,2,128,128]{3,2,1,0:T(8,128)(2,1)S(1)}, bf16[2,2,128,128]{3,2,1,0:T(8,128)(2,1)S(1)}, bf16[2,2,128,128]{3,2,1,0:T(8,128)(2,1)S(1)}, bf16[...) custom-call(s32[2]{0:T(128)S(1)} %pad_add_fusion.here, ...), custom_call_target="tpu_custom_call" | custom-call | flops 469762048 | tf_op jit(solution)/shard_map/pallas_call | solution.py:228
  55.5 1.4 %collective-permute-start.43 = (bf16[2,2,128,128]{3,2,1,0:T(8,128)(2,1)S(1)}, bf16[2,2,128,128]{3,2,1,0:T(8,128)(2,1)S(1)}, u32[]{:S(2)}, u32[]{:S(2)}) collective-permute-start(bf16[2,2,128,128]{3,2,1,0:T(8,128)(2,1)S(1)} %get-tuple-element.94), channel_id=1, source_target_pairs={{0,6},{1,7},{2,4},{3,5},{4,2},{5,3},{6,0},{7,1},{8,14},{9,15},{10,... | collective-permute-start | bytes 393224 | tf_op jit(solution)/shard_map/ppermute | solution.py:249
  58.4 2.2 %shard_map.76 = (bf16[2,2,128,128]{3,2,1,0:T(8,128)(2,1)S(1)}, bf16[2,2,128,128]{3,2,1,0:T(8,128)(2,1)S(1)}, bf16[2,2,128,128]{3,2,1,0:T(8,128)(2,1)S(1)}, bf16[...) custom-call(s32[2]{0:T(128)S(1)} %pad_add_fusion.here, ...), custom_call_target="tpu_custom_call" | custom-call | flops 469762048 | tf_op jit(solution)/shard_map/pallas_call | solution.py:228
  62.7 1.4 %collective-permute-start.29 = (bf16[2,2,128,128]{3,2,1,0:T(8,128)(2,1)S(1)}, bf16[2,2,128,128]{3,2,1,0:T(8,128)(2,1)S(1)}, u32[]{:S(2)}, u32[]{:S(2)}) collective-permute-start(bf16[2,2,128,128]{3,2,1,0:T(8,128)(2,1)S(1)} %get-tuple-element.84), channel_id=1, source_target_pairs={{0,6},{1,7},{2,4},{3,5},{4,2},{5,3},{6,0},{7,1},{8,14},{9,15},{10,... | collective-permute-start | bytes 393224 | tf_op jit(solution)/shard_map/ppermute | solution.py:249
  64.6 1.7 %collective-permute-done.27.refs_1_ = bf16[2,2,128,128]{3,2,1,0:T(8,128)(2,1)S(1)} collective-permute-done((bf16[2,2,128,128]{3,2,1,0:T(8,128)(2,1)S(1)}, bf16[2,2,128,128]{3,2,1,0:T(8,128)(2,1)S(1)}, u32[]{:S(2)}, u32[]{:S(2)}) %collective-permute-start.27) | collective-permute-done | bytes 131104 | tf_op jit(solution)/shard_map/ppermute | solution.py:249
  66.3 1.7 %collective-permute-done.28.refs_2_ = bf16[2,2,128,128]{3,2,1,0:T(8,128)(2,1)S(1)} collective-permute-done((bf16[2,2,128,128]{3,2,1,0:T(8,128)(2,1)S(1)}, bf16[2,2,128,128]{3,2,1,0:T(8,128)(2,1)S(1)}, u32[]{:S(2)}, u32[]{:S(2)}) %collective-permute-start.28) | collective-permute-done | bytes 131104 | tf_op jit(solution)/shard_map/ppermute | solution.py:249
  68.0 2.3 %collective-permute-done.29.refs_3_ = bf16[2,2,128,128]{3,2,1,0:T(8,128)(2,1)S(1)} collective-permute-done((bf16[2,2,128,128]{3,2,1,0:T(8,128)(2,1)S(1)}, bf16[2,2,128,128]{3,2,1,0:T(8,128)(2,1)S(1)}, u32[]{:S(2)}, u32[]{:S(2)}) %collective-permute-start.29) | collective-permute-done | bytes 131104 | tf_op jit(solution)/shard_map/ppermute | solution.py:249
  72.2 1.6 %shard_map.78 = (bf16[2,128,128]{2,1,0:T(8,128)(2,1)S(1)}, bf16[2,128,128]{2,1,0:T(8,128)(2,1)S(1)}, bf16[2,128,128]{2,1,0:T(8,128)(2,1)S(1)}, bf16[2,128,128]{2...) custom-call(s32[2]{0:T(128)S(1)} %pad_add_fusion.here, ...), custom_call_target="tpu_custom_call" | custom-call | flops 67108864 | tf_op jit(solution)/shard_map/pallas_call | solution.py:228
  76.0 1.4 %collective-permute-start.57 = (bf16[2,128,128]{2,1,0:T(8,128)(2,1)S(1)}, bf16[2,128,128]{2,1,0:T(8,128)(2,1)S(1)}, u32[]{:S(2)}, u32[]{:S(2)}) collective-permute-start(bf16[2,128,128]{2,1,0:T(8,128)(2,1)S(1)} %get-tuple-element.104), channel_id=1, source_target_pairs={{0,6},{1,7},{2,4},{3,5},{4,2},{5,3},{6,0},{7,1},{8,14},{9,15},{10,... | collective-permute-start | bytes 196616 | tf_op jit(solution)/shard_map/ppermute | solution.py:249
  79.2 2.0 %collective-permute-done.57.refs_3_ = bf16[2,128,128]{2,1,0:T(8,128)(2,1)S(1)} collective-permute-done((bf16[2,128,128]{2,1,0:T(8,128)(2,1)S(1)}, bf16[2,128,128]{2,1,0:T(8,128)(2,1)S(1)}, u32[]{:S(2)}, u32[]{:S(2)}) %collective-permute-start.57) | collective-permute-done | bytes 65568 | tf_op jit(solution)/shard_map/ppermute | solution.py:249
  82.4 1.6 %shard_map.80 = bf16[1,8,128,128]{3,2,1,0:T(8,128)(2,1)S(1)} custom-call(s32[2]{0:T(128)S(1)} %pad_add_fusion.here, bf16[2,128,128]{2,1,0:T(8,128)(2,1)S(1)} %get-tuple-element.101.refs_0_, bf16[2,128,128]{2,1,0:T(8,128)(2,1)S(1)} %collective-permute-done.55.refs_1_, bf16[2,128,128]{2,1,0:T(8,128)(2,1)S(1)} %collective-permute-done.56.refs_2_, ...), custom_call_target="tpu_custom_call" | custom-call | flops 301989888 | tf_op jit(solution)/shard_map/pallas_call | solution.py:228
  84.0 3.5 %collective-permute-start.62 = (bf16[1,8,128,128]{3,2,1,0:T(8,128)(2,1)S(1)}, bf16[1,8,128,128]{3,2,1,0:T(8,128)(2,1)S(1)}, u32[]{:S(2)}, u32[]{:S(2)}) collective-permute-start(bf16[1,8,128,128]{3,2,1,0:T(8,128)(2,1)S(1)} %shard_map.80), channel_id=1, source_target_pairs={{0,8},{1,9},{2,10},{3,11},{4,12},{5,13},{6,14},{7,15},{8,0},{9,1},... | collective-permute-start | bytes 786440 | tf_op jit(solution)/shard_map/ppermute | solution.py:261
  88.2 1.7 %collective-permute-start.49 = (bf16[2,128,128]{2,1,0:T(8,128)(2,1)S(1)}, bf16[2,128,128]{2,1,0:T(8,128)(2,1)S(1)}, u32[]{:S(2)}, u32[]{:S(2)}) collective-permute-start(bf16[2,128,128]{2,1,0:T(8,128)(2,1)S(1)} %get-tuple-element.97), channel_id=1, source_target_pairs={{0,4},{1,5},{2,6},{3,7},{4,0},{5,1},{6,2},{7,3},{8,12},{9,13},{10,... | collective-permute-start | bytes 196616 | tf_op jit(solution)/shard_map/ppermute | solution.py:249
  91.8 3.8 %collective-permute-done.49.refs_2_ = bf16[2,128,128]{2,1,0:T(8,128)(2,1)S(1)} collective-permute-done((bf16[2,128,128]{2,1,0:T(8,128)(2,1)S(1)}, bf16[2,128,128]{2,1,0:T(8,128)(2,1)S(1)}, u32[]{:S(2)}, u32[]{:S(2)}) %collective-permute-start.49) | collective-permute-done | bytes 65568 | tf_op jit(solution)/shard_map/ppermute | solution.py:249
  97.5 2.4 %shard_map.79 = bf16[2,8,128,128]{3,2,1,0:T(8,128)(2,1)} custom-call(s32[2]{0:T(128)S(1)} %pad_add_fusion.here, bf16[2,128,128]{2,1,0:T(8,128)(2,1)S(1)} %get-tuple-element.95.refs_0_, bf16[2,128,128]{2,1,0:T(8,128)(2,1)S(1)} %collective-permute-done.48.refs_1_, bf16[2,128,128]{2,1,0:T(8,128)(2,1)S(1)} %collective-permute-done.49.refs_2_, ...), custom_call_target="tpu_custom_call" | custom-call | flops 301989888 | tf_op jit(solution)/shard_map/pallas_call | solution.py:228
  (155 shorter events, 38.5 us)
Async XLA Ops:
  0.7 8.7 %collective-permute-start.1 = (bf16[3,128]{1,0:T(4,128)(2,1)S(1)}, bf16[3,128]{1,0:T(4,128)(2,1)S(1)}, u32[]{:S(2)}, u32[]{:S(2)}) collective-permute-start(bf16[3,128]{1,0:T(4,128)(2,1)S(1)} %bitcast.50), channel_id=1, source_target_pairs={{16,0},{0,16},{17,1},{1,17},{18,2},{2,18},{19,3},{3,19},{20,4},{4,... | collective-permute-start | bytes 2312 | tf_op jit(solution)/shard_map/ppermute | solution.py:268
  3.6 5.9 %collective-permute-start = (bf16[5,128,128]{2,1,0:T(8,128)(2,1)}, bf16[5,128,128]{2,1,0:T(8,128)(2,1)S(1)}, u32[]{:S(2)}, u32[]{:S(2)}) collective-permute-start(bf16[5,128,128]{2,1,0:T(8,128)(2,1)} %bitcast.47), channel_id=1, source_target_pairs={{16,0},{0,16},{17,1},{1,17},{18,2},{2,18},{19,3},{3,19},{20,4},{4,... | collective-permute-start | bytes 491528 | tf_op jit(solution)/shard_map/ppermute | solution.py:268
  4.8 14.6 %collective-permute-start.9 = (bf16[8,128,128]{2,1,0:T(8,128)(2,1)S(1)}, bf16[8,128,128]{2,1,0:T(8,128)(2,1)S(1)}, u32[]{:S(2)}, u32[]{:S(2)}) collective-permute-start(bf16[8,128,128]{2,1,0:T(8,128)(2,1)S(1)} %get-tuple-element.107), channel_id=1, source_target_pairs={{0,8},{1,9},{2,10},{3,11},{4,12},{5,13},{6,14},{7,15},{8,0},{9,1},... | collective-permute-start | bytes 786440 | tf_op jit(solution)/shard_map/ppermute | solution.py:261
  9.5 6.8 %collective-permute-start.10 = (bf16[128,128]{0,1:T(8,128)(2,1)S(1)}, bf16[128,128]{0,1:T(8,128)(2,1)S(1)}, u32[]{:S(2)}, u32[]{:S(2)}) collective-permute-start(bf16[128,128]{0,1:T(8,128)(2,1)S(1)} %bitcast.48), channel_id=1, source_target_pairs={{16,0},{0,16},{17,1},{1,17},{18,2},{2,18},{19,3},{3,19},{20,4},{4,... | collective-permute-start | bytes 98312 | tf_op jit(solution)/shard_map/ppermute | solution.py:268
  11.0 10.0 %collective-permute-start.11 = (bf16[128,512]{0,1:T(8,128)(2,1)S(1)}, bf16[128,512]{0,1:T(8,128)(2,1)S(1)}, u32[]{:S(2)}, u32[]{:S(2)}) collective-permute-start(bf16[128,512]{0,1:T(8,128)(2,1)S(1)} %bitcast.45), channel_id=1, source_target_pairs={{16,0},{0,16},{17,1},{1,17},{18,2},{2,18},{19,3},{3,19},{20,4},{4,... | collective-permute-start | bytes 393224 | tf_op jit(solution)/shard_map/ppermute | solution.py:268
  11.6 9.5 %collective-permute-start.12 = (bf16[512,128]{0,1:T(8,128)(2,1)S(1)}, bf16[512,128]{0,1:T(8,128)(2,1)S(1)}, u32[]{:S(2)}, u32[]{:S(2)}) collective-permute-start(bf16[512,128]{0,1:T(8,128)(2,1)S(1)} %bitcast.43), channel_id=1, source_target_pairs={{16,0},{0,16},{17,1},{1,17},{18,2},{2,18},{19,3},{3,19},{20,4},{4,... | collective-permute-start | bytes 393224 | tf_op jit(solution)/shard_map/ppermute | solution.py:268
  14.7 9.5 %collective-permute-start.2 = (bf16[2,2,128,128]{3,2,1,0:T(8,128)(2,1)S(1)}, bf16[2,2,128,128]{3,2,1,0:T(8,128)(2,1)S(1)}, u32[]{:S(2)}, u32[]{:S(2)}) collective-permute-start(bf16[2,2,128,128]{3,2,1,0:T(8,128)(2,1)S(1)} %get-tuple-element.58), channel_id=1, source_target_pairs={{0,2},{1,3},{2,0},{3,1},{4,6},{5,7},{6,4},{7,5},{8,10},{9,11},{10,... | collective-permute-start | bytes 393224 | tf_op jit(solution)/shard_map/ppermute | solution.py:249
  16.3 9.3 %collective-permute-start.3 = (bf16[2,2,128,128]{3,2,1,0:T(8,128)(2,1)S(1)}, bf16[2,2,128,128]{3,2,1,0:T(8,128)(2,1)S(1)}, u32[]{:S(2)}, u32[]{:S(2)}) collective-permute-start(bf16[2,2,128,128]{3,2,1,0:T(8,128)(2,1)S(1)} %get-tuple-element.59), channel_id=1, source_target_pairs={{0,4},{1,5},{2,6},{3,7},{4,0},{5,1},{6,2},{7,3},{8,12},{9,13},{10,... | collective-permute-start | bytes 393224 | tf_op jit(solution)/shard_map/ppermute | solution.py:249
  19.4 7.9 %collective-permute-start.4 = (bf16[2,2,128,128]{3,2,1,0:T(8,128)(2,1)S(1)}, bf16[2,2,128,128]{3,2,1,0:T(8,128)(2,1)S(1)}, u32[]{:S(2)}, u32[]{:S(2)}) collective-permute-start(bf16[2,2,128,128]{3,2,1,0:T(8,128)(2,1)S(1)} %get-tuple-element.60), channel_id=1, source_target_pairs={{0,6},{1,7},{2,4},{3,5},{4,2},{5,3},{6,0},{7,1},{8,14},{9,15},{10,... | collective-permute-start | bytes 393224 | tf_op jit(solution)/shard_map/ppermute | solution.py:249
  21.0 6.2 %collective-permute-start.5 = (bf16[2,2,128,128]{3,2,1,0:T(8,128)(2,1)S(1)}, bf16[2,2,128,128]{3,2,1,0:T(8,128)(2,1)S(1)}, u32[]{:S(2)}, u32[]{:S(2)}) collective-permute-start(bf16[2,2,128,128]{3,2,1,0:T(8,128)(2,1)S(1)} %get-tuple-element.57.refs_0_), channel_id=1, source_target_pairs={{0,1},{1,0},{2,3},{3,2},{4,5},{5,4},{6,7},{7,6},{8,9},{9,8},{10,11... | collective-permute-start | bytes 393224 | tf_op jit(solution)/shard_map/ppermute | solution.py:250
  24.3 5.7 %collective-permute-start.14 = (bf16[2,2,128,128]{3,2,1,0:T(8,128)(2,1)S(1)}, bf16[2,2,128,128]{3,2,1,0:T(8,128)(2,1)S(1)}, u32[]{:S(2)}, u32[]{:S(2)}) collective-permute-start(bf16[2,2,128,128]{3,2,1,0:T(8,128)(2,1)S(1)} %get-tuple-element.67), channel_id=1, source_target_pairs={{0,4},{1,5},{2,6},{3,7},{4,0},{5,1},{6,2},{7,3},{8,12},{9,13},{10,... | collective-permute-start | bytes 393224 | tf_op jit(solution)/shard_map/ppermute | solution.py:249
  25.6 7.4 %collective-permute-start.15 = (bf16[2,2,128,128]{3,2,1,0:T(8,128)(2,1)S(1)}, bf16[2,2,128,128]{3,2,1,0:T(8,128)(2,1)S(1)}, u32[]{:S(2)}, u32[]{:S(2)}) collective-permute-start(bf16[2,2,128,128]{3,2,1,0:T(8,128)(2,1)S(1)} %get-tuple-element.68), channel_id=1, source_target_pairs={{0,6},{1,7},{2,4},{3,5},{4,2},{5,3},{6,0},{7,1},{8,14},{9,15},{10,... | collective-permute-start | bytes 393224 | tf_op jit(solution)/shard_map/ppermute | solution.py:249
  27.3 5.8 %collective-permute-start.16 = (bf16[2,2,128,128]{3,2,1,0:T(8,128)(2,1)S(1)}, bf16[2,2,128,128]{3,2,1,0:T(8,128)(2,1)S(1)}, u32[]{:S(2)}, u32[]{:S(2)}) collective-permute-start(bf16[2,2,128,128]{3,2,1,0:T(8,128)(2,1)S(1)} %get-tuple-element.65.refs_8_), channel_id=1, source_target_pairs={{0,1},{1,0},{2,3},{3,2},{4,5},{5,4},{6,7},{7,6},{8,9},{9,8},{10,11... | collective-permute-start | bytes 393224 | tf_op jit(solution)/shard_map/ppermute | solution.py:250
  27.3 6.3 %collective-permute-start.6 = (bf16[2,2,128,128]{3,2,1,0:T(8,128)(2,1)S(1)}, bf16[2,2,128,128]{3,2,1,0:T(8,128)(2,1)S(1)}, u32[]{:S(2)}, u32[]{:S(2)}) collective-permute-start(bf16[2,2,128,128]{3,2,1,0:T(8,128)(2,1)S(1)} %collective-permute-done.2.refs_1_), channel_id=1, source_target_pairs={{0,1},{1,0},{2,3},{3,2},{4,5},{5,4},{6,7},{7,6},{8,9},{9,8},{10,11... | collective-permute-start | bytes 393224 | tf_op jit(solution)/shard_map/ppermute | solution.py:250
  39.0 6.4 %collective-permute-start.20 = (bf16[2,128,128]{2,1,0:T(8,128)(2,1)S(1)}, bf16[2,128,128]{2,1,0:T(8,128)(2,1)S(1)}, u32[]{:S(2)}, u32[]{:S(2)}) collective-permute-start(bf16[2,128,128]{2,1,0:T(8,128)(2,1)S(1)} %get-tuple-element.70), channel_id=1, source_target_pairs={{0,2},{1,3},{2,0},{3,1},{4,6},{5,7},{6,4},{7,5},{8,10},{9,11},{10,... | collective-permute-start | bytes 196616 | tf_op jit(solution)/shard_map/ppermute | solution.py:249
  39.6 5.9 %collective-permute-start.34 = (bf16[2,128,128]{2,1,0:T(8,128)(2,1)S(1)}, bf16[2,128,128]{2,1,0:T(8,128)(2,1)S(1)}, u32[]{:S(2)}, u32[]{:S(2)}) collective-permute-start(bf16[2,128,128]{2,1,0:T(8,128)(2,1)S(1)} %get-tuple-element.86), channel_id=1, source_target_pairs={{0,2},{1,3},{2,0},{3,1},{4,6},{5,7},{6,4},{7,5},{8,10},{9,11},{10,... | collective-permute-start | bytes 196616 | tf_op jit(solution)/shard_map/ppermute | solution.py:249
  47.1 7.5 %collective-permute-start.22 = (bf16[2,128,128]{2,1,0:T(8,128)(2,1)S(1)}, bf16[2,128,128]{2,1,0:T(8,128)(2,1)S(1)}, u32[]{:S(2)}, u32[]{:S(2)}) collective-permute-start(bf16[2,128,128]{2,1,0:T(8,128)(2,1)S(1)} %get-tuple-element.72), channel_id=1, source_target_pairs={{0,6},{1,7},{2,4},{3,5},{4,2},{5,3},{6,0},{7,1},{8,14},{9,15},{10,... | collective-permute-start | bytes 196616 | tf_op jit(solution)/shard_map/ppermute | solution.py:249
  48.2 7.3 %collective-permute-start.23 = (bf16[2,128,128]{2,1,0:T(8,128)(2,1)S(1)}, bf16[2,128,128]{2,1,0:T(8,128)(2,1)S(1)}, u32[]{:S(2)}, u32[]{:S(2)}) collective-permute-start(bf16[2,128,128]{2,1,0:T(8,128)(2,1)S(1)} %get-tuple-element.69.refs_0_), channel_id=1, source_target_pairs={{0,1},{1,0},{2,3},{3,2},{4,5},{5,4},{6,7},{7,6},{8,9},{9,8},{10,11... | collective-permute-start | bytes 196616 | tf_op jit(solution)/shard_map/ppermute | solution.py:250
  49.3 7.6 %collective-permute-start.24 = (bf16[2,128,128]{2,1,0:T(8,128)(2,1)S(1)}, bf16[2,128,128]{2,1,0:T(8,128)(2,1)S(1)}, u32[]{:S(2)}, u32[]{:S(2)}) collective-permute-start(bf16[2,128,128]{2,1,0:T(8,128)(2,1)S(1)} %collective-permute-done.20.refs_1_), channel_id=1, source_target_pairs={{0,1},{1,0},{2,3},{3,2},{4,5},{5,4},{6,7},{7,6},{8,9},{9,8},{10,11... | collective-permute-start | bytes 196616 | tf_op jit(solution)/shard_map/ppermute | solution.py:250
  50.7 6.2 %collective-permute-start.25 = (bf16[2,128,128]{2,1,0:T(8,128)(2,1)S(1)}, bf16[2,128,128]{2,1,0:T(8,128)(2,1)S(1)}, u32[]{:S(2)}, u32[]{:S(2)}) collective-permute-start(bf16[2,128,128]{2,1,0:T(8,128)(2,1)S(1)} %collective-permute-done.21.refs_2_), channel_id=1, source_target_pairs={{0,1},{1,0},{2,3},{3,2},{4,5},{5,4},{6,7},{7,6},{8,9},{9,8},{10,11... | collective-permute-start | bytes 196616 | tf_op jit(solution)/shard_map/ppermute | solution.py:250
  53.4 8.3 %collective-permute-start.41 = (bf16[2,2,128,128]{3,2,1,0:T(8,128)(2,1)S(1)}, bf16[2,2,128,128]{3,2,1,0:T(8,128)(2,1)S(1)}, u32[]{:S(2)}, u32[]{:S(2)}) collective-permute-start(bf16[2,2,128,128]{3,2,1,0:T(8,128)(2,1)S(1)} %get-tuple-element.92), channel_id=1, source_target_pairs={{0,2},{1,3},{2,0},{3,1},{4,6},{5,7},{6,4},{7,5},{8,10},{9,11},{10,... | collective-permute-start | bytes 393224 | tf_op jit(solution)/shard_map/ppermute | solution.py:249
  54.5 8.2 %collective-permute-start.42 = (bf16[2,2,128,128]{3,2,1,0:T(8,128)(2,1)S(1)}, bf16[2,2,128,128]{3,2,1,0:T(8,128)(2,1)S(1)}, u32[]{:S(2)}, u32[]{:S(2)}) collective-permute-start(bf16[2,2,128,128]{3,2,1,0:T(8,128)(2,1)S(1)} %get-tuple-element.93), channel_id=1, source_target_pairs={{0,4},{1,5},{2,6},{3,7},{4,0},{5,1},{6,2},{7,3},{8,12},{9,13},{10,... | collective-permute-start | bytes 393224 | tf_op jit(solution)/shard_map/ppermute | solution.py:249
  55.5 8.6 %collective-permute-start.43 = (bf16[2,2,128,128]{3,2,1,0:T(8,128)(2,1)S(1)}, bf16[2,2,128,128]{3,2,1,0:T(8,128)(2,1)S(1)}, u32[]{:S(2)}, u32[]{:S(2)}) collective-permute-start(bf16[2,2,128,128]{3,2,1,0:T(8,128)(2,1)S(1)} %get-tuple-element.94), channel_id=1, source_target_pairs={{0,6},{1,7},{2,4},{3,5},{4,2},{5,3},{6,0},{7,1},{8,14},{9,15},{10,... | collective-permute-start | bytes 393224 | tf_op jit(solution)/shard_map/ppermute | solution.py:249
  56.9 7.2 %collective-permute-start.44 = (bf16[2,2,128,128]{3,2,1,0:T(8,128)(2,1)S(1)}, bf16[2,2,128,128]{3,2,1,0:T(8,128)(2,1)S(1)}, u32[]{:S(2)}, u32[]{:S(2)}) collective-permute-start(bf16[2,2,128,128]{3,2,1,0:T(8,128)(2,1)S(1)} %get-tuple-element.91.refs_8_), channel_id=1, source_target_pairs={{0,1},{1,0},{2,3},{3,2},{4,5},{5,4},{6,7},{7,6},{8,9},{9,8},{10,11... | collective-permute-start | bytes 393224 | tf_op jit(solution)/shard_map/ppermute | solution.py:250
  60.5 5.8 %collective-permute-start.27 = (bf16[2,2,128,128]{3,2,1,0:T(8,128)(2,1)S(1)}, bf16[2,2,128,128]{3,2,1,0:T(8,128)(2,1)S(1)}, u32[]{:S(2)}, u32[]{:S(2)}) collective-permute-start(bf16[2,2,128,128]{3,2,1,0:T(8,128)(2,1)S(1)} %get-tuple-element.82), channel_id=1, source_target_pairs={{0,2},{1,3},{2,0},{3,1},{4,6},{5,7},{6,4},{7,5},{8,10},{9,11},{10,... | collective-permute-start | bytes 393224 | tf_op jit(solution)/shard_map/ppermute | solution.py:249
  61.7 6.4 %collective-permute-start.28 = (bf16[2,2,128,128]{3,2,1,0:T(8,128)(2,1)S(1)}, bf16[2,2,128,128]{3,2,1,0:T(8,128)(2,1)S(1)}, u32[]{:S(2)}, u32[]{:S(2)}) collective-permute-start(bf16[2,2,128,128]{3,2,1,0:T(8,128)(2,1)S(1)} %get-tuple-element.83), channel_id=1, source_target_pairs={{0,4},{1,5},{2,6},{3,7},{4,0},{5,1},{6,2},{7,3},{8,12},{9,13},{10,... | collective-permute-start | bytes 393224 | tf_op jit(solution)/shard_map/ppermute | solution.py:249
  62.7 7.7 %collective-permute-start.29 = (bf16[2,2,128,128]{3,2,1,0:T(8,128)(2,1)S(1)}, bf16[2,2,128,128]{3,2,1,0:T(8,128)(2,1)S(1)}, u32[]{:S(2)}, u32[]{:S(2)}) collective-permute-start(bf16[2,2,128,128]{3,2,1,0:T(8,128)(2,1)S(1)} %get-tuple-element.84), channel_id=1, source_target_pairs={{0,6},{1,7},{2,4},{3,5},{4,2},{5,3},{6,0},{7,1},{8,14},{9,15},{10,... | collective-permute-start | bytes 393224 | tf_op jit(solution)/shard_map/ppermute | solution.py:249
  64.1 6.3 %collective-permute-start.30 = (bf16[2,2,128,128]{3,2,1,0:T(8,128)(2,1)S(1)}, bf16[2,2,128,128]{3,2,1,0:T(8,128)(2,1)S(1)}, u32[]{:S(2)}, u32[]{:S(2)}) collective-permute-start(bf16[2,2,128,128]{3,2,1,0:T(8,128)(2,1)S(1)} %get-tuple-element.81.refs_0_), channel_id=1, source_target_pairs={{0,1},{1,0},{2,3},{3,2},{4,5},{5,4},{6,7},{7,6},{8,9},{9,8},{10,11... | collective-permute-start | bytes 393224 | tf_op jit(solution)/shard_map/ppermute | solution.py:250
  64.1 6.8 %collective-permute-start.45 = (bf16[2,2,128,128]{3,2,1,0:T(8,128)(2,1)S(1)}, bf16[2,2,128,128]{3,2,1,0:T(8,128)(2,1)S(1)}, u32[]{:S(2)}, u32[]{:S(2)}) collective-permute-start(bf16[2,2,128,128]{3,2,1,0:T(8,128)(2,1)S(1)} %collective-permute-done.41.refs_9_), channel_id=1, source_target_pairs={{0,1},{1,0},{2,3},{3,2},{4,5},{5,4},{6,7},{7,6},{8,9},{9,8},{10,11... | collective-permute-start | bytes 393224 | tf_op jit(solution)/shard_map/ppermute | solution.py:250
  84.0 15.9 %collective-permute-start.62 = (bf16[1,8,128,128]{3,2,1,0:T(8,128)(2,1)S(1)}, bf16[1,8,128,128]{3,2,1,0:T(8,128)(2,1)S(1)}, u32[]{:S(2)}, u32[]{:S(2)}) collective-permute-start(bf16[1,8,128,128]{3,2,1,0:T(8,128)(2,1)S(1)} %shard_map.80), channel_id=1, source_target_pairs={{0,8},{1,9},{2,10},{3,11},{4,12},{5,13},{6,14},{7,15},{8,0},{9,1},... | collective-permute-start | bytes 786440 | tf_op jit(solution)/shard_map/ppermute | solution.py:261
  88.2 7.3 %collective-permute-start.49 = (bf16[2,128,128]{2,1,0:T(8,128)(2,1)S(1)}, bf16[2,128,128]{2,1,0:T(8,128)(2,1)S(1)}, u32[]{:S(2)}, u32[]{:S(2)}) collective-permute-start(bf16[2,128,128]{2,1,0:T(8,128)(2,1)S(1)} %get-tuple-element.97), channel_id=1, source_target_pairs={{0,4},{1,5},{2,6},{3,7},{4,0},{5,1},{6,2},{7,3},{8,12},{9,13},{10,... | collective-permute-start | bytes 196616 | tf_op jit(solution)/shard_map/ppermute | solution.py:249
  90.0 6.3 %collective-permute-start.50 = (bf16[2,128,128]{2,1,0:T(8,128)(2,1)S(1)}, bf16[2,128,128]{2,1,0:T(8,128)(2,1)S(1)}, u32[]{:S(2)}, u32[]{:S(2)}) collective-permute-start(bf16[2,128,128]{2,1,0:T(8,128)(2,1)S(1)} %get-tuple-element.98), channel_id=1, source_target_pairs={{0,6},{1,7},{2,4},{3,5},{4,2},{5,3},{6,0},{7,1},{8,14},{9,15},{10,... | collective-permute-start | bytes 196616 | tf_op jit(solution)/shard_map/ppermute | solution.py:249
  (48 other events, 154.2 us)
where the time goes:
time: 101 us
  starting transfers between devices  45.9 us (45%)
  waiting for transfers between devices  31.1 us (31%)
  Pallas kernels  15 us (15%)
  local copies, waits for them, and re-layouts  7.12 us (7%)
  other arithmetic  1.17 us (1%)
    ppermute x24, starting transfers between devices, exchange(): lax.ppermute(blocks[i], 'axial', [(j, j ^ 2 * i) for j in range(size)])  28.6 us
    ppermute x24, waiting for transfers between devices, exchange(): lax.ppermute(blocks[i], 'axial', [(j, j ^ 2 * i) for j in range(size)])  22.7 us
    pallas_call x8, Pallas kernels, pallas(): pl.pallas_call(kernel, out_shape=[jax.ShapeDtypeStruct(shape, dtype) for...  15 us
    ppermute x32, waiting for transfers between devices, exchange(): lax.ppermute(pair, 'axial', [(j, j ^ 1) for j in range(size)])  6.82 us
    ppermute x2, starting transfers between devices, move_parts(): lax.ppermute(values, 'axial', [(j, (j + distance * width) % size) for j i...  6.65 us
    ppermute x5, starting transfers between devices, from_sections(): lax.ppermute(weight, 'section', [((i + shift) % sections, i) for i in ran...  6.51 us
    unnamed x37, local copies, waits for them, and re-layouts  4.68 us
    ppermute x32, starting transfers between devices, exchange(): lax.ppermute(pair, 'axial', [(j, j ^ 1) for j in range(size)])  4.09 us
  transfers between devices with their start and end apart: 63, of which 28 were waited for; matrix products, arithmetic and copies ran while one was open for 3% of the time, Pallas kernels for 9%

commit v1 on v0

--- a/solution.py
+++ b/solution.py
@@ -11,7 +11,7 @@
 epsilon = 1e-05
 LANES = 128
 TOGETHER = 1024
-VMEM_BYTES = 48 * 1024 * 1024
+VMEM_BYTES = 24 * 1024 * 1024
 
 
 def sigmoid(x):
@@ -107,7 +107,7 @@
             pair_f, row, rows, read_rows(mask, row, count), proj, repeat(gains[0], count),
             left_scr, right_scr,
         )
-        write_rows(gate, row, opened)
+        write_rows(gate, row, opened.astype(jnp.bfloat16))
         return carry
 
     lax.fori_loop(0, rows // count, step, 0)
@@ -167,9 +167,8 @@
     rows, channels = pair.shape[:2]
     tri = take_rows(prod_scr, row, count, rows, channels)
     tri_norm = (normalize(tri) * repeat(gains[1], count)).astype(jnp.bfloat16)
-    mid = read_rows(pair, row, count).astype(jnp.float32) + read_rows(gate, row, count) * matmul(
-        out_t[...], tri_norm
-    )
+    opened = read_rows(gate, row, count).astype(jnp.float32)
+    mid = read_rows(pair, row, count).astype(jnp.float32) + opened * matmul(out_t[...], tri_norm)
     trans_in = (normalize(mid) * repeat(gains[2], count)).astype(jnp.bfloat16)
     hidden = jnp.maximum(matmul(up_t[...], trans_in), 0.0).astype(jnp.bfloat16)
     return (mid + matmul(down_t[...], hidden)).astype(jnp.bfloat16)
@@ -192,7 +191,7 @@
             new.astype(jnp.float32), row, rows, read_rows(mask, row, count), proj,
             repeat(next_gains[0], count), left_scr, right_scr,
         )
-        write_rows(next_gate, row, opened)
+        write_rows(next_gate, row, opened.astype(jnp.bfloat16))
         return carry
 
     lax.fori_loop(0, rows // count, step, 0)
@@ -245,7 +244,7 @@
         return [whole[2 * i : 2 * i + 2] for i in range(half)] * 2
     size = lax.axis_size("axial")
     own = list(blocks)
-    for i in range(half - 1, 0, -1):
+    for i in range(1, half):
         own[i] = lax.ppermute(blocks[i], "axial", [(j, j ^ (2 * i)) for j in range(size)])
     return own + [lax.ppermute(pair, "axial", [(j, j ^ 1) for j in range(size)]) for pair in own]
 
@@ -301,11 +300,11 @@
             pair_in, section * own_count + (part + parts - k) % parts, 0, keepdims=False
         )
         pairs.append(move_parts(crop, -k, width))
-    projs, gains = [from_sections(w[0], sections) for w in (proj_weights, norm_gains)]
+    projs = from_sections(proj_weights[0], sections)
+    gains = from_sections(norm_gains[0], sections)
     others = (out_weights[0], up_weights[0], down_weights[0])
     *others, projs[-1] = lax.optimization_barrier((*others, projs[-1]))
     others = [from_sections(w, sections) for w in others]
-    pairs[-1], others = lax.optimization_barrier((pairs[-1], others))
     projs = [w.transpose(0, 2, 1).reshape(-1, channels) for w in by_layer(projs, section)]
     outs, ups, downs = [[w.T for w in by_layer(slots, section)] for slots in others]
     gains = [
@@ -330,7 +329,7 @@
     scratch = (tiles, channels * rows, LANES)
     edges_out = [((2, 2, block, columns), jnp.bfloat16)] * half
     state_out = [
-        ((rows, channels, columns), jnp.bfloat16), ((rows, channels, columns), jnp.float32)
+        ((rows, channels, columns), jnp.bfloat16), ((rows, channels, columns), jnp.bfloat16)
     ]
     hidden = ups[0].shape[0]
     points = rows * columns

time: 101 us -> 97.6 us (0.966)
  local copies, waits for them, and re-layouts: 7.12 us -> 4.95 us
  waiting for transfers between devices: 31.1 us -> 29.2 us
    unnamed x37 -> x19, local copies, waits for them, and re-layouts: 4.68 us -> 2.48 us
    ppermute x32, waiting for transfers between devices: 6.82 us -> 5.09 us  [exchange(): lax.ppermute(pair, 'axial', [(j, j ^ 1) for j in range(size)])]
    ppermute x2, starting transfers between devices: 6.65 us -> 7.79 us  [move_parts(): lax.ppermute(values, 'axial', [(j, (j + distance * width) % size) for j i...]
  transfers between devices with their start and end apart: 63 -> 63, of which waited for: 28 -> 24; matrix products, arithmetic and copies ran while one was open for 3% -> 3% of each run, Pallas kernels for 9% -> 12%
where the time goes in v1:
time: 97.6 us; the launch traced here: 96.8 us
  starting transfers between devices  46.5 us (48%)
  waiting for transfers between devices  29.2 us (30%)
  Pallas kernels  14.9 us (15%)
  local copies, waits for them, and re-layouts  4.95 us (5%)
  other arithmetic  1.02 us (1%)
    ppermute x24, starting transfers between devices, exchange(): lax.ppermute(blocks[i], 'axial', [(j, j ^ 2 * i) for j in range(size)])  28.6 us
    ppermute x24, waiting for transfers between devices, exchange(): lax.ppermute(blocks[i], 'axial', [(j, j ^ 2 * i) for j in range(size)])  22.3 us
    pallas_call x8, Pallas kernels, pallas(): pl.pallas_call(kernel, out_shape=[jax.ShapeDtypeStruct(shape, dtype) for...  14.9 us
    ppermute x2, starting transfers between devices, move_parts(): lax.ppermute(values, 'axial', [(j, (j + distance * width) % size) for j i...  7.79 us
    ppermute x5, starting transfers between devices, from_sections(): lax.ppermute(weight, 'section', [((i + shift) % sections, i) for i in ran...  5.75 us
    ppermute x32, waiting for transfers between devices, exchange(): lax.ppermute(pair, 'axial', [(j, j ^ 1) for j in range(size)])  5.09 us
    ppermute x32, starting transfers between devices, exchange(): lax.ppermute(pair, 'axial', [(j, j ^ 1) for j in range(size)])  4.36 us
    unnamed x19, local copies, waits for them, and re-layouts  2.48 us
  transfers between devices with their start and end apart: 63, of which 24 were waited for; matrix products, arithmetic and copies ran while one was open for 3% of the time, Pallas kernels for 12%

profile of v1, /device:TPU:0, one launch (start us, length us, event | category | flops | bytes accessed | tf_op | source)
XLA Modules:
  0.0 96.8 jit_solution(3556810888632028815)
XLA Ops:
  1.1 4.1 %collective-permute-start.9 = (bf16[8,128,128]{2,1,0:T(8,128)(2,1)S(1)}, bf16[8,128,128]{2,1,0:T(8,128)(2,1)S(1)}, u32[]{:S(2)}, u32[]{:S(2)}) collective-permute-start(bf16[8,128,128]{2,1,0:T(8,128)(2,1)S(1)} %get-tuple-element.93), channel_id=1, source_target_pairs={{0,8},{1,9},{2,10},{3,11},{4,12},{5,13},{6,14},{7,15},{8,0},{9,1},... | collective-permute-start | bytes 786440 | tf_op jit(solution)/shard_map/ppermute | solution.py:260
  5.3 1.5 %collective-permute-start = (bf16[5,128,128]{2,1,0:T(8,128)(2,1)S(1)}, bf16[5,128,128]{2,1,0:T(8,128)(2,1)S(1)}, u32[]{:S(2)}, u32[]{:S(2)}) collective-permute-start(bf16[5,128,128]{2,1,0:T(8,128)(2,1)S(1)} %bitcast.47), channel_id=1, source_target_pairs={{16,0},{0,16},{17,1},{1,17},{18,2},{2,18},{19,3},{3,19},{20,4},{4,... | collective-permute-start | bytes 491528 | tf_op jit(solution)/shard_map/ppermute | solution.py:267
  11.3 1.4 %shard_map.73 = (bf16[2,2,128,128]{3,2,1,0:T(8,128)(2,1)S(1)}, bf16[2,2,128,128]{3,2,1,0:T(8,128)(2,1)S(1)}, bf16[2,2,128,128]{3,2,1,0:T(8,128)(2,1)S(1)}, bf16[...) custom-call(s32[2]{0:T(128)S(1)} %pad_add_fusion.here, ...), custom_call_target="tpu_custom_call" | custom-call | flops 167772160 | tf_op jit(solution)/shard_map/pallas_call | solution.py:227
  12.7 1.6 %collective-permute-start.2 = (bf16[2,2,128,128]{3,2,1,0:T(8,128)(2,1)S(1)}, bf16[2,2,128,128]{3,2,1,0:T(8,128)(2,1)S(1)}, u32[]{:S(2)}, u32[]{:S(2)}) collective-permute-start(bf16[2,2,128,128]{3,2,1,0:T(8,128)(2,1)S(1)} %get-tuple-element.51), channel_id=1, source_target_pairs={{0,2},{1,3},{2,0},{3,1},{4,6},{5,7},{6,4},{7,5},{8,10},{9,11},{10,... | collective-permute-start | bytes 393224 | tf_op jit(solution)/shard_map/ppermute | solution.py:248
  14.3 1.6 %collective-permute-start.3 = (bf16[2,2,128,128]{3,2,1,0:T(8,128)(2,1)S(1)}, bf16[2,2,128,128]{3,2,1,0:T(8,128)(2,1)S(1)}, u32[]{:S(2)}, u32[]{:S(2)}) collective-permute-start(bf16[2,2,128,128]{3,2,1,0:T(8,128)(2,1)S(1)} %get-tuple-element.52), channel_id=1, source_target_pairs={{0,4},{1,5},{2,6},{3,7},{4,0},{5,1},{6,2},{7,3},{8,12},{9,13},{10,... | collective-permute-start | bytes 393224 | tf_op jit(solution)/shard_map/ppermute | solution.py:248
  17.3 1.4 %shard_map.74 = (bf16[2,2,128,128]{3,2,1,0:T(8,128)(2,1)S(1)}, bf16[2,2,128,128]{3,2,1,0:T(8,128)(2,1)S(1)}, bf16[2,2,128,128]{3,2,1,0:T(8,128)(2,1)S(1)}, bf16[...) custom-call(s32[2]{0:T(128)S(1)} %pad_add_fusion.here, ...), custom_call_target="tpu_custom_call" | custom-call | flops 167772160 | tf_op jit(solution)/shard_map/pallas_call | solution.py:227
  18.6 1.6 %collective-permute-start.10 = (bf16[2,2,128,128]{3,2,1,0:T(8,128)(2,1)S(1)}, bf16[2,2,128,128]{3,2,1,0:T(8,128)(2,1)S(1)}, u32[]{:S(2)}, u32[]{:S(2)}) collective-permute-start(bf16[2,2,128,128]{3,2,1,0:T(8,128)(2,1)S(1)} %get-tuple-element.55), channel_id=1, source_target_pairs={{0,2},{1,3},{2,0},{3,1},{4,6},{5,7},{6,4},{7,5},{8,10},{9,11},{10,... | collective-permute-start | bytes 393224 | tf_op jit(solution)/shard_map/ppermute | solution.py:248
  20.9 1.3 %collective-permute-start.12 = (bf16[2,2,128,128]{3,2,1,0:T(8,128)(2,1)S(1)}, bf16[2,2,128,128]{3,2,1,0:T(8,128)(2,1)S(1)}, u32[]{:S(2)}, u32[]{:S(2)}) collective-permute-start(bf16[2,2,128,128]{3,2,1,0:T(8,128)(2,1)S(1)} %get-tuple-element.57), channel_id=1, source_target_pairs={{0,6},{1,7},{2,4},{3,5},{4,2},{5,3},{6,0},{7,1},{8,14},{9,15},{10,... | collective-permute-start | bytes 393224 | tf_op jit(solution)/shard_map/ppermute | solution.py:248
  22.2 1.7 %collective-permute-done.4.refs_3_ = bf16[2,2,128,128]{3,2,1,0:T(8,128)(2,1)S(1)} collective-permute-done((bf16[2,2,128,128]{3,2,1,0:T(8,128)(2,1)S(1)}, bf16[2,2,128,128]{3,2,1,0:T(8,128)(2,1)S(1)}, u32[]{:S(2)}, u32[]{:S(2)}) %collective-permute-start.4) | collective-permute-done | bytes 131104 | tf_op jit(solution)/shard_map/ppermute | solution.py:248
  24.5 1.9 %collective-permute-done.10.refs_9_ = bf16[2,2,128,128]{3,2,1,0:T(8,128)(2,1)S(1)} collective-permute-done((bf16[2,2,128,128]{3,2,1,0:T(8,128)(2,1)S(1)}, bf16[2,2,128,128]{3,2,1,0:T(8,128)(2,1)S(1)}, u32[]{:S(2)}, u32[]{:S(2)}) %collective-permute-start.10) | collective-permute-done | bytes 131104 | tf_op jit(solution)/shard_map/ppermute | solution.py:248
  26.9 2.6 %collective-permute-done.12.refs_11_ = bf16[2,2,128,128]{3,2,1,0:T(8,128)(2,1)S(1)} collective-permute-done((bf16[2,2,128,128]{3,2,1,0:T(8,128)(2,1)S(1)}, bf16[2,2,128,128]{3,2,1,0:T(8,128)(2,1)S(1)}, u32[]{:S(2)}, u32[]{:S(2)}) %collective-permute-start.12) | collective-permute-done | bytes 131104 | tf_op jit(solution)/shard_map/ppermute | solution.py:248
  30.1 1.5 %collective-permute-start.24 = (bf16[128,128]{0,1:T(8,128)(2,1)S(1)}, bf16[128,128]{0,1:T(8,128)(2,1)}, u32[]{:S(2)}, u32[]{:S(2)}) collective-permute-start(bf16[128,128]{0,1:T(8,128)(2,1)S(1)} %bitcast.48), channel_id=1, source_target_pairs={{16,0},{0,16},{17,1},{1,17},{18,2},{2,18},{19,3},{3,19},{20,4},{4,... | collective-permute-start | bytes 98312 | tf_op jit(solution)/shard_map/ppermute | solution.py:267
  32.3 1.5 %collective-permute-start.26 = (bf16[512,128]{0,1:T(8,128)(2,1)}, bf16[512,128]{0,1:T(8,128)(2,1)S(1)}, u32[]{:S(2)}, u32[]{:S(2)}) collective-permute-start(bf16[512,128]{0,1:T(8,128)(2,1)} %bitcast.43), channel_id=1, source_target_pairs={{16,0},{0,16},{17,1},{1,17},{18,2},{2,18},{19,3},{3,19},{20,4},{4,... | collective-permute-start | bytes 393224 | tf_op jit(solution)/shard_map/ppermute | solution.py:267
  33.8 2.2 %shard_map.75 = (bf16[2,128,128]{2,1,0:T(8,128)(2,1)S(1)}, bf16[2,128,128]{2,1,0:T(8,128)(2,1)S(1)}, bf16[2,128,128]{2,1,0:T(8,128)(2,1)S(1)}, bf16[2,128,128]{2...) custom-call(s32[2]{0:T(128)S(1)} %pad_add_fusion.here, ...), custom_call_target="tpu_custom_call" | custom-call | flops 67108864 | tf_op jit(solution)/shard_map/pallas_call | solution.py:227
  38.1 2.3 %collective-permute-start.36 = (bf16[2,128,128]{2,1,0:T(8,128)(2,1)S(1)}, bf16[2,128,128]{2,1,0:T(8,128)(2,1)S(1)}, u32[]{:S(2)}, u32[]{:S(2)}) collective-permute-start(bf16[2,128,128]{2,1,0:T(8,128)(2,1)S(1)} %get-tuple-element.74), channel_id=1, source_target_pairs={{0,6},{1,7},{2,4},{3,5},{4,2},{5,3},{6,0},{7,1},{8,14},{9,15},{10,... | collective-permute-start | bytes 196616 | tf_op jit(solution)/shard_map/ppermute | solution.py:248
  41.7 1.5 %collective-permute-done.36.refs_3_ = bf16[2,128,128]{2,1,0:T(8,128)(2,1)S(1)} collective-permute-done((bf16[2,128,128]{2,1,0:T(8,128)(2,1)S(1)}, bf16[2,128,128]{2,1,0:T(8,128)(2,1)S(1)}, u32[]{:S(2)}, u32[]{:S(2)}) %collective-permute-start.36) | collective-permute-done | bytes 65568 | tf_op jit(solution)/shard_map/ppermute | solution.py:248
  43.3 2.5 %collective-permute-start.19 = (bf16[2,128,128]{2,1,0:T(8,128)(2,1)S(1)}, bf16[2,128,128]{2,1,0:T(8,128)(2,1)S(1)}, u32[]{:S(2)}, u32[]{:S(2)}) collective-permute-start(bf16[2,128,128]{2,1,0:T(8,128)(2,1)S(1)} %get-tuple-element.61), channel_id=1, source_target_pairs={{0,6},{1,7},{2,4},{3,5},{4,2},{5,3},{6,0},{7,1},{8,14},{9,15},{10,... | collective-permute-start | bytes 196616 | tf_op jit(solution)/shard_map/ppermute | solution.py:248
  47.6 2.2 %shard_map.77 = (bf16[2,2,128,128]{3,2,1,0:T(8,128)(2,1)S(1)}, bf16[2,2,128,128]{3,2,1,0:T(8,128)(2,1)S(1)}, bf16[2,2,128,128]{3,2,1,0:T(8,128)(2,1)S(1)}, bf16[...) custom-call(s32[2]{0:T(128)S(1)} %pad_add_fusion.here, ...), custom_call_target="tpu_custom_call" | custom-call | flops 469762048 | tf_op jit(solution)/shard_map/pallas_call | solution.py:227
  50.9 2.5 %collective-permute-start.43 = (bf16[2,2,128,128]{3,2,1,0:T(8,128)(2,1)S(1)}, bf16[2,2,128,128]{3,2,1,0:T(8,128)(2,1)S(1)}, u32[]{:S(2)}, u32[]{:S(2)}) collective-permute-start(bf16[2,2,128,128]{3,2,1,0:T(8,128)(2,1)S(1)} %get-tuple-element.80), channel_id=1, source_target_pairs={{0,6},{1,7},{2,4},{3,5},{4,2},{5,3},{6,0},{7,1},{8,14},{9,15},{10,... | collective-permute-start | bytes 393224 | tf_op jit(solution)/shard_map/ppermute | solution.py:248
  54.8 2.2 %shard_map.76 = (bf16[2,2,128,128]{3,2,1,0:T(8,128)(2,1)S(1)}, bf16[2,2,128,128]{3,2,1,0:T(8,128)(2,1)S(1)}, bf16[2,2,128,128]{3,2,1,0:T(8,128)(2,1)S(1)}, bf16[...) custom-call(s32[2]{0:T(128)S(1)} %pad_add_fusion.here, ...), custom_call_target="tpu_custom_call" | custom-call | flops 469762048 | tf_op jit(solution)/shard_map/pallas_call | solution.py:227
  58.1 2.5 %collective-permute-start.29 = (bf16[2,2,128,128]{3,2,1,0:T(8,128)(2,1)S(1)}, bf16[2,2,128,128]{3,2,1,0:T(8,128)(2,1)S(1)}, u32[]{:S(2)}, u32[]{:S(2)}) collective-permute-start(bf16[2,2,128,128]{3,2,1,0:T(8,128)(2,1)S(1)} %get-tuple-element.70), channel_id=1, source_target_pairs={{0,6},{1,7},{2,4},{3,5},{4,2},{5,3},{6,0},{7,1},{8,14},{9,15},{10,... | collective-permute-start | bytes 393224 | tf_op jit(solution)/shard_map/ppermute | solution.py:248
  61.1 1.7 %collective-permute-done.27.refs_1_ = bf16[2,2,128,128]{3,2,1,0:T(8,128)(2,1)S(1)} collective-permute-done((bf16[2,2,128,128]{3,2,1,0:T(8,128)(2,1)S(1)}, bf16[2,2,128,128]{3,2,1,0:T(8,128)(2,1)S(1)}, u32[]{:S(2)}, u32[]{:S(2)}) %collective-permute-start.27) | collective-permute-done | bytes 131104 | tf_op jit(solution)/shard_map/ppermute | solution.py:248
  62.8 1.5 %collective-permute-done.28.refs_2_ = bf16[2,2,128,128]{3,2,1,0:T(8,128)(2,1)S(1)} collective-permute-done((bf16[2,2,128,128]{3,2,1,0:T(8,128)(2,1)S(1)}, bf16[2,2,128,128]{3,2,1,0:T(8,128)(2,1)S(1)}, u32[]{:S(2)}, u32[]{:S(2)}) %collective-permute-start.28) | collective-permute-done | bytes 131104 | tf_op jit(solution)/shard_map/ppermute | solution.py:248
  64.3 2.5 %collective-permute-done.29.refs_3_ = bf16[2,2,128,128]{3,2,1,0:T(8,128)(2,1)S(1)} collective-permute-done((bf16[2,2,128,128]{3,2,1,0:T(8,128)(2,1)S(1)}, bf16[2,2,128,128]{3,2,1,0:T(8,128)(2,1)S(1)}, u32[]{:S(2)}, u32[]{:S(2)}) %collective-permute-start.29) | collective-permute-done | bytes 131104 | tf_op jit(solution)/shard_map/ppermute | solution.py:248
  68.7 1.6 %shard_map.78 = (bf16[2,128,128]{2,1,0:T(8,128)(2,1)S(1)}, bf16[2,128,128]{2,1,0:T(8,128)(2,1)S(1)}, bf16[2,128,128]{2,1,0:T(8,128)(2,1)S(1)}, bf16[2,128,128]{2...) custom-call(s32[2]{0:T(128)S(1)} %pad_add_fusion.here, ...), custom_call_target="tpu_custom_call" | custom-call | flops 67108864 | tf_op jit(solution)/shard_map/pallas_call | solution.py:227
  71.5 2.3 %collective-permute-start.57 = (bf16[2,128,128]{2,1,0:T(8,128)(2,1)S(1)}, bf16[2,128,128]{2,1,0:T(8,128)(2,1)S(1)}, u32[]{:S(2)}, u32[]{:S(2)}) collective-permute-start(bf16[2,128,128]{2,1,0:T(8,128)(2,1)S(1)} %get-tuple-element.90), channel_id=1, source_target_pairs={{0,6},{1,7},{2,4},{3,5},{4,2},{5,3},{6,0},{7,1},{8,14},{9,15},{10,... | collective-permute-start | bytes 196616 | tf_op jit(solution)/shard_map/ppermute | solution.py:248
  78.3 1.6 %shard_map.80 = bf16[1,8,128,128]{3,2,1,0:T(8,128)(2,1)S(1)} custom-call(s32[2]{0:T(128)S(1)} %pad_add_fusion.here, bf16[2,128,128]{2,1,0:T(8,128)(2,1)S(1)} %get-tuple-element.87.refs_0_, bf16[2,128,128]{2,1,0:T(8,128)(2,1)S(1)} %collective-permute-done.55.refs_1_, bf16[2,128,128]{2,1,0:T(8,128)(2,1)S(1)} %collective-permute-done.56.refs_2_, ...), custom_call_target="tpu_custom_call" | custom-call | flops 301989888 | tf_op jit(solution)/shard_map/pallas_call | solution.py:227
  80.0 3.7 %collective-permute-start.62 = (bf16[1,8,128,128]{3,2,1,0:T(8,128)(2,1)S(1)}, bf16[1,8,128,128]{3,2,1,0:T(8,128)(2,1)S(1)}, u32[]{:S(2)}, u32[]{:S(2)}) collective-permute-start(bf16[1,8,128,128]{3,2,1,0:T(8,128)(2,1)S(1)} %shard_map.80), channel_id=1, source_target_pairs={{0,8},{1,9},{2,10},{3,11},{4,12},{5,13},{6,14},{7,15},{8,0},{9,1},... | collective-permute-start | bytes 786440 | tf_op jit(solution)/shard_map/ppermute | solution.py:260
  83.6 1.3 %collective-permute-start.48 = (bf16[2,128,128]{2,1,0:T(8,128)(2,1)S(1)}, bf16[2,128,128]{2,1,0:T(8,128)(2,1)S(1)}, u32[]{:S(2)}, u32[]{:S(2)}) collective-permute-start(bf16[2,128,128]{2,1,0:T(8,128)(2,1)S(1)} %get-tuple-element.82), channel_id=1, source_target_pairs={{0,2},{1,3},{2,0},{3,1},{4,6},{5,7},{6,4},{7,5},{8,10},{9,11},{10,... | collective-permute-start | bytes 196616 | tf_op jit(solution)/shard_map/ppermute | solution.py:248
  85.3 1.8 %collective-permute-start.50 = (bf16[2,128,128]{2,1,0:T(8,128)(2,1)S(1)}, bf16[2,128,128]{2,1,0:T(8,128)(2,1)S(1)}, u32[]{:S(2)}, u32[]{:S(2)}) collective-permute-start(bf16[2,128,128]{2,1,0:T(8,128)(2,1)S(1)} %get-tuple-element.84), channel_id=1, source_target_pairs={{0,6},{1,7},{2,4},{3,5},{4,2},{5,3},{6,0},{7,1},{8,14},{9,15},{10,... | collective-permute-start | bytes 196616 | tf_op jit(solution)/shard_map/ppermute | solution.py:248
  87.9 3.8 %collective-permute-done.49.refs_2_ = bf16[2,128,128]{2,1,0:T(8,128)(2,1)S(1)} collective-permute-done((bf16[2,128,128]{2,1,0:T(8,128)(2,1)S(1)}, bf16[2,128,128]{2,1,0:T(8,128)(2,1)S(1)}, u32[]{:S(2)}, u32[]{:S(2)}) %collective-permute-start.49) | collective-permute-done | bytes 65568 | tf_op jit(solution)/shard_map/ppermute | solution.py:248
  93.6 2.4 %shard_map.79 = bf16[2,8,128,128]{3,2,1,0:T(8,128)(2,1)} custom-call(s32[2]{0:T(128)S(1)} %pad_add_fusion.here, bf16[2,128,128]{2,1,0:T(8,128)(2,1)S(1)} %get-tuple-element.81.refs_0_, bf16[2,128,128]{2,1,0:T(8,128)(2,1)S(1)} %collective-permute-done.48.refs_1_, bf16[2,128,128]{2,1,0:T(8,128)(2,1)S(1)} %collective-permute-done.49.refs_2_, ...), custom_call_target="tpu_custom_call" | custom-call | flops 301989888 | tf_op jit(solution)/shard_map/pallas_call | solution.py:227
  (137 shorter events, 30.8 us)
Async XLA Ops:
  1.1 16.2 %collective-permute-start.9 = (bf16[8,128,128]{2,1,0:T(8,128)(2,1)S(1)}, bf16[8,128,128]{2,1,0:T(8,128)(2,1)S(1)}, u32[]{:S(2)}, u32[]{:S(2)}) collective-permute-start(bf16[8,128,128]{2,1,0:T(8,128)(2,1)S(1)} %get-tuple-element.93), channel_id=1, source_target_pairs={{0,8},{1,9},{2,10},{3,11},{4,12},{5,13},{6,14},{7,15},{8,0},{9,1},... | collective-permute-start | bytes 786440 | tf_op jit(solution)/shard_map/ppermute | solution.py:260
  5.3 5.7 %collective-permute-start = (bf16[5,128,128]{2,1,0:T(8,128)(2,1)S(1)}, bf16[5,128,128]{2,1,0:T(8,128)(2,1)S(1)}, u32[]{:S(2)}, u32[]{:S(2)}) collective-permute-start(bf16[5,128,128]{2,1,0:T(8,128)(2,1)S(1)} %bitcast.47), channel_id=1, source_target_pairs={{16,0},{0,16},{17,1},{1,17},{18,2},{2,18},{19,3},{3,19},{20,4},{4,... | collective-permute-start | bytes 491528 | tf_op jit(solution)/shard_map/ppermute | solution.py:267
  12.7 7.6 %collective-permute-start.2 = (bf16[2,2,128,128]{3,2,1,0:T(8,128)(2,1)S(1)}, bf16[2,2,128,128]{3,2,1,0:T(8,128)(2,1)S(1)}, u32[]{:S(2)}, u32[]{:S(2)}) collective-permute-start(bf16[2,2,128,128]{3,2,1,0:T(8,128)(2,1)S(1)} %get-tuple-element.51), channel_id=1, source_target_pairs={{0,2},{1,3},{2,0},{3,1},{4,6},{5,7},{6,4},{7,5},{8,10},{9,11},{10,... | collective-permute-start | bytes 393224 | tf_op jit(solution)/shard_map/ppermute | solution.py:248
  14.3 6.6 %collective-permute-start.3 = (bf16[2,2,128,128]{3,2,1,0:T(8,128)(2,1)S(1)}, bf16[2,2,128,128]{3,2,1,0:T(8,128)(2,1)S(1)}, u32[]{:S(2)}, u32[]{:S(2)}) collective-permute-start(bf16[2,2,128,128]{3,2,1,0:T(8,128)(2,1)S(1)} %get-tuple-element.52), channel_id=1, source_target_pairs={{0,4},{1,5},{2,6},{3,7},{4,0},{5,1},{6,2},{7,3},{8,12},{9,13},{10,... | collective-permute-start | bytes 393224 | tf_op jit(solution)/shard_map/ppermute | solution.py:248
  15.8 8.1 %collective-permute-start.4 = (bf16[2,2,128,128]{3,2,1,0:T(8,128)(2,1)S(1)}, bf16[2,2,128,128]{3,2,1,0:T(8,128)(2,1)S(1)}, u32[]{:S(2)}, u32[]{:S(2)}) collective-permute-start(bf16[2,2,128,128]{3,2,1,0:T(8,128)(2,1)S(1)} %get-tuple-element.53), channel_id=1, source_target_pairs={{0,6},{1,7},{2,4},{3,5},{4,2},{5,3},{6,0},{7,1},{8,14},{9,15},{10,... | collective-permute-start | bytes 393224 | tf_op jit(solution)/shard_map/ppermute | solution.py:248
  16.2 7.7 %collective-permute-start.5 = (bf16[2,2,128,128]{3,2,1,0:T(8,128)(2,1)S(1)}, bf16[2,2,128,128]{3,2,1,0:T(8,128)(2,1)S(1)}, u32[]{:S(2)}, u32[]{:S(2)}) collective-permute-start(bf16[2,2,128,128]{3,2,1,0:T(8,128)(2,1)S(1)} %get-tuple-element.50.refs_0_), channel_id=1, source_target_pairs={{0,1},{1,0},{2,3},{3,2},{4,5},{5,4},{6,7},{7,6},{8,9},{9,8},{10,11... | collective-permute-start | bytes 393224 | tf_op jit(solution)/shard_map/ppermute | solution.py:249
  18.6 7.8 %collective-permute-start.10 = (bf16[2,2,128,128]{3,2,1,0:T(8,128)(2,1)S(1)}, bf16[2,2,128,128]{3,2,1,0:T(8,128)(2,1)S(1)}, u32[]{:S(2)}, u32[]{:S(2)}) collective-permute-start(bf16[2,2,128,128]{3,2,1,0:T(8,128)(2,1)S(1)} %get-tuple-element.55), channel_id=1, source_target_pairs={{0,2},{1,3},{2,0},{3,1},{4,6},{5,7},{6,4},{7,5},{8,10},{9,11},{10,... | collective-permute-start | bytes 393224 | tf_op jit(solution)/shard_map/ppermute | solution.py:248
  20.3 6.4 %collective-permute-start.11 = (bf16[2,2,128,128]{3,2,1,0:T(8,128)(2,1)S(1)}, bf16[2,2,128,128]{3,2,1,0:T(8,128)(2,1)S(1)}, u32[]{:S(2)}, u32[]{:S(2)}) collective-permute-start(bf16[2,2,128,128]{3,2,1,0:T(8,128)(2,1)S(1)} %get-tuple-element.56), channel_id=1, source_target_pairs={{0,4},{1,5},{2,6},{3,7},{4,0},{5,1},{6,2},{7,3},{8,12},{9,13},{10,... | collective-permute-start | bytes 393224 | tf_op jit(solution)/shard_map/ppermute | solution.py:248
  20.9 8.6 %collective-permute-start.12 = (bf16[2,2,128,128]{3,2,1,0:T(8,128)(2,1)S(1)}, bf16[2,2,128,128]{3,2,1,0:T(8,128)(2,1)S(1)}, u32[]{:S(2)}, u32[]{:S(2)}) collective-permute-start(bf16[2,2,128,128]{3,2,1,0:T(8,128)(2,1)S(1)} %get-tuple-element.57), channel_id=1, source_target_pairs={{0,6},{1,7},{2,4},{3,5},{4,2},{5,3},{6,0},{7,1},{8,14},{9,15},{10,... | collective-permute-start | bytes 393224 | tf_op jit(solution)/shard_map/ppermute | solution.py:248
  23.9 5.5 %collective-permute-start.13 = (bf16[2,2,128,128]{3,2,1,0:T(8,128)(2,1)S(1)}, bf16[2,2,128,128]{3,2,1,0:T(8,128)(2,1)S(1)}, u32[]{:S(2)}, u32[]{:S(2)}) collective-permute-start(bf16[2,2,128,128]{3,2,1,0:T(8,128)(2,1)S(1)} %get-tuple-element.54.refs_8_), channel_id=1, source_target_pairs={{0,1},{1,0},{2,3},{3,2},{4,5},{5,4},{6,7},{7,6},{8,9},{9,8},{10,11... | collective-permute-start | bytes 393224 | tf_op jit(solution)/shard_map/ppermute | solution.py:249
  23.9 6.0 %collective-permute-start.6 = (bf16[2,2,128,128]{3,2,1,0:T(8,128)(2,1)S(1)}, bf16[2,2,128,128]{3,2,1,0:T(8,128)(2,1)S(1)}, u32[]{:S(2)}, u32[]{:S(2)}) collective-permute-start(bf16[2,2,128,128]{3,2,1,0:T(8,128)(2,1)S(1)} %collective-permute-done.2.refs_1_), channel_id=1, source_target_pairs={{0,1},{1,0},{2,3},{3,2},{4,5},{5,4},{6,7},{7,6},{8,9},{9,8},{10,11... | collective-permute-start | bytes 393224 | tf_op jit(solution)/shard_map/ppermute | solution.py:249
  30.1 7.3 %collective-permute-start.24 = (bf16[128,128]{0,1:T(8,128)(2,1)S(1)}, bf16[128,128]{0,1:T(8,128)(2,1)}, u32[]{:S(2)}, u32[]{:S(2)}) collective-permute-start(bf16[128,128]{0,1:T(8,128)(2,1)S(1)} %bitcast.48), channel_id=1, source_target_pairs={{16,0},{0,16},{17,1},{1,17},{18,2},{2,18},{19,3},{3,19},{20,4},{4,... | collective-permute-start | bytes 98312 | tf_op jit(solution)/shard_map/ppermute | solution.py:267
  31.7 8.6 %collective-permute-start.25 = (bf16[128,512]{0,1:T(8,128)(2,1)}, bf16[128,512]{0,1:T(8,128)(2,1)S(1)}, u32[]{:S(2)}, u32[]{:S(2)}) collective-permute-start(bf16[128,512]{0,1:T(8,128)(2,1)} %bitcast.45), channel_id=1, source_target_pairs={{16,0},{0,16},{17,1},{1,17},{18,2},{2,18},{19,3},{3,19},{20,4},{4,... | collective-permute-start | bytes 393224 | tf_op jit(solution)/shard_map/ppermute | solution.py:267
  32.3 8.0 %collective-permute-start.26 = (bf16[512,128]{0,1:T(8,128)(2,1)}, bf16[512,128]{0,1:T(8,128)(2,1)S(1)}, u32[]{:S(2)}, u32[]{:S(2)}) collective-permute-start(bf16[512,128]{0,1:T(8,128)(2,1)} %bitcast.43), channel_id=1, source_target_pairs={{16,0},{0,16},{17,1},{1,17},{18,2},{2,18},{19,3},{3,19},{20,4},{4,... | collective-permute-start | bytes 393224 | tf_op jit(solution)/shard_map/ppermute | solution.py:267
  40.4 5.4 %collective-permute-start.37 = (bf16[2,128,128]{2,1,0:T(8,128)(2,1)S(1)}, bf16[2,128,128]{2,1,0:T(8,128)(2,1)S(1)}, u32[]{:S(2)}, u32[]{:S(2)}) collective-permute-start(bf16[2,128,128]{2,1,0:T(8,128)(2,1)S(1)} %get-tuple-element.71.refs_0_), channel_id=1, source_target_pairs={{0,1},{1,0},{2,3},{3,2},{4,5},{5,4},{6,7},{7,6},{8,9},{9,8},{10,11... | collective-permute-start | bytes 196616 | tf_op jit(solution)/shard_map/ppermute | solution.py:249
  40.4 5.4 %collective-permute-start.17 = (bf16[2,128,128]{2,1,0:T(8,128)(2,1)S(1)}, bf16[2,128,128]{2,1,0:T(8,128)(2,1)S(1)}, u32[]{:S(2)}, u32[]{:S(2)}) collective-permute-start(bf16[2,128,128]{2,1,0:T(8,128)(2,1)S(1)} %get-tuple-element.59), channel_id=1, source_target_pairs={{0,2},{1,3},{2,0},{3,1},{4,6},{5,7},{6,4},{7,5},{8,10},{9,11},{10,... | collective-permute-start | bytes 196616 | tf_op jit(solution)/shard_map/ppermute | solution.py:248
  43.3 7.5 %collective-permute-start.19 = (bf16[2,128,128]{2,1,0:T(8,128)(2,1)S(1)}, bf16[2,128,128]{2,1,0:T(8,128)(2,1)S(1)}, u32[]{:S(2)}, u32[]{:S(2)}) collective-permute-start(bf16[2,128,128]{2,1,0:T(8,128)(2,1)S(1)} %get-tuple-element.61), channel_id=1, source_target_pairs={{0,6},{1,7},{2,4},{3,5},{4,2},{5,3},{6,0},{7,1},{8,14},{9,15},{10,... | collective-permute-start | bytes 196616 | tf_op jit(solution)/shard_map/ppermute | solution.py:248
  46.3 7.1 %collective-permute-start.21 = (bf16[2,128,128]{2,1,0:T(8,128)(2,1)S(1)}, bf16[2,128,128]{2,1,0:T(8,128)(2,1)S(1)}, u32[]{:S(2)}, u32[]{:S(2)}) collective-permute-start(bf16[2,128,128]{2,1,0:T(8,128)(2,1)S(1)} %collective-permute-done.17.refs_1_), channel_id=1, source_target_pairs={{0,1},{1,0},{2,3},{3,2},{4,5},{5,4},{6,7},{7,6},{8,9},{9,8},{10,11... | collective-permute-start | bytes 196616 | tf_op jit(solution)/shard_map/ppermute | solution.py:249
  47.2 6.2 %collective-permute-start.22 = (bf16[2,128,128]{2,1,0:T(8,128)(2,1)S(1)}, bf16[2,128,128]{2,1,0:T(8,128)(2,1)S(1)}, u32[]{:S(2)}, u32[]{:S(2)}) collective-permute-start(bf16[2,128,128]{2,1,0:T(8,128)(2,1)S(1)} %collective-permute-done.18.refs_2_), channel_id=1, source_target_pairs={{0,1},{1,0},{2,3},{3,2},{4,5},{5,4},{6,7},{7,6},{8,9},{9,8},{10,11... | collective-permute-start | bytes 196616 | tf_op jit(solution)/shard_map/ppermute | solution.py:249
  49.8 8.1 %collective-permute-start.41 = (bf16[2,2,128,128]{3,2,1,0:T(8,128)(2,1)S(1)}, bf16[2,2,128,128]{3,2,1,0:T(8,128)(2,1)S(1)}, u32[]{:S(2)}, u32[]{:S(2)}) collective-permute-start(bf16[2,2,128,128]{3,2,1,0:T(8,128)(2,1)S(1)} %get-tuple-element.78), channel_id=1, source_target_pairs={{0,2},{1,3},{2,0},{3,1},{4,6},{5,7},{6,4},{7,5},{8,10},{9,11},{10,... | collective-permute-start | bytes 393224 | tf_op jit(solution)/shard_map/ppermute | solution.py:248
  50.8 7.3 %collective-permute-start.42 = (bf16[2,2,128,128]{3,2,1,0:T(8,128)(2,1)S(1)}, bf16[2,2,128,128]{3,2,1,0:T(8,128)(2,1)S(1)}, u32[]{:S(2)}, u32[]{:S(2)}) collective-permute-start(bf16[2,2,128,128]{3,2,1,0:T(8,128)(2,1)S(1)} %get-tuple-element.79), channel_id=1, source_target_pairs={{0,4},{1,5},{2,6},{3,7},{4,0},{5,1},{6,2},{7,3},{8,12},{9,13},{10,... | collective-permute-start | bytes 393224 | tf_op jit(solution)/shard_map/ppermute | solution.py:248
  50.9 9.7 %collective-permute-start.43 = (bf16[2,2,128,128]{3,2,1,0:T(8,128)(2,1)S(1)}, bf16[2,2,128,128]{3,2,1,0:T(8,128)(2,1)S(1)}, u32[]{:S(2)}, u32[]{:S(2)}) collective-permute-start(bf16[2,2,128,128]{3,2,1,0:T(8,128)(2,1)S(1)} %get-tuple-element.80), channel_id=1, source_target_pairs={{0,6},{1,7},{2,4},{3,5},{4,2},{5,3},{6,0},{7,1},{8,14},{9,15},{10,... | collective-permute-start | bytes 393224 | tf_op jit(solution)/shard_map/ppermute | solution.py:248
  53.4 7.2 %collective-permute-start.44 = (bf16[2,2,128,128]{3,2,1,0:T(8,128)(2,1)S(1)}, bf16[2,2,128,128]{3,2,1,0:T(8,128)(2,1)S(1)}, u32[]{:S(2)}, u32[]{:S(2)}) collective-permute-start(bf16[2,2,128,128]{3,2,1,0:T(8,128)(2,1)S(1)} %get-tuple-element.77.refs_8_), channel_id=1, source_target_pairs={{0,1},{1,0},{2,3},{3,2},{4,5},{5,4},{6,7},{7,6},{8,9},{9,8},{10,11... | collective-permute-start | bytes 393224 | tf_op jit(solution)/shard_map/ppermute | solution.py:249
  57.0 5.8 %collective-permute-start.27 = (bf16[2,2,128,128]{3,2,1,0:T(8,128)(2,1)S(1)}, bf16[2,2,128,128]{3,2,1,0:T(8,128)(2,1)S(1)}, u32[]{:S(2)}, u32[]{:S(2)}) collective-permute-start(bf16[2,2,128,128]{3,2,1,0:T(8,128)(2,1)S(1)} %get-tuple-element.68), channel_id=1, source_target_pairs={{0,2},{1,3},{2,0},{3,1},{4,6},{5,7},{6,4},{7,5},{8,10},{9,11},{10,... | collective-permute-start | bytes 393224 | tf_op jit(solution)/shard_map/ppermute | solution.py:248
  58.0 6.4 %collective-permute-start.28 = (bf16[2,2,128,128]{3,2,1,0:T(8,128)(2,1)S(1)}, bf16[2,2,128,128]{3,2,1,0:T(8,128)(2,1)S(1)}, u32[]{:S(2)}, u32[]{:S(2)}) collective-permute-start(bf16[2,2,128,128]{3,2,1,0:T(8,128)(2,1)S(1)} %get-tuple-element.69), channel_id=1, source_target_pairs={{0,4},{1,5},{2,6},{3,7},{4,0},{5,1},{6,2},{7,3},{8,12},{9,13},{10,... | collective-permute-start | bytes 393224 | tf_op jit(solution)/shard_map/ppermute | solution.py:248
  58.1 8.7 %collective-permute-start.29 = (bf16[2,2,128,128]{3,2,1,0:T(8,128)(2,1)S(1)}, bf16[2,2,128,128]{3,2,1,0:T(8,128)(2,1)S(1)}, u32[]{:S(2)}, u32[]{:S(2)}) collective-permute-start(bf16[2,2,128,128]{3,2,1,0:T(8,128)(2,1)S(1)} %get-tuple-element.70), channel_id=1, source_target_pairs={{0,6},{1,7},{2,4},{3,5},{4,2},{5,3},{6,0},{7,1},{8,14},{9,15},{10,... | collective-permute-start | bytes 393224 | tf_op jit(solution)/shard_map/ppermute | solution.py:248
  60.6 6.2 %collective-permute-start.30 = (bf16[2,2,128,128]{3,2,1,0:T(8,128)(2,1)S(1)}, bf16[2,2,128,128]{3,2,1,0:T(8,128)(2,1)S(1)}, u32[]{:S(2)}, u32[]{:S(2)}) collective-permute-start(bf16[2,2,128,128]{3,2,1,0:T(8,128)(2,1)S(1)} %get-tuple-element.67.refs_0_), channel_id=1, source_target_pairs={{0,1},{1,0},{2,3},{3,2},{4,5},{5,4},{6,7},{7,6},{8,9},{9,8},{10,11... | collective-permute-start | bytes 393224 | tf_op jit(solution)/shard_map/ppermute | solution.py:249
  60.6 6.7 %collective-permute-start.45 = (bf16[2,2,128,128]{3,2,1,0:T(8,128)(2,1)S(1)}, bf16[2,2,128,128]{3,2,1,0:T(8,128)(2,1)S(1)}, u32[]{:S(2)}, u32[]{:S(2)}) collective-permute-start(bf16[2,2,128,128]{3,2,1,0:T(8,128)(2,1)S(1)} %collective-permute-done.41.refs_9_), channel_id=1, source_target_pairs={{0,1},{1,0},{2,3},{3,2},{4,5},{5,4},{6,7},{7,6},{8,9},{9,8},{10,11... | collective-permute-start | bytes 393224 | tf_op jit(solution)/shard_map/ppermute | solution.py:249
  71.5 5.6 %collective-permute-start.57 = (bf16[2,128,128]{2,1,0:T(8,128)(2,1)S(1)}, bf16[2,128,128]{2,1,0:T(8,128)(2,1)S(1)}, u32[]{:S(2)}, u32[]{:S(2)}) collective-permute-start(bf16[2,128,128]{2,1,0:T(8,128)(2,1)S(1)} %get-tuple-element.90), channel_id=1, source_target_pairs={{0,6},{1,7},{2,4},{3,5},{4,2},{5,3},{6,0},{7,1},{8,14},{9,15},{10,... | collective-permute-start | bytes 196616 | tf_op jit(solution)/shard_map/ppermute | solution.py:248
  80.0 16.1 %collective-permute-start.62 = (bf16[1,8,128,128]{3,2,1,0:T(8,128)(2,1)S(1)}, bf16[1,8,128,128]{3,2,1,0:T(8,128)(2,1)S(1)}, u32[]{:S(2)}, u32[]{:S(2)}) collective-permute-start(bf16[1,8,128,128]{3,2,1,0:T(8,128)(2,1)S(1)} %shard_map.80), channel_id=1, source_target_pairs={{0,8},{1,9},{2,10},{3,11},{4,12},{5,13},{6,14},{7,15},{8,0},{9,1},... | collective-permute-start | bytes 786440 | tf_op jit(solution)/shard_map/ppermute | solution.py:260
  85.0 6.7 %collective-permute-start.49 = (bf16[2,128,128]{2,1,0:T(8,128)(2,1)S(1)}, bf16[2,128,128]{2,1,0:T(8,128)(2,1)S(1)}, u32[]{:S(2)}, u32[]{:S(2)}) collective-permute-start(bf16[2,128,128]{2,1,0:T(8,128)(2,1)S(1)} %get-tuple-element.83), channel_id=1, source_target_pairs={{0,4},{1,5},{2,6},{3,7},{4,0},{5,1},{6,2},{7,3},{8,12},{9,13},{10,... | collective-permute-start | bytes 196616 | tf_op jit(solution)/shard_map/ppermute | solution.py:248
  85.3 7.1 %collective-permute-start.50 = (bf16[2,128,128]{2,1,0:T(8,128)(2,1)S(1)}, bf16[2,128,128]{2,1,0:T(8,128)(2,1)S(1)}, u32[]{:S(2)}, u32[]{:S(2)}) collective-permute-start(bf16[2,128,128]{2,1,0:T(8,128)(2,1)S(1)} %get-tuple-element.84), channel_id=1, source_target_pairs={{0,6},{1,7},{2,4},{3,5},{4,2},{5,3},{6,0},{7,1},{8,14},{9,15},{10,... | collective-permute-start | bytes 196616 | tf_op jit(solution)/shard_map/ppermute | solution.py:248
  (39 other events, 133.1 us)

commit v2 on v1

--- a/solution.py
+++ b/solution.py
@@ -11,6 +11,7 @@
 epsilon = 1e-05
 LANES = 128
 TOGETHER = 1024
+UNROLL = 4
 VMEM_BYTES = 24 * 1024 * 1024
 
 
@@ -72,18 +73,14 @@
 
 
 def write_edges(left_scr, right_scr, here, edges):
-    block = edges[0].shape[2]
+    block = edges[0].shape[1]
     for which, scr in enumerate((left_scr, right_scr)):
-        for m in range(2 * len(edges)):
-            start = pl.multiple_of((here[0] ^ m) * block, block)
+        for i, edge in enumerate(edges):
+            start = pl.multiple_of((here[0] ^ i) * block, block)
             for tile in range(scr.shape[0]):
-                edges[m // 2][m % 2, which, :, tile * LANES : (tile + 1) * LANES] = scr[
+                edge[which, :, tile * LANES : (tile + 1) * LANES] = scr[
                     tile, pl.ds(start, block), :
                 ].astype(jnp.bfloat16)
-
-
-def arrived(own, cross, m):
-    return cross[m // 2][1] if m % 2 else own[m // 2][0]
 
 
 def repeat(gains, count):
@@ -115,50 +112,46 @@
 
 
 def triangle_kernel(half, chunks, here, *refs):
-    groups = 2 * half
-    sources = [refs[k * groups : (k + 1) * groups] for k in range(chunks)]
-    refs = refs[chunks * groups :]
+    sources = [refs[k * 2 * half : (k + 1) * 2 * half] for k in range(chunks)]
+    refs = refs[chunks * 2 * half :]
     products = [refs[k * half : (k + 1) * half] for k in range(chunks)]
-    wide, sums = refs[chunks * half :]
+    lefts, rights, sums = refs[chunks * half :]
     block, columns = sums.shape[1:]
-    places = groups * chunks
+    places = 2 * half * chunks
     rows = columns // places
-
-    def place_of(k, m):
-        return lax.rem(here[1] + k, chunks) * groups + (here[0] ^ m)
-
     for k in range(chunks):
-        for m in range(groups):
-            values = arrived(sources[k][:half], sources[k][half:], m)
-            for which in range(2):
-                wide[which, place_of(k, m)] = values[which].astype(jnp.float32)
+        for i in range(half):
+            chip = lax.rem(here[2] + k, chunks) * half + (here[0] ^ i)
+            lefts[k * half + i] = sources[k][i][0].astype(jnp.float32)
+            rights[2 * chip + here[1]] = sources[k][i][1].astype(jnp.float32)
+            rights[2 * chip + 1 - here[1]] = sources[k][half + i][1].astype(jnp.float32)
 
     def step(c, carry):
         at = pl.ds(pl.multiple_of(c * rows, rows), rows)
         left, right = [
-            jnp.concatenate([wide[which, p, at, :] for p in range(places)], axis=0).astype(
+            jnp.concatenate([wide[p, at, :] for p in range(wide.shape[0])], axis=0).astype(
                 jnp.bfloat16
             )
-            for which in range(2)
+            for wide in (lefts, rights)
         ]
         total = lax.dot_general(
             left, right, (((1,), (1,)), ((), ())), preferred_element_type=jnp.float32
         )
-        for p in range(places):
+        for p in range(half * chunks):
             sums[p, at, :] = total[p * rows : (p + 1) * rows]
         return carry
 
-    lax.fori_loop(0, block // rows, step, 0, unroll=min(4, block // rows))
+    lax.fori_loop(0, block // rows, step, 0, unroll=min(UNROLL, block // rows))
     for k in range(chunks):
-        for m in range(groups):
-            products[k][m // 2][m % 2] = sums[place_of(k, m)].astype(jnp.bfloat16)
-
-
-def load_product(here, own, cross, prod_scr):
-    block = own[0].shape[1]
-    for m in range(2 * len(own)):
-        values = arrived(own, cross, m).astype(jnp.float32)
-        start = pl.multiple_of((here[0] ^ m) * block, block)
+        for i in range(half):
+            products[k][i][...] = sums[k * half + i].astype(jnp.bfloat16)
+
+
+def load_product(here, own, prod_scr):
+    block = own[0].shape[0]
+    for i, piece in enumerate(own):
+        values = piece[...].astype(jnp.float32)
+        start = pl.multiple_of((here[0] ^ i) * block, block)
         for tile in range(prod_scr.shape[0]):
             prod_scr[tile, pl.ds(start, block), :] = values[:, tile * LANES : (tile + 1) * LANES]
 
@@ -175,13 +168,13 @@
 
 
 def middle_kernel(half, here, *refs):
-    own, cross, refs = refs[:half], refs[half : 2 * half], refs[2 * half :]
+    own, refs = refs[:half], refs[half:]
     pair, gate, out_t, up_t, down_t, gains, mask, proj, next_gains = refs[:9]
     edges, refs = refs[9 : 9 + half], refs[9 + half :]
     next_pair, next_gate, prod_scr, left_scr, right_scr = refs
     rows, _, columns = pair.shape
     count = rows_together(rows, columns)
-    load_product(here, own, cross, prod_scr)
+    load_product(here, own, prod_scr)
 
     def step(i, carry):
         row = i * count
@@ -199,12 +192,12 @@
 
 
 def last_kernel(half, here, *refs):
-    own, cross, refs = refs[:half], refs[half : 2 * half], refs[2 * half :]
+    own, refs = refs[:half], refs[half:]
     pair, gate, out_t, up_t, down_t, gains, result, prod_scr = refs
     rows, _, columns = pair.shape
     count = rows_together(rows, columns)
-    slot = here[1] if result.shape[0] > 1 else 0
-    load_product(here, own, cross, prod_scr)
+    slot = here[2] if result.shape[0] > 1 else 0
+    load_product(here, own, prod_scr)
 
     def step(i, carry):
         row = i * count
@@ -239,14 +232,22 @@
     half = len(blocks)
     if not by_permutes(width):
         whole = lax.all_to_all(
-            jnp.concatenate(blocks), "axial", 0, 0, tiled=True, axis_index_groups=groups
-        )
-        return [whole[2 * i : 2 * i + 2] for i in range(half)] * 2
+            jnp.stack(blocks), "axial", 0, 0, tiled=True, axis_index_groups=groups
+        )
+        return [whole[i] for i in range(half)]
     size = lax.axis_size("axial")
     own = list(blocks)
     for i in range(1, half):
         own[i] = lax.ppermute(blocks[i], "axial", [(j, j ^ (2 * i)) for j in range(size)])
-    return own + [lax.ppermute(pair, "axial", [(j, j ^ 1) for j in range(size)]) for pair in own]
+    return own
+
+
+def with_neighbour(own):
+    swap = [(j, j ^ 1) for j in range(lax.axis_size("axial"))]
+    if not by_permutes(2 * len(own)):
+        whole = lax.ppermute(jnp.stack(own), "axial", swap)
+        return own + [whole[i] for i in range(len(own))]
+    return own + [lax.ppermute(piece, "axial", swap) for piece in own]
 
 
 def by_permutes(width):
@@ -289,10 +290,13 @@
     parts = own_count
     width = axial // parts
     half = width // 2
-    block = channels // width * rows
+    block = channels // half * rows
     part, place = lax.axis_index("axial") // width, lax.axis_index("axial") % width
-    groups = [[p * width + i for i in range(width)] for p in range(parts)]
-    here = jnp.stack((place if by_permutes(width) else 0 * place, part)).astype(jnp.int32)
+    groups = [
+        [p * width + 2 * i + core for i in range(half)] for p in range(parts) for core in range(2)
+    ]
+    chip = place // 2 if by_permutes(width) else 0 * place
+    here = jnp.stack((chip, place % 2, part)).astype(jnp.int32)
 
     pairs = []
     for k in range(parts):
@@ -327,7 +331,7 @@
 
     tiles = columns // LANES
     scratch = (tiles, channels * rows, LANES)
-    edges_out = [((2, 2, block, columns), jnp.bfloat16)] * half
+    edges_out = [((2, block, columns), jnp.bfloat16)] * half
     state_out = [
         ((rows, channels, columns), jnp.bfloat16), ((rows, channels, columns), jnp.bfloat16)
     ]
@@ -341,13 +345,15 @@
             functools.partial(first_kernel, half), edges_out + state_out, [scratch] * 2,
             head_flops, here, pairs[k], masks[k], projs[0], gains[0],
         )
-        edges[k], state[k] = exchange(sent, width, groups), (pair, gate)
+        edges[k] = exchange(sent, width, groups)
+        state[k] = (pair, gate)
     finished = [None] * parts
     for layer in range(sections):
-        places = (parts * width, block, columns)
+        edges = [with_neighbour(edges[k]) for k in range(parts)]
+        sides = [(n * parts * half, block, columns) for n in (1, 2, 1)]
         products = call(
             functools.partial(triangle_kernel, half, parts),
-            [((2, block, columns), jnp.bfloat16)] * (half * parts), [(2,) + places, places],
+            [((block, columns), jnp.bfloat16)] * (half * parts), sides,
             2 * channels // width * columns**3, here, *sum(edges, []),
         )
         last = layer == sections - 1

time: 97.6 us -> 94 us (0.963)
  starting transfers between devices: 46.5 us -> 42.6 us
  Pallas kernels: 14.9 us -> 16.1 us
    ppermute x32 -> x16, waiting for transfers between devices: 5.09 us -> 1.31 us  [with_neighbour(): return own + [lax.ppermute(piece, 'axial', swap) for piece in own]]
    ppermute x32 -> x16, starting transfers between devices: 4.36 us -> 2.13 us  [with_neighbour(): return own + [lax.ppermute(piece, 'axial', swap) for piece in own]]
    ppermute x24, waiting for transfers between devices: 22.3 us -> 24.4 us  [exchange(): lax.ppermute(blocks[i], 'axial', [(j, j ^ 2 * i) for j in range(size)])]
    ppermute x5, waiting for transfers between devices: 0.8 us -> 2.38 us  [from_sections(): lax.ppermute(weight, 'section', [((i + shift) % sections, i) for i in ran...]
    pallas_call x8, Pallas kernels: 14.9 us -> 16.1 us  [pallas(): pl.pallas_call(kernel, out_shape=[jax.ShapeDtypeStruct(shape, dtype) for...]
    unnamed x19 -> x17, local copies, waits for them, and re-layouts: 2.48 us -> 1.79 us
  transfers between devices with their start and end apart: 63 -> 47, of which waited for: 24 -> 22; matrix products, arithmetic and copies ran while one was open for 3% -> 4% of each run, Pallas kernels for 12% -> 13%
where the time goes in v2:
time: 94 us; the launch traced here: 93.7 us
  starting transfers between devices  42.6 us (45%)
  waiting for transfers between devices  29.2 us (31%)
  Pallas kernels  16.1 us (17%)
  local copies, waits for them, and re-layouts  4.25 us (5%)
  other arithmetic  1.23 us (1%)
    ppermute x24, starting transfers between devices, exchange(): lax.ppermute(blocks[i], 'axial', [(j, j ^ 2 * i) for j in range(size)])  28 us
    ppermute x24, waiting for transfers between devices, exchange(): lax.ppermute(blocks[i], 'axial', [(j, j ^ 2 * i) for j in range(size)])  24.4 us
    pallas_call x8, Pallas kernels, pallas(): pl.pallas_call(kernel, out_shape=[jax.ShapeDtypeStruct(shape, dtype) for...  16.1 us
    ppermute x2, starting transfers between devices, move_parts(): lax.ppermute(values, 'axial', [(j, (j + distance * width) % size) for j i...  6.89 us
    ppermute x5, starting transfers between devices, from_sections(): lax.ppermute(weight, 'section', [((i + shift) % sections, i) for i in ran...  5.61 us
    ppermute x5, waiting for transfers between devices, from_sections(): lax.ppermute(weight, 'section', [((i + shift) % sections, i) for i in ran...  2.38 us
    ppermute x16, starting transfers between devices, with_neighbour(): return own + [lax.ppermute(piece, 'axial', swap) for piece in own]  2.13 us
  transfers between devices with their start and end apart: 47, of which 22 were waited for; matrix products, arithmetic and copies ran while one was open for 4% of the time, Pallas kernels for 13%

profile of v2, /device:TPU:0, one launch (start us, length us, event | category | flops | bytes accessed | tf_op | source)
XLA Modules:
  0.0 93.7 jit_solution(9399513771175369038)
XLA Ops:
  1.1 4.1 %collective-permute-start.9 = (bf16[8,128,128]{2,1,0:T(8,128)(2,1)S(1)}, bf16[8,128,128]{2,1,0:T(8,128)(2,1)S(1)}, u32[]{:S(2)}, u32[]{:S(2)}) collective-permute-start(bf16[8,128,128]{2,1,0:T(8,128)(2,1)S(1)} %get-tuple-element.93), channel_id=1, source_target_pairs={{0,8},{1,9},{2,10},{3,11},{4,12},{5,13},{6,14},{7,15},{8,0},{9,1},... | collective-permute-start | bytes 786440 | tf_op jit(solution)/shard_map/ppermute | solution.py:261
  5.3 1.5 %collective-permute-start = (bf16[5,128,128]{2,1,0:T(8,128)(2,1)S(1)}, bf16[5,128,128]{2,1,0:T(8,128)(2,1)S(1)}, u32[]{:S(2)}, u32[]{:S(2)}) collective-permute-start(bf16[5,128,128]{2,1,0:T(8,128)(2,1)S(1)} %bitcast.46), channel_id=1, source_target_pairs={{16,0},{0,16},{17,1},{1,17},{18,2},{2,18},{19,3},{3,19},{20,4},{4,... | collective-permute-start | bytes 491528 | tf_op jit(solution)/shard_map/ppermute | solution.py:268
  9.4 1.6 %collective-permute-done.1 = bf16[3,128]{1,0:T(4,128)(2,1)S(1)} collective-permute-done((bf16[3,128]{1,0:T(4,128)(2,1)S(1)}, bf16[3,128]{1,0:T(4,128)(2,1)S(1)}, u32[]{:S(2)}, u32[]{:S(2)}) %collective-permute-start.1) | collective-permute-done | bytes 800 | tf_op jit(solution)/shard_map/ppermute | solution.py:268
  11.3 1.4 %shard_map.73 = (bf16[2,256,128]{2,1,0:T(8,128)(2,1)S(1)}, bf16[2,256,128]{2,1,0:T(8,128)(2,1)S(1)}, bf16[2,256,128]{2,1,0:T(8,128)(2,1)S(1)}, bf16[2,256,128]{2...) custom-call(s32[3]{0:T(128)S(1)} %pad_add_fusion.here, ...), custom_call_target="tpu_custom_call" | custom-call | flops 167772160 | tf_op jit(solution)/shard_map/pallas_call | solution.py:220
  12.7 1.6 %collective-permute-start.2 = (bf16[2,256,128]{2,1,0:T(8,128)(2,1)S(1)}, bf16[2,256,128]{2,1,0:T(8,128)(2,1)S(1)}, u32[]{:S(2)}, u32[]{:S(2)}) collective-permute-start(bf16[2,256,128]{2,1,0:T(8,128)(2,1)S(1)} %get-tuple-element.51), channel_id=1, source_target_pairs={{0,2},{1,3},{2,0},{3,1},{4,6},{5,7},{6,4},{7,5},{8,10},{9,11},{10,... | collective-permute-start | bytes 393224 | tf_op jit(solution)/shard_map/ppermute | solution.py:241
  14.3 1.5 %collective-permute-start.20 = (bf16[128,128]{0,1:T(8,128)(2,1)S(1)}, bf16[128,128]{0,1:T(8,128)(2,1)S(1)}, u32[]{:S(2)}, u32[]{:S(2)}) collective-permute-start(bf16[128,128]{0,1:T(8,128)(2,1)S(1)} %bitcast.47), channel_id=1, source_target_pairs={{16,0},{0,16},{17,1},{1,17},{18,2},{2,18},{19,3},{3,19},{20,4},{4,... | collective-permute-start | bytes 98312 | tf_op jit(solution)/shard_map/ppermute | solution.py:268
  15.8 1.6 %collective-permute-start.3 = (bf16[2,256,128]{2,1,0:T(8,128)(2,1)S(1)}, bf16[2,256,128]{2,1,0:T(8,128)(2,1)S(1)}, u32[]{:S(2)}, u32[]{:S(2)}) collective-permute-start(bf16[2,256,128]{2,1,0:T(8,128)(2,1)S(1)} %get-tuple-element.52), channel_id=1, source_target_pairs={{0,4},{1,5},{2,6},{3,7},{4,0},{5,1},{6,2},{7,3},{8,12},{9,13},{10,... | collective-permute-start | bytes 393224 | tf_op jit(solution)/shard_map/ppermute | solution.py:241
  17.7 1.4 %shard_map.74 = (bf16[2,256,128]{2,1,0:T(8,128)(2,1)S(1)}, bf16[2,256,128]{2,1,0:T(8,128)(2,1)S(1)}, bf16[2,256,128]{2,1,0:T(8,128)(2,1)S(1)}, bf16[2,256,128]{2...) custom-call(s32[3]{0:T(128)S(1)} %pad_add_fusion.here, ...), custom_call_target="tpu_custom_call" | custom-call | flops 167772160 | tf_op jit(solution)/shard_map/pallas_call | solution.py:220
  20.3 1.5 %collective-permute-start.10 = (bf16[2,256,128]{2,1,0:T(8,128)(2,1)S(1)}, bf16[2,256,128]{2,1,0:T(8,128)(2,1)S(1)}, u32[]{:S(2)}, u32[]{:S(2)}) collective-permute-start(bf16[2,256,128]{2,1,0:T(8,128)(2,1)S(1)} %get-tuple-element.55), channel_id=1, source_target_pairs={{0,2},{1,3},{2,0},{3,1},{4,6},{5,7},{6,4},{7,5},{8,10},{9,11},{10,... | collective-permute-start | bytes 393224 | tf_op jit(solution)/shard_map/ppermute | solution.py:241
  25.4 1.5 %collective-permute-done.10.refs_9_ = bf16[2,256,128]{2,1,0:T(8,128)(2,1)S(1)} collective-permute-done((bf16[2,256,128]{2,1,0:T(8,128)(2,1)S(1)}, bf16[2,256,128]{2,1,0:T(8,128)(2,1)S(1)}, u32[]{:S(2)}, u32[]{:S(2)}) %collective-permute-start.10) | collective-permute-done | bytes 131104 | tf_op jit(solution)/shard_map/ppermute | solution.py:241
  26.9 1.5 %collective-permute-done.11.refs_10_ = bf16[2,256,128]{2,1,0:T(8,128)(2,1)S(1)} collective-permute-done((bf16[2,256,128]{2,1,0:T(8,128)(2,1)S(1)}, bf16[2,256,128]{2,1,0:T(8,128)(2,1)S(1)}, u32[]{:S(2)}, u32[]{:S(2)}) %collective-permute-start.11) | collective-permute-done | bytes 131104 | tf_op jit(solution)/shard_map/ppermute | solution.py:241
  32.2 2.6 %shard_map.75 = (bf16[256,128]{1,0:T(8,128)(2,1)S(1)}, bf16[256,128]{1,0:T(8,128)(2,1)S(1)}, bf16[256,128]{1,0:T(8,128)(2,1)S(1)}, bf16[256,128]{1,0:T(8,128)(2,...) custom-call(s32[3]{0:T(128)S(1)} %pad_add_fusion.here, ...), custom_call_target="tpu_custom_call" | custom-call | flops 67108864 | tf_op jit(solution)/shard_map/pallas_call | solution.py:220
  34.8 1.6 %collective-permute-start.30 = (bf16[256,128]{1,0:T(8,128)(2,1)S(1)}, bf16[256,128]{1,0:T(8,128)(2,1)S(1)}, u32[]{:S(2)}, u32[]{:S(2)}) collective-permute-start(bf16[256,128]{1,0:T(8,128)(2,1)S(1)} %get-tuple-element.72), channel_id=1, source_target_pairs={{0,2},{1,3},{2,0},{3,1},{4,6},{5,7},{6,4},{7,5},{8,10},{9,11},{10,... | collective-permute-start | bytes 196616 | tf_op jit(solution)/shard_map/ppermute | solution.py:241
  38.4 1.5 %collective-permute-start.17 = (bf16[256,128]{1,0:T(8,128)(2,1)S(1)}, bf16[256,128]{1,0:T(8,128)(2,1)S(1)}, u32[]{:S(2)}, u32[]{:S(2)}) collective-permute-start(bf16[256,128]{1,0:T(8,128)(2,1)S(1)} %get-tuple-element.59), channel_id=1, source_target_pairs={{0,2},{1,3},{2,0},{3,1},{4,6},{5,7},{6,4},{7,5},{8,10},{9,11},{10,... | collective-permute-start | bytes 196616 | tf_op jit(solution)/shard_map/ppermute | solution.py:241
  41.1 2.0 %collective-permute-done.32.refs_3_ = bf16[256,128]{1,0:T(8,128)(2,1)S(1)} collective-permute-done((bf16[256,128]{1,0:T(8,128)(2,1)S(1)}, bf16[256,128]{1,0:T(8,128)(2,1)S(1)}, u32[]{:S(2)}, u32[]{:S(2)}) %collective-permute-start.32) | collective-permute-done | bytes 65568 | tf_op jit(solution)/shard_map/ppermute | solution.py:241
  43.2 2.2 %shard_map.77 = (bf16[2,256,128]{2,1,0:T(8,128)(2,1)S(1)}, bf16[2,256,128]{2,1,0:T(8,128)(2,1)S(1)}, bf16[2,256,128]{2,1,0:T(8,128)(2,1)S(1)}, bf16[2,256,128]{2...) custom-call(s32[3]{0:T(128)S(1)} %pad_add_fusion.here, ...), custom_call_target="tpu_custom_call" | custom-call | flops 469762048 | tf_op jit(solution)/shard_map/pallas_call | solution.py:220
  46.8 2.2 %collective-permute-start.35 = (bf16[2,256,128]{2,1,0:T(8,128)(2,1)S(1)}, bf16[2,256,128]{2,1,0:T(8,128)(2,1)S(1)}, u32[]{:S(2)}, u32[]{:S(2)}) collective-permute-start(bf16[2,256,128]{2,1,0:T(8,128)(2,1)S(1)} %get-tuple-element.80), channel_id=1, source_target_pairs={{0,6},{1,7},{2,4},{3,5},{4,2},{5,3},{6,0},{7,1},{8,14},{9,15},{10,... | collective-permute-start | bytes 393224 | tf_op jit(solution)/shard_map/ppermute | solution.py:241
  49.8 4.9 %collective-permute-done.19.refs_3_ = bf16[256,128]{1,0:T(8,128)(2,1)S(1)} collective-permute-done((bf16[256,128]{1,0:T(8,128)(2,1)S(1)}, bf16[256,128]{1,0:T(8,128)(2,1)S(1)}, u32[]{:S(2)}, u32[]{:S(2)}) %collective-permute-start.19) | collective-permute-done | bytes 65568 | tf_op jit(solution)/shard_map/ppermute | solution.py:241
  54.7 2.2 %shard_map.76 = (bf16[2,256,128]{2,1,0:T(8,128)(2,1)S(1)}, bf16[2,256,128]{2,1,0:T(8,128)(2,1)S(1)}, bf16[2,256,128]{2,1,0:T(8,128)(2,1)S(1)}, bf16[2,256,128]{2...) custom-call(s32[3]{0:T(128)S(1)} %pad_add_fusion.here, ...), custom_call_target="tpu_custom_call" | custom-call | flops 469762048 | tf_op jit(solution)/shard_map/pallas_call | solution.py:220
  59.1 1.4 %collective-permute-start.25 = (bf16[2,256,128]{2,1,0:T(8,128)(2,1)S(1)}, bf16[2,256,128]{2,1,0:T(8,128)(2,1)S(1)}, u32[]{:S(2)}, u32[]{:S(2)}) collective-permute-start(bf16[2,256,128]{2,1,0:T(8,128)(2,1)S(1)} %get-tuple-element.70), channel_id=1, source_target_pairs={{0,6},{1,7},{2,4},{3,5},{4,2},{5,3},{6,0},{7,1},{8,14},{9,15},{10,... | collective-permute-start | bytes 393224 | tf_op jit(solution)/shard_map/ppermute | solution.py:241
  61.0 1.4 %collective-permute-done.23.refs_1_ = bf16[2,256,128]{2,1,0:T(8,128)(2,1)S(1)} collective-permute-done((bf16[2,256,128]{2,1,0:T(8,128)(2,1)S(1)}, bf16[2,256,128]{2,1,0:T(8,128)(2,1)S(1)}, u32[]{:S(2)}, u32[]{:S(2)}) %collective-permute-start.23) | collective-permute-done | bytes 131104 | tf_op jit(solution)/shard_map/ppermute | solution.py:241
  62.4 1.6 %collective-permute-done.24.refs_2_ = bf16[2,256,128]{2,1,0:T(8,128)(2,1)S(1)} collective-permute-done((bf16[2,256,128]{2,1,0:T(8,128)(2,1)S(1)}, bf16[2,256,128]{2,1,0:T(8,128)(2,1)S(1)}, u32[]{:S(2)}, u32[]{:S(2)}) %collective-permute-start.24) | collective-permute-done | bytes 131104 | tf_op jit(solution)/shard_map/ppermute | solution.py:241
  64.1 2.1 %collective-permute-done.25.refs_3_ = bf16[2,256,128]{2,1,0:T(8,128)(2,1)S(1)} collective-permute-done((bf16[2,256,128]{2,1,0:T(8,128)(2,1)S(1)}, bf16[2,256,128]{2,1,0:T(8,128)(2,1)S(1)}, u32[]{:S(2)}, u32[]{:S(2)}) %collective-permute-start.25) | collective-permute-done | bytes 131104 | tf_op jit(solution)/shard_map/ppermute | solution.py:241
  68.0 2.4 %shard_map.78 = (bf16[256,128]{1,0:T(8,128)(2,1)S(1)}, bf16[256,128]{1,0:T(8,128)(2,1)S(1)}, bf16[256,128]{1,0:T(8,128)(2,1)S(1)}, bf16[256,128]{1,0:T(8,128)(2,...) custom-call(s32[3]{0:T(128)S(1)} %pad_add_fusion.here, ...), custom_call_target="tpu_custom_call" | custom-call | flops 67108864 | tf_op jit(solution)/shard_map/pallas_call | solution.py:220
  72.3 1.7 %collective-permute-start.45 = (bf16[256,128]{1,0:T(8,128)(2,1)S(1)}, bf16[256,128]{1,0:T(8,128)(2,1)S(1)}, u32[]{:S(2)}, u32[]{:S(2)}) collective-permute-start(bf16[256,128]{1,0:T(8,128)(2,1)S(1)} %get-tuple-element.90), channel_id=1, source_target_pairs={{0,6},{1,7},{2,4},{3,5},{4,2},{5,3},{6,0},{7,1},{8,14},{9,15},{10,... | collective-permute-start | bytes 196616 | tf_op jit(solution)/shard_map/ppermute | solution.py:241
  75.9 1.6 %collective-permute-done.45.refs_3_ = bf16[256,128]{1,0:T(8,128)(2,1)S(1)} collective-permute-done((bf16[256,128]{1,0:T(8,128)(2,1)S(1)}, bf16[256,128]{1,0:T(8,128)(2,1)S(1)}, u32[]{:S(2)}, u32[]{:S(2)}) %collective-permute-start.45) | collective-permute-done | bytes 65568 | tf_op jit(solution)/shard_map/ppermute | solution.py:241
  77.5 1.6 %shard_map.80 = bf16[1,8,128,128]{3,2,1,0:T(8,128)(2,1)S(1)} custom-call(s32[3]{0:T(128)S(1)} %pad_add_fusion.here, bf16[256,128]{1,0:T(8,128)(2,1)S(1)} %get-tuple-element.87.refs_0_, bf16[256,128]{1,0:T(8,128)(2,1)S(1)} %collective-permute-done.43.refs_1_, bf16[256,128]{1,0:T(8,128)(2,1)S(1)} %collective-permute-done.44.refs_2_, ...), custom_call_target="tpu_custom_call" | custom-call | flops 301989888 | tf_op jit(solution)/shard_map/pallas_call | solution.py:220
  79.1 2.7 %collective-permute-start.46 = (bf16[1,8,128,128]{3,2,1,0:T(8,128)(2,1)S(1)}, bf16[1,8,128,128]{3,2,1,0:T(8,128)(2,1)S(1)}, u32[]{:S(2)}, u32[]{:S(2)}) collective-permute-start(bf16[1,8,128,128]{3,2,1,0:T(8,128)(2,1)S(1)} %shard_map.80), channel_id=1, source_target_pairs={{0,8},{1,9},{2,10},{3,11},{4,12},{5,13},{6,14},{7,15},{8,0},{9,1},... | collective-permute-start | bytes 786440 | tf_op jit(solution)/shard_map/ppermute | solution.py:261
  84.1 1.3 %collective-permute-start.42 = (bf16[256,128]{1,0:T(8,128)(2,1)S(1)}, bf16[256,128]{1,0:T(8,128)(2,1)S(1)}, u32[]{:S(2)}, u32[]{:S(2)}) collective-permute-start(bf16[256,128]{1,0:T(8,128)(2,1)S(1)} %get-tuple-element.84), channel_id=1, source_target_pairs={{0,6},{1,7},{2,4},{3,5},{4,2},{5,3},{6,0},{7,1},{8,14},{9,15},{10,... | collective-permute-start | bytes 196616 | tf_op jit(solution)/shard_map/ppermute | solution.py:241
  85.4 1.5 %collective-permute-done.40.refs_1_ = bf16[256,128]{1,0:T(8,128)(2,1)S(1)} collective-permute-done((bf16[256,128]{1,0:T(8,128)(2,1)S(1)}, bf16[256,128]{1,0:T(8,128)(2,1)S(1)}, u32[]{:S(2)}, u32[]{:S(2)}) %collective-permute-start.40) | collective-permute-done | bytes 65568 | tf_op jit(solution)/shard_map/ppermute | solution.py:241
  86.9 1.9 %collective-permute-done.41.refs_2_ = bf16[256,128]{1,0:T(8,128)(2,1)S(1)} collective-permute-done((bf16[256,128]{1,0:T(8,128)(2,1)S(1)}, bf16[256,128]{1,0:T(8,128)(2,1)S(1)}, u32[]{:S(2)}, u32[]{:S(2)}) %collective-permute-start.41) | collective-permute-done | bytes 65568 | tf_op jit(solution)/shard_map/ppermute | solution.py:241
  89.5 2.4 %shard_map.79 = bf16[2,8,128,128]{3,2,1,0:T(8,128)(2,1)} custom-call(s32[3]{0:T(128)S(1)} %pad_add_fusion.here, bf16[256,128]{1,0:T(8,128)(2,1)S(1)} %get-tuple-element.81.refs_0_, bf16[256,128]{1,0:T(8,128)(2,1)S(1)} %collective-permute-done.40.refs_1_, bf16[256,128]{1,0:T(8,128)(2,1)S(1)} %collective-permute-done.41.refs_2_, ...), custom_call_target="tpu_custom_call" | custom-call | flops 301989888 | tf_op jit(solution)/shard_map/pallas_call | solution.py:220
  (103 shorter events, 31.4 us)
Async XLA Ops:
  1.1 16.6 %collective-permute-start.9 = (bf16[8,128,128]{2,1,0:T(8,128)(2,1)S(1)}, bf16[8,128,128]{2,1,0:T(8,128)(2,1)S(1)}, u32[]{:S(2)}, u32[]{:S(2)}) collective-permute-start(bf16[8,128,128]{2,1,0:T(8,128)(2,1)S(1)} %get-tuple-element.93), channel_id=1, source_target_pairs={{0,8},{1,9},{2,10},{3,11},{4,12},{5,13},{6,14},{7,15},{8,0},{9,1},... | collective-permute-start | bytes 786440 | tf_op jit(solution)/shard_map/ppermute | solution.py:261
  5.3 5.7 %collective-permute-start = (bf16[5,128,128]{2,1,0:T(8,128)(2,1)S(1)}, bf16[5,128,128]{2,1,0:T(8,128)(2,1)S(1)}, u32[]{:S(2)}, u32[]{:S(2)}) collective-permute-start(bf16[5,128,128]{2,1,0:T(8,128)(2,1)S(1)} %bitcast.46), channel_id=1, source_target_pairs={{16,0},{0,16},{17,1},{1,17},{18,2},{2,18},{19,3},{3,19},{20,4},{4,... | collective-permute-start | bytes 491528 | tf_op jit(solution)/shard_map/ppermute | solution.py:268
  12.7 7.6 %collective-permute-start.2 = (bf16[2,256,128]{2,1,0:T(8,128)(2,1)S(1)}, bf16[2,256,128]{2,1,0:T(8,128)(2,1)S(1)}, u32[]{:S(2)}, u32[]{:S(2)}) collective-permute-start(bf16[2,256,128]{2,1,0:T(8,128)(2,1)S(1)} %get-tuple-element.51), channel_id=1, source_target_pairs={{0,2},{1,3},{2,0},{3,1},{4,6},{5,7},{6,4},{7,5},{8,10},{9,11},{10,... | collective-permute-start | bytes 393224 | tf_op jit(solution)/shard_map/ppermute | solution.py:241
  15.8 6.2 %collective-permute-start.3 = (bf16[2,256,128]{2,1,0:T(8,128)(2,1)S(1)}, bf16[2,256,128]{2,1,0:T(8,128)(2,1)S(1)}, u32[]{:S(2)}, u32[]{:S(2)}) collective-permute-start(bf16[2,256,128]{2,1,0:T(8,128)(2,1)S(1)} %get-tuple-element.52), channel_id=1, source_target_pairs={{0,4},{1,5},{2,6},{3,7},{4,0},{5,1},{6,2},{7,3},{8,12},{9,13},{10,... | collective-permute-start | bytes 393224 | tf_op jit(solution)/shard_map/ppermute | solution.py:241
  17.3 6.5 %collective-permute-start.4 = (bf16[2,256,128]{2,1,0:T(8,128)(2,1)S(1)}, bf16[2,256,128]{2,1,0:T(8,128)(2,1)S(1)}, u32[]{:S(2)}, u32[]{:S(2)}) collective-permute-start(bf16[2,256,128]{2,1,0:T(8,128)(2,1)S(1)} %get-tuple-element.53), channel_id=1, source_target_pairs={{0,6},{1,7},{2,4},{3,5},{4,2},{5,3},{6,0},{7,1},{8,14},{9,15},{10,... | collective-permute-start | bytes 393224 | tf_op jit(solution)/shard_map/ppermute | solution.py:241
  17.7 6.9 %collective-permute-start.5 = (bf16[2,256,128]{2,1,0:T(8,128)(2,1)S(1)}, bf16[2,256,128]{2,1,0:T(8,128)(2,1)S(1)}, u32[]{:S(2)}, u32[]{:S(2)}) collective-permute-start(bf16[2,256,128]{2,1,0:T(8,128)(2,1)S(1)} %get-tuple-element.50.refs_0_), channel_id=1, source_target_pairs={{0,1},{1,0},{2,3},{3,2},{4,5},{5,4},{6,7},{7,6},{8,9},{9,8},{10,11... | collective-permute-start | bytes 393224 | tf_op jit(solution)/shard_map/ppermute | solution.py:250
  19.1 6.3 %collective-permute-start.21 = (bf16[128,512]{0,1:T(8,128)(2,1)}, bf16[128,512]{0,1:T(8,128)(2,1)}, u32[]{:S(2)}, u32[]{:S(2)}) collective-permute-start(bf16[128,512]{0,1:T(8,128)(2,1)} %bitcast.7), channel_id=1, source_target_pairs={{16,0},{0,16},{17,1},{1,17},{18,2},{2,18},{19,3},{3,19},{20,4},{4,... | collective-permute-start | bytes 393224 | tf_op jit(solution)/shard_map/ppermute | solution.py:268
  20.3 6.6 %collective-permute-start.10 = (bf16[2,256,128]{2,1,0:T(8,128)(2,1)S(1)}, bf16[2,256,128]{2,1,0:T(8,128)(2,1)S(1)}, u32[]{:S(2)}, u32[]{:S(2)}) collective-permute-start(bf16[2,256,128]{2,1,0:T(8,128)(2,1)S(1)} %get-tuple-element.55), channel_id=1, source_target_pairs={{0,2},{1,3},{2,0},{3,1},{4,6},{5,7},{6,4},{7,5},{8,10},{9,11},{10,... | collective-permute-start | bytes 393224 | tf_op jit(solution)/shard_map/ppermute | solution.py:241
  22.0 6.4 %collective-permute-start.11 = (bf16[2,256,128]{2,1,0:T(8,128)(2,1)S(1)}, bf16[2,256,128]{2,1,0:T(8,128)(2,1)S(1)}, u32[]{:S(2)}, u32[]{:S(2)}) collective-permute-start(bf16[2,256,128]{2,1,0:T(8,128)(2,1)S(1)} %get-tuple-element.56), channel_id=1, source_target_pairs={{0,4},{1,5},{2,6},{3,7},{4,0},{5,1},{6,2},{7,3},{8,12},{9,13},{10,... | collective-permute-start | bytes 393224 | tf_op jit(solution)/shard_map/ppermute | solution.py:241
  23.9 6.3 %collective-permute-start.12 = (bf16[2,256,128]{2,1,0:T(8,128)(2,1)S(1)}, bf16[2,256,128]{2,1,0:T(8,128)(2,1)S(1)}, u32[]{:S(2)}, u32[]{:S(2)}) collective-permute-start(bf16[2,256,128]{2,1,0:T(8,128)(2,1)S(1)} %get-tuple-element.57), channel_id=1, source_target_pairs={{0,6},{1,7},{2,4},{3,5},{4,2},{5,3},{6,0},{7,1},{8,14},{9,15},{10,... | collective-permute-start | bytes 393224 | tf_op jit(solution)/shard_map/ppermute | solution.py:241
  24.6 5.5 %collective-permute-start.13 = (bf16[2,256,128]{2,1,0:T(8,128)(2,1)S(1)}, bf16[2,256,128]{2,1,0:T(8,128)(2,1)S(1)}, u32[]{:S(2)}, u32[]{:S(2)}) collective-permute-start(bf16[2,256,128]{2,1,0:T(8,128)(2,1)S(1)} %get-tuple-element.54.refs_8_), channel_id=1, source_target_pairs={{0,1},{1,0},{2,3},{3,2},{4,5},{5,4},{6,7},{7,6},{8,9},{9,8},{10,11... | collective-permute-start | bytes 393224 | tf_op jit(solution)/shard_map/ppermute | solution.py:250
  25.4 5.3 %collective-permute-start.6 = (bf16[2,256,128]{2,1,0:T(8,128)(2,1)S(1)}, bf16[2,256,128]{2,1,0:T(8,128)(2,1)S(1)}, u32[]{:S(2)}, u32[]{:S(2)}) collective-permute-start(bf16[2,256,128]{2,1,0:T(8,128)(2,1)S(1)} %collective-permute-done.2.refs_1_), channel_id=1, source_target_pairs={{0,1},{1,0},{2,3},{3,2},{4,5},{5,4},{6,7},{7,6},{8,9},{9,8},{10,11... | collective-permute-start | bytes 393224 | tf_op jit(solution)/shard_map/ppermute | solution.py:250
  28.4 11.5 %collective-permute-start.22 = (bf16[512,128]{0,1:T(8,128)(2,1)S(1)}, bf16[512,128]{0,1:T(8,128)(2,1)S(1)}, u32[]{:S(2)}, u32[]{:S(2)}) collective-permute-start(bf16[512,128]{0,1:T(8,128)(2,1)S(1)} %bitcast.44), channel_id=1, source_target_pairs={{16,0},{0,16},{17,1},{1,17},{18,2},{2,18},{19,3},{3,19},{20,4},{4,... | collective-permute-start | bytes 393224 | tf_op jit(solution)/shard_map/ppermute | solution.py:268
  34.8 6.2 %collective-permute-start.30 = (bf16[256,128]{1,0:T(8,128)(2,1)S(1)}, bf16[256,128]{1,0:T(8,128)(2,1)S(1)}, u32[]{:S(2)}, u32[]{:S(2)}) collective-permute-start(bf16[256,128]{1,0:T(8,128)(2,1)S(1)} %get-tuple-element.72), channel_id=1, source_target_pairs={{0,2},{1,3},{2,0},{3,1},{4,6},{5,7},{6,4},{7,5},{8,10},{9,11},{10,... | collective-permute-start | bytes 196616 | tf_op jit(solution)/shard_map/ppermute | solution.py:241
  37.4 5.7 %collective-permute-start.32 = (bf16[256,128]{1,0:T(8,128)(2,1)S(1)}, bf16[256,128]{1,0:T(8,128)(2,1)S(1)}, u32[]{:S(2)}, u32[]{:S(2)}) collective-permute-start(bf16[256,128]{1,0:T(8,128)(2,1)S(1)} %get-tuple-element.74), channel_id=1, source_target_pairs={{0,6},{1,7},{2,4},{3,5},{4,2},{5,3},{6,0},{7,1},{8,14},{9,15},{10,... | collective-permute-start | bytes 196616 | tf_op jit(solution)/shard_map/ppermute | solution.py:241
  38.4 10.6 %collective-permute-start.17 = (bf16[256,128]{1,0:T(8,128)(2,1)S(1)}, bf16[256,128]{1,0:T(8,128)(2,1)S(1)}, u32[]{:S(2)}, u32[]{:S(2)}) collective-permute-start(bf16[256,128]{1,0:T(8,128)(2,1)S(1)} %get-tuple-element.59), channel_id=1, source_target_pairs={{0,2},{1,3},{2,0},{3,1},{4,6},{5,7},{6,4},{7,5},{8,10},{9,11},{10,... | collective-permute-start | bytes 196616 | tf_op jit(solution)/shard_map/ppermute | solution.py:241
  39.9 9.1 %collective-permute-start.18 = (bf16[256,128]{1,0:T(8,128)(2,1)S(1)}, bf16[256,128]{1,0:T(8,128)(2,1)S(1)}, u32[]{:S(2)}, u32[]{:S(2)}) collective-permute-start(bf16[256,128]{1,0:T(8,128)(2,1)S(1)} %get-tuple-element.60), channel_id=1, source_target_pairs={{0,4},{1,5},{2,6},{3,7},{4,0},{5,1},{6,2},{7,3},{8,12},{9,13},{10,... | collective-permute-start | bytes 196616 | tf_op jit(solution)/shard_map/ppermute | solution.py:241
  45.4 12.6 %collective-permute-start.33 = (bf16[2,256,128]{2,1,0:T(8,128)(2,1)S(1)}, bf16[2,256,128]{2,1,0:T(8,128)(2,1)S(1)}, u32[]{:S(2)}, u32[]{:S(2)}) collective-permute-start(bf16[2,256,128]{2,1,0:T(8,128)(2,1)S(1)} %get-tuple-element.78), channel_id=1, source_target_pairs={{0,2},{1,3},{2,0},{3,1},{4,6},{5,7},{6,4},{7,5},{8,10},{9,11},{10,... | collective-permute-start | bytes 393224 | tf_op jit(solution)/shard_map/ppermute | solution.py:241
  45.8 13.3 %collective-permute-start.34 = (bf16[2,256,128]{2,1,0:T(8,128)(2,1)S(1)}, bf16[2,256,128]{2,1,0:T(8,128)(2,1)S(1)}, u32[]{:S(2)}, u32[]{:S(2)}) collective-permute-start(bf16[2,256,128]{2,1,0:T(8,128)(2,1)S(1)} %get-tuple-element.79), channel_id=1, source_target_pairs={{0,4},{1,5},{2,6},{3,7},{4,0},{5,1},{6,2},{7,3},{8,12},{9,13},{10,... | collective-permute-start | bytes 393224 | tf_op jit(solution)/shard_map/ppermute | solution.py:241
  46.8 13.7 %collective-permute-start.35 = (bf16[2,256,128]{2,1,0:T(8,128)(2,1)S(1)}, bf16[2,256,128]{2,1,0:T(8,128)(2,1)S(1)}, u32[]{:S(2)}, u32[]{:S(2)}) collective-permute-start(bf16[2,256,128]{2,1,0:T(8,128)(2,1)S(1)} %get-tuple-element.80), channel_id=1, source_target_pairs={{0,6},{1,7},{2,4},{3,5},{4,2},{5,3},{6,0},{7,1},{8,14},{9,15},{10,... | collective-permute-start | bytes 393224 | tf_op jit(solution)/shard_map/ppermute | solution.py:241
  49.0 11.5 %collective-permute-start.36 = (bf16[2,256,128]{2,1,0:T(8,128)(2,1)S(1)}, bf16[2,256,128]{2,1,0:T(8,128)(2,1)S(1)}, u32[]{:S(2)}, u32[]{:S(2)}) collective-permute-start(bf16[2,256,128]{2,1,0:T(8,128)(2,1)S(1)} %get-tuple-element.77.refs_8_), channel_id=1, source_target_pairs={{0,1},{1,0},{2,3},{3,2},{4,5},{5,4},{6,7},{7,6},{8,9},{9,8},{10,11... | collective-permute-start | bytes 393224 | tf_op jit(solution)/shard_map/ppermute | solution.py:250
  49.0 5.7 %collective-permute-start.19 = (bf16[256,128]{1,0:T(8,128)(2,1)S(1)}, bf16[256,128]{1,0:T(8,128)(2,1)S(1)}, u32[]{:S(2)}, u32[]{:S(2)}) collective-permute-start(bf16[256,128]{1,0:T(8,128)(2,1)S(1)} %get-tuple-element.61), channel_id=1, source_target_pairs={{0,6},{1,7},{2,4},{3,5},{4,2},{5,3},{6,0},{7,1},{8,14},{9,15},{10,... | collective-permute-start | bytes 196616 | tf_op jit(solution)/shard_map/ppermute | solution.py:241
  56.9 5.5 %collective-permute-start.23 = (bf16[2,256,128]{2,1,0:T(8,128)(2,1)S(1)}, bf16[2,256,128]{2,1,0:T(8,128)(2,1)S(1)}, u32[]{:S(2)}, u32[]{:S(2)}) collective-permute-start(bf16[2,256,128]{2,1,0:T(8,128)(2,1)S(1)} %get-tuple-element.68), channel_id=1, source_target_pairs={{0,2},{1,3},{2,0},{3,1},{4,6},{5,7},{6,4},{7,5},{8,10},{9,11},{10,... | collective-permute-start | bytes 393224 | tf_op jit(solution)/shard_map/ppermute | solution.py:241
  58.1 6.0 %collective-permute-start.24 = (bf16[2,256,128]{2,1,0:T(8,128)(2,1)S(1)}, bf16[2,256,128]{2,1,0:T(8,128)(2,1)S(1)}, u32[]{:S(2)}, u32[]{:S(2)}) collective-permute-start(bf16[2,256,128]{2,1,0:T(8,128)(2,1)S(1)} %get-tuple-element.69), channel_id=1, source_target_pairs={{0,4},{1,5},{2,6},{3,7},{4,0},{5,1},{6,2},{7,3},{8,12},{9,13},{10,... | collective-permute-start | bytes 393224 | tf_op jit(solution)/shard_map/ppermute | solution.py:241
  59.1 7.1 %collective-permute-start.25 = (bf16[2,256,128]{2,1,0:T(8,128)(2,1)S(1)}, bf16[2,256,128]{2,1,0:T(8,128)(2,1)S(1)}, u32[]{:S(2)}, u32[]{:S(2)}) collective-permute-start(bf16[2,256,128]{2,1,0:T(8,128)(2,1)S(1)} %get-tuple-element.70), channel_id=1, source_target_pairs={{0,6},{1,7},{2,4},{3,5},{4,2},{5,3},{6,0},{7,1},{8,14},{9,15},{10,... | collective-permute-start | bytes 393224 | tf_op jit(solution)/shard_map/ppermute | solution.py:241
  60.5 5.7 %collective-permute-start.26 = (bf16[2,256,128]{2,1,0:T(8,128)(2,1)S(1)}, bf16[2,256,128]{2,1,0:T(8,128)(2,1)S(1)}, u32[]{:S(2)}, u32[]{:S(2)}) collective-permute-start(bf16[2,256,128]{2,1,0:T(8,128)(2,1)S(1)} %get-tuple-element.67.refs_0_), channel_id=1, source_target_pairs={{0,1},{1,0},{2,3},{3,2},{4,5},{5,4},{6,7},{7,6},{8,9},{9,8},{10,11... | collective-permute-start | bytes 393224 | tf_op jit(solution)/shard_map/ppermute | solution.py:250
  60.5 6.2 %collective-permute-start.37 = (bf16[2,256,128]{2,1,0:T(8,128)(2,1)S(1)}, bf16[2,256,128]{2,1,0:T(8,128)(2,1)S(1)}, u32[]{:S(2)}, u32[]{:S(2)}) collective-permute-start(bf16[2,256,128]{2,1,0:T(8,128)(2,1)S(1)} %collective-permute-done.33.refs_9_), channel_id=1, source_target_pairs={{0,1},{1,0},{2,3},{3,2},{4,5},{5,4},{6,7},{7,6},{8,9},{9,8},{10,11... | collective-permute-start | bytes 393224 | tf_op jit(solution)/shard_map/ppermute | solution.py:250
  72.3 5.2 %collective-permute-start.45 = (bf16[256,128]{1,0:T(8,128)(2,1)S(1)}, bf16[256,128]{1,0:T(8,128)(2,1)S(1)}, u32[]{:S(2)}, u32[]{:S(2)}) collective-permute-start(bf16[256,128]{1,0:T(8,128)(2,1)S(1)} %get-tuple-element.90), channel_id=1, source_target_pairs={{0,6},{1,7},{2,4},{3,5},{4,2},{5,3},{6,0},{7,1},{8,14},{9,15},{10,... | collective-permute-start | bytes 196616 | tf_op jit(solution)/shard_map/ppermute | solution.py:241
  79.1 13.9 %collective-permute-start.46 = (bf16[1,8,128,128]{3,2,1,0:T(8,128)(2,1)S(1)}, bf16[1,8,128,128]{3,2,1,0:T(8,128)(2,1)S(1)}, u32[]{:S(2)}, u32[]{:S(2)}) collective-permute-start(bf16[1,8,128,128]{3,2,1,0:T(8,128)(2,1)S(1)} %shard_map.80), channel_id=1, source_target_pairs={{0,8},{1,9},{2,10},{3,11},{4,12},{5,13},{6,14},{7,15},{8,0},{9,1},... | collective-permute-start | bytes 786440 | tf_op jit(solution)/shard_map/ppermute | solution.py:261
  81.9 5.0 %collective-permute-start.40 = (bf16[256,128]{1,0:T(8,128)(2,1)S(1)}, bf16[256,128]{1,0:T(8,128)(2,1)S(1)}, u32[]{:S(2)}, u32[]{:S(2)}) collective-permute-start(bf16[256,128]{1,0:T(8,128)(2,1)S(1)} %get-tuple-element.82), channel_id=1, source_target_pairs={{0,2},{1,3},{2,0},{3,1},{4,6},{5,7},{6,4},{7,5},{8,10},{9,11},{10,... | collective-permute-start | bytes 196616 | tf_op jit(solution)/shard_map/ppermute | solution.py:241
  82.8 6.0 %collective-permute-start.41 = (bf16[256,128]{1,0:T(8,128)(2,1)S(1)}, bf16[256,128]{1,0:T(8,128)(2,1)S(1)}, u32[]{:S(2)}, u32[]{:S(2)}) collective-permute-start(bf16[256,128]{1,0:T(8,128)(2,1)S(1)} %get-tuple-element.83), channel_id=1, source_target_pairs={{0,4},{1,5},{2,6},{3,7},{4,0},{5,1},{6,2},{7,3},{8,12},{9,13},{10,... | collective-permute-start | bytes 196616 | tf_op jit(solution)/shard_map/ppermute | solution.py:241
  84.1 5.4 %collective-permute-start.42 = (bf16[256,128]{1,0:T(8,128)(2,1)S(1)}, bf16[256,128]{1,0:T(8,128)(2,1)S(1)}, u32[]{:S(2)}, u32[]{:S(2)}) collective-permute-start(bf16[256,128]{1,0:T(8,128)(2,1)S(1)} %get-tuple-element.84), channel_id=1, source_target_pairs={{0,6},{1,7},{2,4},{3,5},{4,2},{5,3},{6,0},{7,1},{8,14},{9,15},{10,... | collective-permute-start | bytes 196616 | tf_op jit(solution)/shard_map/ppermute | solution.py:241
  (22 other events, 78.8 us)

commit v3 on v2

--- a/solution.py
+++ b/solution.py
@@ -11,12 +11,8 @@
 epsilon = 1e-05
 LANES = 128
 TOGETHER = 1024
-UNROLL = 4
+UNROLL = 32
 VMEM_BYTES = 24 * 1024 * 1024
-
-
-def sigmoid(x):
-    return 0.5 * jnp.tanh(0.5 * x) + 0.5
 
 
 def normalize(values):
@@ -67,9 +63,9 @@
     normed = (normalize(pair_f) * gain).astype(jnp.bfloat16)
     linear = matmul(proj[...], normed)
     p0, p1, p2, p3, p4 = [linear[e * channels : (e + 1) * channels] for e in range(5)]
-    put_rows(left_scr, row, rows, sigmoid(p1) * p0 * mask)
-    put_rows(right_scr, row, rows, sigmoid(p3) * p2 * mask)
-    return sigmoid(p4)
+    put_rows(left_scr, row, rows, (jnp.tanh(p1) + 1.0) * p0 * mask)
+    put_rows(right_scr, row, rows, (jnp.tanh(p3) + 1.0) * p2 * mask)
+    return 0.5 * jnp.tanh(p4) + 0.5
 
 
 def write_edges(left_scr, right_scr, here, edges):
@@ -111,18 +107,19 @@
     write_edges(left_scr, right_scr, here, edges)
 
 
-def triangle_kernel(half, chunks, here, *refs):
+def triangle_kernel(half, chunks, taken, here, *refs):
     sources = [refs[k * 2 * half : (k + 1) * 2 * half] for k in range(chunks)]
     refs = refs[chunks * 2 * half :]
-    products = [refs[k * half : (k + 1) * half] for k in range(chunks)]
-    lefts, rights, sums = refs[chunks * half :]
+    products = [refs[n * half : (n + 1) * half] for n in range(len(taken))]
+    lefts, rights, sums = refs[len(taken) * half :]
     block, columns = sums.shape[1:]
     places = 2 * half * chunks
     rows = columns // places
     for k in range(chunks):
         for i in range(half):
             chip = lax.rem(here[2] + k, chunks) * half + (here[0] ^ i)
-            lefts[k * half + i] = sources[k][i][0].astype(jnp.float32)
+            if k in taken:
+                lefts[taken.index(k) * half + i] = sources[k][i][0].astype(jnp.float32)
             rights[2 * chip + here[1]] = sources[k][i][1].astype(jnp.float32)
             rights[2 * chip + 1 - here[1]] = sources[k][half + i][1].astype(jnp.float32)
 
@@ -137,14 +134,14 @@
         total = lax.dot_general(
             left, right, (((1,), (1,)), ((), ())), preferred_element_type=jnp.float32
         )
-        for p in range(half * chunks):
+        for p in range(half * len(taken)):
             sums[p, at, :] = total[p * rows : (p + 1) * rows]
         return carry
 
     lax.fori_loop(0, block // rows, step, 0, unroll=min(UNROLL, block // rows))
-    for k in range(chunks):
+    for n in range(len(taken)):
         for i in range(half):
-            products[k][i][...] = sums[k * half + i].astype(jnp.bfloat16)
+            products[n][i][...] = sums[n * half + i].astype(jnp.bfloat16)
 
 
 def load_product(here, own, prod_scr):
@@ -309,7 +306,10 @@
     others = (out_weights[0], up_weights[0], down_weights[0])
     *others, projs[-1] = lax.optimization_barrier((*others, projs[-1]))
     others = [from_sections(w, sections) for w in others]
-    projs = [w.transpose(0, 2, 1).reshape(-1, channels) for w in by_layer(projs, section)]
+    projs = [
+        (0.5 * w).astype(w.dtype).transpose(0, 2, 1).reshape(-1, channels)
+        for w in by_layer(projs, section)
+    ]
     outs, ups, downs = [[w.T for w in by_layer(slots, section)] for slots in others]
     gains = [
         jnp.broadcast_to(g.astype(jnp.float32)[:, :, None], g.shape + (columns,))
@@ -350,15 +350,18 @@
     finished = [None] * parts
     for layer in range(sections):
         edges = [with_neighbour(edges[k]) for k in range(parts)]
-        sides = [(n * parts * half, block, columns) for n in (1, 2, 1)]
-        products = call(
-            functools.partial(triangle_kernel, half, parts),
-            [((block, columns), jnp.bfloat16)] * (half * parts), sides,
-            2 * channels // width * columns**3, here, *sum(edges, []),
-        )
         last = layer == sections - 1
         order = range(parts - 1, -1, -1) if last else range(parts)
-        tri = {k: exchange(products[k * half : (k + 1) * half], width, groups) for k in order}
+        tri = {}
+        for taken in [(k,) for k in order] if last else [tuple(order)]:
+            sides = [(n * half, block, columns) for n in (len(taken), 2 * parts, len(taken))]
+            products = call(
+                functools.partial(triangle_kernel, half, parts, taken),
+                [((block, columns), jnp.bfloat16)] * (half * len(taken)), sides,
+                2 * channels // width * columns**3 * len(taken) // parts, here, *sum(edges, []),
+            )
+            for n, k in enumerate(taken):
+                tri[k] = exchange(products[n * half : (n + 1) * half], width, groups)
         for k in order:
             operands = (*tri[k], *state[k], outs[layer], ups[layer], downs[layer], gains[layer])
             if not last:

time: 94 us -> 95.2 us (1.013)
  waiting for transfers between devices: 29.2 us -> 31.6 us
  Pallas kernels: 16.1 us -> 15.1 us
    ppermute x24, waiting for transfers between devices: 24.4 us -> 28 us  [exchange(): lax.ppermute(blocks[i], 'axial', [(j, j ^ 2 * i) for j in range(size)])]
    ppermute x2, waiting for transfers between devices: 1.05 us -> 0.01 us  [move_parts(): lax.ppermute(values, 'axial', [(j, (j + distance * width) % size) for j i...]
    pallas_call x8 -> x9, Pallas kernels: 16.1 us -> 15.1 us  [pallas(): pl.pallas_call(kernel, out_shape=[jax.ShapeDtypeStruct(shape, dtype) for...]
  transfers between devices with their start and end apart: 47 -> 47, of which waited for: 22 -> 21; matrix products, arithmetic and copies ran while one was open for 4% -> 4% of each run, Pallas kernels for 13% -> 13%
where the time goes in v3:
time: 95.2 us; the launch traced here: 95 us
  starting transfers between devices  42.5 us (45%)
  waiting for transfers between devices  31.6 us (33%)
  Pallas kernels  15.1 us (16%)
  local copies, waits for them, and re-layouts  4.26 us (4%)
  other arithmetic  1.24 us (1%)
    ppermute x24, waiting for transfers between devices, exchange(): lax.ppermute(blocks[i], 'axial', [(j, j ^ 2 * i) for j in range(size)])  28 us
    ppermute x24, starting transfers between devices, exchange(): lax.ppermute(blocks[i], 'axial', [(j, j ^ 2 * i) for j in range(size)])  27.8 us
    pallas_call x9, Pallas kernels, pallas(): pl.pallas_call(kernel, out_shape=[jax.ShapeDtypeStruct(shape, dtype) for...  15.1 us
    ppermute x2, starting transfers between devices, move_parts(): lax.ppermute(values, 'axial', [(j, (j + distance * width) % size) for j i...  6.89 us
    ppermute x5, starting transfers between devices, from_sections(): lax.ppermute(weight, 'section', [((i + shift) % sections, i) for i in ran...  5.61 us
    ppermute x5, waiting for transfers between devices, from_sections(): lax.ppermute(weight, 'section', [((i + shift) % sections, i) for i in ran...  2.32 us
    ppermute x16, starting transfers between devices, with_neighbour(): return own + [lax.ppermute(piece, 'axial', swap) for piece in own]  2.13 us
  transfers between devices with their start and end apart: 47, of which 21 were waited for; matrix products, arithmetic and copies ran while one was open for 4% of the time, Pallas kernels for 13%

profile of v3, /device:TPU:0, one launch (start us, length us, event | category | flops | bytes accessed | tf_op | source)
XLA Modules:
  0.0 95.0 jit_solution(11132101534523764948)
XLA Ops:
  1.1 4.1 %collective-permute-start.9 = (bf16[8,128,128]{2,1,0:T(8,128)(2,1)S(1)}, bf16[8,128,128]{2,1,0:T(8,128)(2,1)S(1)}, u32[]{:S(2)}, u32[]{:S(2)}) collective-permute-start(bf16[8,128,128]{2,1,0:T(8,128)(2,1)S(1)} %get-tuple-element.93), channel_id=1, source_target_pairs={{0,8},{1,9},{2,10},{3,11},{4,12},{5,13},{6,14},{7,15},{8,0},{9,1},... | collective-permute-start | bytes 786440 | tf_op jit(solution)/shard_map/ppermute | solution.py:258
  5.3 1.5 %collective-permute-start = (bf16[5,128,128]{2,1,0:T(8,128)(2,1)S(1)}, bf16[5,128,128]{2,1,0:T(8,128)(2,1)S(1)}, u32[]{:S(2)}, u32[]{:S(2)}) collective-permute-start(bf16[5,128,128]{2,1,0:T(8,128)(2,1)S(1)} %bitcast.46), channel_id=1, source_target_pairs={{16,0},{0,16},{17,1},{1,17},{18,2},{2,18},{19,3},{3,19},{20,4},{4,... | collective-permute-start | bytes 491528 | tf_op jit(solution)/shard_map/ppermute | solution.py:265
  9.4 1.6 %collective-permute-done.1 = bf16[3,128]{1,0:T(4,128)(2,1)S(1)} collective-permute-done((bf16[3,128]{1,0:T(4,128)(2,1)S(1)}, bf16[3,128]{1,0:T(4,128)(2,1)S(1)}, u32[]{:S(2)}, u32[]{:S(2)}) %collective-permute-start.1) | collective-permute-done | bytes 800 | tf_op jit(solution)/shard_map/ppermute | solution.py:265
  11.3 1.3 %shard_map.73 = (bf16[2,256,128]{2,1,0:T(8,128)(2,1)S(1)}, bf16[2,256,128]{2,1,0:T(8,128)(2,1)S(1)}, bf16[2,256,128]{2,1,0:T(8,128)(2,1)S(1)}, bf16[2,256,128]{2...) custom-call(s32[3]{0:T(128)S(1)} %pad_add_fusion.here, ...), custom_call_target="tpu_custom_call" | custom-call | flops 167772160 | tf_op jit(solution)/shard_map/pallas_call | solution.py:217
  12.7 1.6 %collective-permute-start.2 = (bf16[2,256,128]{2,1,0:T(8,128)(2,1)S(1)}, bf16[2,256,128]{2,1,0:T(8,128)(2,1)S(1)}, u32[]{:S(2)}, u32[]{:S(2)}) collective-permute-start(bf16[2,256,128]{2,1,0:T(8,128)(2,1)S(1)} %get-tuple-element.51), channel_id=1, source_target_pairs={{0,2},{1,3},{2,0},{3,1},{4,6},{5,7},{6,4},{7,5},{8,10},{9,11},{10,... | collective-permute-start | bytes 393224 | tf_op jit(solution)/shard_map/ppermute | solution.py:238
  14.2 1.5 %collective-permute-start.20 = (bf16[128,128]{0,1:T(8,128)(2,1)S(1)}, bf16[128,128]{0,1:T(8,128)(2,1)S(1)}, u32[]{:S(2)}, u32[]{:S(2)}) collective-permute-start(bf16[128,128]{0,1:T(8,128)(2,1)S(1)} %bitcast.47), channel_id=1, source_target_pairs={{16,0},{0,16},{17,1},{1,17},{18,2},{2,18},{19,3},{3,19},{20,4},{4,... | collective-permute-start | bytes 98312 | tf_op jit(solution)/shard_map/ppermute | solution.py:265
  15.7 1.6 %collective-permute-start.3 = (bf16[2,256,128]{2,1,0:T(8,128)(2,1)S(1)}, bf16[2,256,128]{2,1,0:T(8,128)(2,1)S(1)}, u32[]{:S(2)}, u32[]{:S(2)}) collective-permute-start(bf16[2,256,128]{2,1,0:T(8,128)(2,1)S(1)} %get-tuple-element.52), channel_id=1, source_target_pairs={{0,4},{1,5},{2,6},{3,7},{4,0},{5,1},{6,2},{7,3},{8,12},{9,13},{10,... | collective-permute-start | bytes 393224 | tf_op jit(solution)/shard_map/ppermute | solution.py:238
  17.7 1.3 %shard_map.74 = (bf16[2,256,128]{2,1,0:T(8,128)(2,1)S(1)}, bf16[2,256,128]{2,1,0:T(8,128)(2,1)S(1)}, bf16[2,256,128]{2,1,0:T(8,128)(2,1)S(1)}, bf16[2,256,128]{2...) custom-call(s32[3]{0:T(128)S(1)} %pad_add_fusion.here, ...), custom_call_target="tpu_custom_call" | custom-call | flops 167772160 | tf_op jit(solution)/shard_map/pallas_call | solution.py:217
  20.2 1.5 %collective-permute-start.10 = (bf16[2,256,128]{2,1,0:T(8,128)(2,1)S(1)}, bf16[2,256,128]{2,1,0:T(8,128)(2,1)S(1)}, u32[]{:S(2)}, u32[]{:S(2)}) collective-permute-start(bf16[2,256,128]{2,1,0:T(8,128)(2,1)S(1)} %get-tuple-element.55), channel_id=1, source_target_pairs={{0,2},{1,3},{2,0},{3,1},{4,6},{5,7},{6,4},{7,5},{8,10},{9,11},{10,... | collective-permute-start | bytes 393224 | tf_op jit(solution)/shard_map/ppermute | solution.py:238
  25.3 1.5 %collective-permute-done.10.refs_9_ = bf16[2,256,128]{2,1,0:T(8,128)(2,1)S(1)} collective-permute-done((bf16[2,256,128]{2,1,0:T(8,128)(2,1)S(1)}, bf16[2,256,128]{2,1,0:T(8,128)(2,1)S(1)}, u32[]{:S(2)}, u32[]{:S(2)}) %collective-permute-start.10) | collective-permute-done | bytes 131104 | tf_op jit(solution)/shard_map/ppermute | solution.py:238
  26.9 1.5 %collective-permute-done.11.refs_10_ = bf16[2,256,128]{2,1,0:T(8,128)(2,1)S(1)} collective-permute-done((bf16[2,256,128]{2,1,0:T(8,128)(2,1)S(1)}, bf16[2,256,128]{2,1,0:T(8,128)(2,1)S(1)}, u32[]{:S(2)}, u32[]{:S(2)}) %collective-permute-start.11) | collective-permute-done | bytes 131104 | tf_op jit(solution)/shard_map/ppermute | solution.py:238
  32.2 1.5 %shard_map.75 = (bf16[256,128]{1,0:T(8,128)(2,1)S(1)}, bf16[256,128]{1,0:T(8,128)(2,1)S(1)}, bf16[256,128]{1,0:T(8,128)(2,1)S(1)}, bf16[256,128]{1,0:T(8,128)(2,...) custom-call(s32[3]{0:T(128)S(1)} %pad_add_fusion.here, ...), custom_call_target="tpu_custom_call" | custom-call | flops 67108864 | tf_op jit(solution)/shard_map/pallas_call | solution.py:217
  33.7 1.6 %collective-permute-start.30 = (bf16[256,128]{1,0:T(8,128)(2,1)S(1)}, bf16[256,128]{1,0:T(8,128)(2,1)S(1)}, u32[]{:S(2)}, u32[]{:S(2)}) collective-permute-start(bf16[256,128]{1,0:T(8,128)(2,1)S(1)} %get-tuple-element.72), channel_id=1, source_target_pairs={{0,2},{1,3},{2,0},{3,1},{4,6},{5,7},{6,4},{7,5},{8,10},{9,11},{10,... | collective-permute-start | bytes 196616 | tf_op jit(solution)/shard_map/ppermute | solution.py:238
  37.2 1.5 %collective-permute-start.17 = (bf16[256,128]{1,0:T(8,128)(2,1)S(1)}, bf16[256,128]{1,0:T(8,128)(2,1)S(1)}, u32[]{:S(2)}, u32[]{:S(2)}) collective-permute-start(bf16[256,128]{1,0:T(8,128)(2,1)S(1)} %get-tuple-element.59), channel_id=1, source_target_pairs={{0,2},{1,3},{2,0},{3,1},{4,6},{5,7},{6,4},{7,5},{8,10},{9,11},{10,... | collective-permute-start | bytes 196616 | tf_op jit(solution)/shard_map/ppermute | solution.py:238
  40.0 2.0 %collective-permute-done.32.refs_3_ = bf16[256,128]{1,0:T(8,128)(2,1)S(1)} collective-permute-done((bf16[256,128]{1,0:T(8,128)(2,1)S(1)}, bf16[256,128]{1,0:T(8,128)(2,1)S(1)}, u32[]{:S(2)}, u32[]{:S(2)}) %collective-permute-start.32) | collective-permute-done | bytes 65568 | tf_op jit(solution)/shard_map/ppermute | solution.py:238
  42.1 2.1 %shard_map.77 = (bf16[2,256,128]{2,1,0:T(8,128)(2,1)S(1)}, bf16[2,256,128]{2,1,0:T(8,128)(2,1)S(1)}, bf16[2,256,128]{2,1,0:T(8,128)(2,1)S(1)}, bf16[2,256,128]{2...) custom-call(s32[3]{0:T(128)S(1)} %pad_add_fusion.here, ...), custom_call_target="tpu_custom_call" | custom-call | flops 469762048 | tf_op jit(solution)/shard_map/pallas_call | solution.py:217
  45.6 2.2 %collective-permute-start.35 = (bf16[2,256,128]{2,1,0:T(8,128)(2,1)S(1)}, bf16[2,256,128]{2,1,0:T(8,128)(2,1)S(1)}, u32[]{:S(2)}, u32[]{:S(2)}) collective-permute-start(bf16[2,256,128]{2,1,0:T(8,128)(2,1)S(1)} %get-tuple-element.80), channel_id=1, source_target_pairs={{0,6},{1,7},{2,4},{3,5},{4,2},{5,3},{6,0},{7,1},{8,14},{9,15},{10,... | collective-permute-start | bytes 393224 | tf_op jit(solution)/shard_map/ppermute | solution.py:238
  48.6 5.0 %collective-permute-done.19.refs_3_ = bf16[256,128]{1,0:T(8,128)(2,1)S(1)} collective-permute-done((bf16[256,128]{1,0:T(8,128)(2,1)S(1)}, bf16[256,128]{1,0:T(8,128)(2,1)S(1)}, u32[]{:S(2)}, u32[]{:S(2)}) %collective-permute-start.19) | collective-permute-done | bytes 65568 | tf_op jit(solution)/shard_map/ppermute | solution.py:238
  53.5 2.1 %shard_map.76 = (bf16[2,256,128]{2,1,0:T(8,128)(2,1)S(1)}, bf16[2,256,128]{2,1,0:T(8,128)(2,1)S(1)}, bf16[2,256,128]{2,1,0:T(8,128)(2,1)S(1)}, bf16[2,256,128]{2...) custom-call(s32[3]{0:T(128)S(1)} %pad_add_fusion.here, ...), custom_call_target="tpu_custom_call" | custom-call | flops 469762048 | tf_op jit(solution)/shard_map/pallas_call | solution.py:217
  57.8 1.4 %collective-permute-start.25 = (bf16[2,256,128]{2,1,0:T(8,128)(2,1)S(1)}, bf16[2,256,128]{2,1,0:T(8,128)(2,1)S(1)}, u32[]{:S(2)}, u32[]{:S(2)}) collective-permute-start(bf16[2,256,128]{2,1,0:T(8,128)(2,1)S(1)} %get-tuple-element.70), channel_id=1, source_target_pairs={{0,6},{1,7},{2,4},{3,5},{4,2},{5,3},{6,0},{7,1},{8,14},{9,15},{10,... | collective-permute-start | bytes 393224 | tf_op jit(solution)/shard_map/ppermute | solution.py:238
  59.7 1.4 %collective-permute-done.23.refs_1_ = bf16[2,256,128]{2,1,0:T(8,128)(2,1)S(1)} collective-permute-done((bf16[2,256,128]{2,1,0:T(8,128)(2,1)S(1)}, bf16[2,256,128]{2,1,0:T(8,128)(2,1)S(1)}, u32[]{:S(2)}, u32[]{:S(2)}) %collective-permute-start.23) | collective-permute-done | bytes 131104 | tf_op jit(solution)/shard_map/ppermute | solution.py:238
  61.2 1.6 %collective-permute-done.24.refs_2_ = bf16[2,256,128]{2,1,0:T(8,128)(2,1)S(1)} collective-permute-done((bf16[2,256,128]{2,1,0:T(8,128)(2,1)S(1)}, bf16[2,256,128]{2,1,0:T(8,128)(2,1)S(1)}, u32[]{:S(2)}, u32[]{:S(2)}) %collective-permute-start.24) | collective-permute-done | bytes 131104 | tf_op jit(solution)/shard_map/ppermute | solution.py:238
  62.8 2.1 %collective-permute-done.25.refs_3_ = bf16[2,256,128]{2,1,0:T(8,128)(2,1)S(1)} collective-permute-done((bf16[2,256,128]{2,1,0:T(8,128)(2,1)S(1)}, bf16[2,256,128]{2,1,0:T(8,128)(2,1)S(1)}, u32[]{:S(2)}, u32[]{:S(2)}) %collective-permute-start.25) | collective-permute-done | bytes 131104 | tf_op jit(solution)/shard_map/ppermute | solution.py:238
  66.8 1.3 %shard_map.80 = (bf16[256,128]{1,0:T(8,128)(2,1)S(1)}, bf16[256,128]{1,0:T(8,128)(2,1)S(1)}, bf16[256,128]{1,0:T(8,128)(2,1)S(1)}, bf16[256,128]{1,0:T(8,128)(2,1)S(1)}) custom-call(s32[3]{0:T(128)S(1)} %pad_add_fusion.here, bf16[2,256,128]{2,1,0:T(8,128)(2,1)S(1)} %get-tuple-element.67.refs_0_, bf16[2,256,128]{2,1,0:T(8,128)(2,1)S(1)} %collective-permute-done.23.refs_1_, ...), custom_call_target="tpu_custom_call" | custom-call | flops 33554432 | tf_op jit(solution)/shard_map/pallas_call | solution.py:217
  69.9 1.7 %collective-permute-start.45 = (bf16[256,128]{1,0:T(8,128)(2,1)S(1)}, bf16[256,128]{1,0:T(8,128)(2,1)S(1)}, u32[]{:S(2)}, u32[]{:S(2)}) collective-permute-start(bf16[256,128]{1,0:T(8,128)(2,1)S(1)} %get-tuple-element.90), channel_id=1, source_target_pairs={{0,6},{1,7},{2,4},{3,5},{4,2},{5,3},{6,0},{7,1},{8,14},{9,15},{10,... | collective-permute-start | bytes 196616 | tf_op jit(solution)/shard_map/ppermute | solution.py:238
  73.5 1.6 %collective-permute-done.45.refs_3_ = bf16[256,128]{1,0:T(8,128)(2,1)S(1)} collective-permute-done((bf16[256,128]{1,0:T(8,128)(2,1)S(1)}, bf16[256,128]{1,0:T(8,128)(2,1)S(1)}, u32[]{:S(2)}, u32[]{:S(2)}) %collective-permute-start.45) | collective-permute-done | bytes 65568 | tf_op jit(solution)/shard_map/ppermute | solution.py:238
  75.2 1.6 %shard_map.81 = bf16[1,8,128,128]{3,2,1,0:T(8,128)(2,1)S(1)} custom-call(s32[3]{0:T(128)S(1)} %pad_add_fusion.here, bf16[256,128]{1,0:T(8,128)(2,1)S(1)} %get-tuple-element.87.refs_0_, bf16[256,128]{1,0:T(8,128)(2,1)S(1)} %collective-permute-done.43.refs_1_, bf16[256,128]{1,0:T(8,128)(2,1)S(1)} %collective-permute-done.44.refs_2_, ...), custom_call_target="tpu_custom_call" | custom-call | flops 301989888 | tf_op jit(solution)/shard_map/pallas_call | solution.py:217
  76.8 2.7 %collective-permute-start.46 = (bf16[1,8,128,128]{3,2,1,0:T(8,128)(2,1)S(1)}, bf16[1,8,128,128]{3,2,1,0:T(8,128)(2,1)S(1)}, u32[]{:S(2)}, u32[]{:S(2)}) collective-permute-start(bf16[1,8,128,128]{3,2,1,0:T(8,128)(2,1)S(1)} %shard_map.81), channel_id=1, source_target_pairs={{0,8},{1,9},{2,10},{3,11},{4,12},{5,13},{6,14},{7,15},{8,0},{9,1},... | collective-permute-start | bytes 786440 | tf_op jit(solution)/shard_map/ppermute | solution.py:258
  79.5 1.3 %shard_map.78 = (bf16[256,128]{1,0:T(8,128)(2,1)S(1)}, bf16[256,128]{1,0:T(8,128)(2,1)S(1)}, bf16[256,128]{1,0:T(8,128)(2,1)S(1)}, bf16[256,128]{1,0:T(8,128)(2,1)S(1)}) custom-call(s32[3]{0:T(128)S(1)} %pad_add_fusion.here, bf16[2,256,128]{2,1,0:T(8,128)(2,1)S(1)} %get-tuple-element.67.refs_0_, bf16[2,256,128]{2,1,0:T(8,128)(2,1)S(1)} %collective-permute-done.23.refs_1_, ...), custom_call_target="tpu_custom_call" | custom-call | flops 33554432 | tf_op jit(solution)/shard_map/pallas_call | solution.py:217
  84.4 1.4 %collective-permute-done.40.refs_1_ = bf16[256,128]{1,0:T(8,128)(2,1)S(1)} collective-permute-done((bf16[256,128]{1,0:T(8,128)(2,1)S(1)}, bf16[256,128]{1,0:T(8,128)(2,1)S(1)}, u32[]{:S(2)}, u32[]{:S(2)}) %collective-permute-start.40) | collective-permute-done | bytes 65568 | tf_op jit(solution)/shard_map/ppermute | solution.py:238
  86.7 5.1 %collective-permute-done.42.refs_3_ = bf16[256,128]{1,0:T(8,128)(2,1)S(1)} collective-permute-done((bf16[256,128]{1,0:T(8,128)(2,1)S(1)}, bf16[256,128]{1,0:T(8,128)(2,1)S(1)}, u32[]{:S(2)}, u32[]{:S(2)}) %collective-permute-start.42) | collective-permute-done | bytes 65568 | tf_op jit(solution)/shard_map/ppermute | solution.py:238
  91.8 2.4 %shard_map.79 = bf16[2,8,128,128]{3,2,1,0:T(8,128)(2,1)} custom-call(s32[3]{0:T(128)S(1)} %pad_add_fusion.here, bf16[256,128]{1,0:T(8,128)(2,1)S(1)} %get-tuple-element.81.refs_0_, bf16[256,128]{1,0:T(8,128)(2,1)S(1)} %collective-permute-done.40.refs_1_, bf16[256,128]{1,0:T(8,128)(2,1)S(1)} %collective-permute-done.41.refs_2_, ...), custom_call_target="tpu_custom_call" | custom-call | flops 301989888 | tf_op jit(solution)/shard_map/pallas_call | solution.py:217
  (104 shorter events, 31.8 us)
Async XLA Ops:
  1.1 16.6 %collective-permute-start.9 = (bf16[8,128,128]{2,1,0:T(8,128)(2,1)S(1)}, bf16[8,128,128]{2,1,0:T(8,128)(2,1)S(1)}, u32[]{:S(2)}, u32[]{:S(2)}) collective-permute-start(bf16[8,128,128]{2,1,0:T(8,128)(2,1)S(1)} %get-tuple-element.93), channel_id=1, source_target_pairs={{0,8},{1,9},{2,10},{3,11},{4,12},{5,13},{6,14},{7,15},{8,0},{9,1},... | collective-permute-start | bytes 786440 | tf_op jit(solution)/shard_map/ppermute | solution.py:258
  5.3 5.7 %collective-permute-start = (bf16[5,128,128]{2,1,0:T(8,128)(2,1)S(1)}, bf16[5,128,128]{2,1,0:T(8,128)(2,1)S(1)}, u32[]{:S(2)}, u32[]{:S(2)}) collective-permute-start(bf16[5,128,128]{2,1,0:T(8,128)(2,1)S(1)} %bitcast.46), channel_id=1, source_target_pairs={{16,0},{0,16},{17,1},{1,17},{18,2},{2,18},{19,3},{3,19},{20,4},{4,... | collective-permute-start | bytes 491528 | tf_op jit(solution)/shard_map/ppermute | solution.py:265
  12.7 7.6 %collective-permute-start.2 = (bf16[2,256,128]{2,1,0:T(8,128)(2,1)S(1)}, bf16[2,256,128]{2,1,0:T(8,128)(2,1)S(1)}, u32[]{:S(2)}, u32[]{:S(2)}) collective-permute-start(bf16[2,256,128]{2,1,0:T(8,128)(2,1)S(1)} %get-tuple-element.51), channel_id=1, source_target_pairs={{0,2},{1,3},{2,0},{3,1},{4,6},{5,7},{6,4},{7,5},{8,10},{9,11},{10,... | collective-permute-start | bytes 393224 | tf_op jit(solution)/shard_map/ppermute | solution.py:238
  15.7 6.2 %collective-permute-start.3 = (bf16[2,256,128]{2,1,0:T(8,128)(2,1)S(1)}, bf16[2,256,128]{2,1,0:T(8,128)(2,1)S(1)}, u32[]{:S(2)}, u32[]{:S(2)}) collective-permute-start(bf16[2,256,128]{2,1,0:T(8,128)(2,1)S(1)} %get-tuple-element.52), channel_id=1, source_target_pairs={{0,4},{1,5},{2,6},{3,7},{4,0},{5,1},{6,2},{7,3},{8,12},{9,13},{10,... | collective-permute-start | bytes 393224 | tf_op jit(solution)/shard_map/ppermute | solution.py:238
  17.3 6.6 %collective-permute-start.4 = (bf16[2,256,128]{2,1,0:T(8,128)(2,1)S(1)}, bf16[2,256,128]{2,1,0:T(8,128)(2,1)S(1)}, u32[]{:S(2)}, u32[]{:S(2)}) collective-permute-start(bf16[2,256,128]{2,1,0:T(8,128)(2,1)S(1)} %get-tuple-element.53), channel_id=1, source_target_pairs={{0,6},{1,7},{2,4},{3,5},{4,2},{5,3},{6,0},{7,1},{8,14},{9,15},{10,... | collective-permute-start | bytes 393224 | tf_op jit(solution)/shard_map/ppermute | solution.py:238
  17.7 6.9 %collective-permute-start.5 = (bf16[2,256,128]{2,1,0:T(8,128)(2,1)S(1)}, bf16[2,256,128]{2,1,0:T(8,128)(2,1)S(1)}, u32[]{:S(2)}, u32[]{:S(2)}) collective-permute-start(bf16[2,256,128]{2,1,0:T(8,128)(2,1)S(1)} %get-tuple-element.50.refs_0_), channel_id=1, source_target_pairs={{0,1},{1,0},{2,3},{3,2},{4,5},{5,4},{6,7},{7,6},{8,9},{9,8},{10,11... | collective-permute-start | bytes 393224 | tf_op jit(solution)/shard_map/ppermute | solution.py:247
  19.0 6.3 %collective-permute-start.21 = (bf16[128,512]{0,1:T(8,128)(2,1)}, bf16[128,512]{0,1:T(8,128)(2,1)}, u32[]{:S(2)}, u32[]{:S(2)}) collective-permute-start(bf16[128,512]{0,1:T(8,128)(2,1)} %bitcast.7), channel_id=1, source_target_pairs={{16,0},{0,16},{17,1},{1,17},{18,2},{2,18},{19,3},{3,19},{20,4},{4,... | collective-permute-start | bytes 393224 | tf_op jit(solution)/shard_map/ppermute | solution.py:265
  20.2 6.6 %collective-permute-start.10 = (bf16[2,256,128]{2,1,0:T(8,128)(2,1)S(1)}, bf16[2,256,128]{2,1,0:T(8,128)(2,1)S(1)}, u32[]{:S(2)}, u32[]{:S(2)}) collective-permute-start(bf16[2,256,128]{2,1,0:T(8,128)(2,1)S(1)} %get-tuple-element.55), channel_id=1, source_target_pairs={{0,2},{1,3},{2,0},{3,1},{4,6},{5,7},{6,4},{7,5},{8,10},{9,11},{10,... | collective-permute-start | bytes 393224 | tf_op jit(solution)/shard_map/ppermute | solution.py:238
  21.9 6.4 %collective-permute-start.11 = (bf16[2,256,128]{2,1,0:T(8,128)(2,1)S(1)}, bf16[2,256,128]{2,1,0:T(8,128)(2,1)S(1)}, u32[]{:S(2)}, u32[]{:S(2)}) collective-permute-start(bf16[2,256,128]{2,1,0:T(8,128)(2,1)S(1)} %get-tuple-element.56), channel_id=1, source_target_pairs={{0,4},{1,5},{2,6},{3,7},{4,0},{5,1},{6,2},{7,3},{8,12},{9,13},{10,... | collective-permute-start | bytes 393224 | tf_op jit(solution)/shard_map/ppermute | solution.py:238
  23.9 6.2 %collective-permute-start.12 = (bf16[2,256,128]{2,1,0:T(8,128)(2,1)S(1)}, bf16[2,256,128]{2,1,0:T(8,128)(2,1)S(1)}, u32[]{:S(2)}, u32[]{:S(2)}) collective-permute-start(bf16[2,256,128]{2,1,0:T(8,128)(2,1)S(1)} %get-tuple-element.57), channel_id=1, source_target_pairs={{0,6},{1,7},{2,4},{3,5},{4,2},{5,3},{6,0},{7,1},{8,14},{9,15},{10,... | collective-permute-start | bytes 393224 | tf_op jit(solution)/shard_map/ppermute | solution.py:238
  24.6 5.5 %collective-permute-start.13 = (bf16[2,256,128]{2,1,0:T(8,128)(2,1)S(1)}, bf16[2,256,128]{2,1,0:T(8,128)(2,1)S(1)}, u32[]{:S(2)}, u32[]{:S(2)}) collective-permute-start(bf16[2,256,128]{2,1,0:T(8,128)(2,1)S(1)} %get-tuple-element.54.refs_8_), channel_id=1, source_target_pairs={{0,1},{1,0},{2,3},{3,2},{4,5},{5,4},{6,7},{7,6},{8,9},{9,8},{10,11... | collective-permute-start | bytes 393224 | tf_op jit(solution)/shard_map/ppermute | solution.py:247
  25.3 5.3 %collective-permute-start.6 = (bf16[2,256,128]{2,1,0:T(8,128)(2,1)S(1)}, bf16[2,256,128]{2,1,0:T(8,128)(2,1)S(1)}, u32[]{:S(2)}, u32[]{:S(2)}) collective-permute-start(bf16[2,256,128]{2,1,0:T(8,128)(2,1)S(1)} %collective-permute-done.2.refs_1_), channel_id=1, source_target_pairs={{0,1},{1,0},{2,3},{3,2},{4,5},{5,4},{6,7},{7,6},{8,9},{9,8},{10,11... | collective-permute-start | bytes 393224 | tf_op jit(solution)/shard_map/ppermute | solution.py:247
  28.4 10.4 %collective-permute-start.22 = (bf16[512,128]{0,1:T(8,128)(2,1)S(1)}, bf16[512,128]{0,1:T(8,128)(2,1)S(1)}, u32[]{:S(2)}, u32[]{:S(2)}) collective-permute-start(bf16[512,128]{0,1:T(8,128)(2,1)S(1)} %bitcast.44), channel_id=1, source_target_pairs={{16,0},{0,16},{17,1},{1,17},{18,2},{2,18},{19,3},{3,19},{20,4},{4,... | collective-permute-start | bytes 393224 | tf_op jit(solution)/shard_map/ppermute | solution.py:265
  33.7 6.1 %collective-permute-start.30 = (bf16[256,128]{1,0:T(8,128)(2,1)S(1)}, bf16[256,128]{1,0:T(8,128)(2,1)S(1)}, u32[]{:S(2)}, u32[]{:S(2)}) collective-permute-start(bf16[256,128]{1,0:T(8,128)(2,1)S(1)} %get-tuple-element.72), channel_id=1, source_target_pairs={{0,2},{1,3},{2,0},{3,1},{4,6},{5,7},{6,4},{7,5},{8,10},{9,11},{10,... | collective-permute-start | bytes 196616 | tf_op jit(solution)/shard_map/ppermute | solution.py:238
  36.2 5.7 %collective-permute-start.32 = (bf16[256,128]{1,0:T(8,128)(2,1)S(1)}, bf16[256,128]{1,0:T(8,128)(2,1)S(1)}, u32[]{:S(2)}, u32[]{:S(2)}) collective-permute-start(bf16[256,128]{1,0:T(8,128)(2,1)S(1)} %get-tuple-element.74), channel_id=1, source_target_pairs={{0,6},{1,7},{2,4},{3,5},{4,2},{5,3},{6,0},{7,1},{8,14},{9,15},{10,... | collective-permute-start | bytes 196616 | tf_op jit(solution)/shard_map/ppermute | solution.py:238
  37.2 10.6 %collective-permute-start.17 = (bf16[256,128]{1,0:T(8,128)(2,1)S(1)}, bf16[256,128]{1,0:T(8,128)(2,1)S(1)}, u32[]{:S(2)}, u32[]{:S(2)}) collective-permute-start(bf16[256,128]{1,0:T(8,128)(2,1)S(1)} %get-tuple-element.59), channel_id=1, source_target_pairs={{0,2},{1,3},{2,0},{3,1},{4,6},{5,7},{6,4},{7,5},{8,10},{9,11},{10,... | collective-permute-start | bytes 196616 | tf_op jit(solution)/shard_map/ppermute | solution.py:238
  38.8 9.0 %collective-permute-start.18 = (bf16[256,128]{1,0:T(8,128)(2,1)S(1)}, bf16[256,128]{1,0:T(8,128)(2,1)S(1)}, u32[]{:S(2)}, u32[]{:S(2)}) collective-permute-start(bf16[256,128]{1,0:T(8,128)(2,1)S(1)} %get-tuple-element.60), channel_id=1, source_target_pairs={{0,4},{1,5},{2,6},{3,7},{4,0},{5,1},{6,2},{7,3},{8,12},{9,13},{10,... | collective-permute-start | bytes 196616 | tf_op jit(solution)/shard_map/ppermute | solution.py:238
  44.2 12.5 %collective-permute-start.33 = (bf16[2,256,128]{2,1,0:T(8,128)(2,1)S(1)}, bf16[2,256,128]{2,1,0:T(8,128)(2,1)S(1)}, u32[]{:S(2)}, u32[]{:S(2)}) collective-permute-start(bf16[2,256,128]{2,1,0:T(8,128)(2,1)S(1)} %get-tuple-element.78), channel_id=1, source_target_pairs={{0,2},{1,3},{2,0},{3,1},{4,6},{5,7},{6,4},{7,5},{8,10},{9,11},{10,... | collective-permute-start | bytes 393224 | tf_op jit(solution)/shard_map/ppermute | solution.py:238
  44.6 13.3 %collective-permute-start.34 = (bf16[2,256,128]{2,1,0:T(8,128)(2,1)S(1)}, bf16[2,256,128]{2,1,0:T(8,128)(2,1)S(1)}, u32[]{:S(2)}, u32[]{:S(2)}) collective-permute-start(bf16[2,256,128]{2,1,0:T(8,128)(2,1)S(1)} %get-tuple-element.79), channel_id=1, source_target_pairs={{0,4},{1,5},{2,6},{3,7},{4,0},{5,1},{6,2},{7,3},{8,12},{9,13},{10,... | collective-permute-start | bytes 393224 | tf_op jit(solution)/shard_map/ppermute | solution.py:238
  45.6 13.7 %collective-permute-start.35 = (bf16[2,256,128]{2,1,0:T(8,128)(2,1)S(1)}, bf16[2,256,128]{2,1,0:T(8,128)(2,1)S(1)}, u32[]{:S(2)}, u32[]{:S(2)}) collective-permute-start(bf16[2,256,128]{2,1,0:T(8,128)(2,1)S(1)} %get-tuple-element.80), channel_id=1, source_target_pairs={{0,6},{1,7},{2,4},{3,5},{4,2},{5,3},{6,0},{7,1},{8,14},{9,15},{10,... | collective-permute-start | bytes 393224 | tf_op jit(solution)/shard_map/ppermute | solution.py:238
  47.8 11.5 %collective-permute-start.36 = (bf16[2,256,128]{2,1,0:T(8,128)(2,1)S(1)}, bf16[2,256,128]{2,1,0:T(8,128)(2,1)S(1)}, u32[]{:S(2)}, u32[]{:S(2)}) collective-permute-start(bf16[2,256,128]{2,1,0:T(8,128)(2,1)S(1)} %get-tuple-element.77.refs_8_), channel_id=1, source_target_pairs={{0,1},{1,0},{2,3},{3,2},{4,5},{5,4},{6,7},{7,6},{8,9},{9,8},{10,11... | collective-permute-start | bytes 393224 | tf_op jit(solution)/shard_map/ppermute | solution.py:247
  47.8 5.7 %collective-permute-start.19 = (bf16[256,128]{1,0:T(8,128)(2,1)S(1)}, bf16[256,128]{1,0:T(8,128)(2,1)S(1)}, u32[]{:S(2)}, u32[]{:S(2)}) collective-permute-start(bf16[256,128]{1,0:T(8,128)(2,1)S(1)} %get-tuple-element.61), channel_id=1, source_target_pairs={{0,6},{1,7},{2,4},{3,5},{4,2},{5,3},{6,0},{7,1},{8,14},{9,15},{10,... | collective-permute-start | bytes 196616 | tf_op jit(solution)/shard_map/ppermute | solution.py:238
  55.7 5.5 %collective-permute-start.23 = (bf16[2,256,128]{2,1,0:T(8,128)(2,1)S(1)}, bf16[2,256,128]{2,1,0:T(8,128)(2,1)S(1)}, u32[]{:S(2)}, u32[]{:S(2)}) collective-permute-start(bf16[2,256,128]{2,1,0:T(8,128)(2,1)S(1)} %get-tuple-element.68), channel_id=1, source_target_pairs={{0,2},{1,3},{2,0},{3,1},{4,6},{5,7},{6,4},{7,5},{8,10},{9,11},{10,... | collective-permute-start | bytes 393224 | tf_op jit(solution)/shard_map/ppermute | solution.py:238
  56.8 6.0 %collective-permute-start.24 = (bf16[2,256,128]{2,1,0:T(8,128)(2,1)S(1)}, bf16[2,256,128]{2,1,0:T(8,128)(2,1)S(1)}, u32[]{:S(2)}, u32[]{:S(2)}) collective-permute-start(bf16[2,256,128]{2,1,0:T(8,128)(2,1)S(1)} %get-tuple-element.69), channel_id=1, source_target_pairs={{0,4},{1,5},{2,6},{3,7},{4,0},{5,1},{6,2},{7,3},{8,12},{9,13},{10,... | collective-permute-start | bytes 393224 | tf_op jit(solution)/shard_map/ppermute | solution.py:238
  57.8 7.1 %collective-permute-start.25 = (bf16[2,256,128]{2,1,0:T(8,128)(2,1)S(1)}, bf16[2,256,128]{2,1,0:T(8,128)(2,1)S(1)}, u32[]{:S(2)}, u32[]{:S(2)}) collective-permute-start(bf16[2,256,128]{2,1,0:T(8,128)(2,1)S(1)} %get-tuple-element.70), channel_id=1, source_target_pairs={{0,6},{1,7},{2,4},{3,5},{4,2},{5,3},{6,0},{7,1},{8,14},{9,15},{10,... | collective-permute-start | bytes 393224 | tf_op jit(solution)/shard_map/ppermute | solution.py:238
  59.2 5.7 %collective-permute-start.26 = (bf16[2,256,128]{2,1,0:T(8,128)(2,1)S(1)}, bf16[2,256,128]{2,1,0:T(8,128)(2,1)S(1)}, u32[]{:S(2)}, u32[]{:S(2)}) collective-permute-start(bf16[2,256,128]{2,1,0:T(8,128)(2,1)S(1)} %get-tuple-element.67.refs_0_), channel_id=1, source_target_pairs={{0,1},{1,0},{2,3},{3,2},{4,5},{5,4},{6,7},{7,6},{8,9},{9,8},{10,11... | collective-permute-start | bytes 393224 | tf_op jit(solution)/shard_map/ppermute | solution.py:247
  59.2 6.2 %collective-permute-start.37 = (bf16[2,256,128]{2,1,0:T(8,128)(2,1)S(1)}, bf16[2,256,128]{2,1,0:T(8,128)(2,1)S(1)}, u32[]{:S(2)}, u32[]{:S(2)}) collective-permute-start(bf16[2,256,128]{2,1,0:T(8,128)(2,1)S(1)} %collective-permute-done.33.refs_9_), channel_id=1, source_target_pairs={{0,1},{1,0},{2,3},{3,2},{4,5},{5,4},{6,7},{7,6},{8,9},{9,8},{10,11... | collective-permute-start | bytes 393224 | tf_op jit(solution)/shard_map/ppermute | solution.py:247
  69.9 5.2 %collective-permute-start.45 = (bf16[256,128]{1,0:T(8,128)(2,1)S(1)}, bf16[256,128]{1,0:T(8,128)(2,1)S(1)}, u32[]{:S(2)}, u32[]{:S(2)}) collective-permute-start(bf16[256,128]{1,0:T(8,128)(2,1)S(1)} %get-tuple-element.90), channel_id=1, source_target_pairs={{0,6},{1,7},{2,4},{3,5},{4,2},{5,3},{6,0},{7,1},{8,14},{9,15},{10,... | collective-permute-start | bytes 196616 | tf_op jit(solution)/shard_map/ppermute | solution.py:238
  76.8 17.4 %collective-permute-start.46 = (bf16[1,8,128,128]{3,2,1,0:T(8,128)(2,1)S(1)}, bf16[1,8,128,128]{3,2,1,0:T(8,128)(2,1)S(1)}, u32[]{:S(2)}, u32[]{:S(2)}) collective-permute-start(bf16[1,8,128,128]{3,2,1,0:T(8,128)(2,1)S(1)} %shard_map.81), channel_id=1, source_target_pairs={{0,8},{1,9},{2,10},{3,11},{4,12},{5,13},{6,14},{7,15},{8,0},{9,1},... | collective-permute-start | bytes 786440 | tf_op jit(solution)/shard_map/ppermute | solution.py:258
  80.9 4.9 %collective-permute-start.40 = (bf16[256,128]{1,0:T(8,128)(2,1)S(1)}, bf16[256,128]{1,0:T(8,128)(2,1)S(1)}, u32[]{:S(2)}, u32[]{:S(2)}) collective-permute-start(bf16[256,128]{1,0:T(8,128)(2,1)S(1)} %get-tuple-element.82), channel_id=1, source_target_pairs={{0,2},{1,3},{2,0},{3,1},{4,6},{5,7},{6,4},{7,5},{8,10},{9,11},{10,... | collective-permute-start | bytes 196616 | tf_op jit(solution)/shard_map/ppermute | solution.py:238
  81.9 4.8 %collective-permute-start.41 = (bf16[256,128]{1,0:T(8,128)(2,1)S(1)}, bf16[256,128]{1,0:T(8,128)(2,1)S(1)}, u32[]{:S(2)}, u32[]{:S(2)}) collective-permute-start(bf16[256,128]{1,0:T(8,128)(2,1)S(1)} %get-tuple-element.83), channel_id=1, source_target_pairs={{0,4},{1,5},{2,6},{3,7},{4,0},{5,1},{6,2},{7,3},{8,12},{9,13},{10,... | collective-permute-start | bytes 196616 | tf_op jit(solution)/shard_map/ppermute | solution.py:238
  83.1 8.7 %collective-permute-start.42 = (bf16[256,128]{1,0:T(8,128)(2,1)S(1)}, bf16[256,128]{1,0:T(8,128)(2,1)S(1)}, u32[]{:S(2)}, u32[]{:S(2)}) collective-permute-start(bf16[256,128]{1,0:T(8,128)(2,1)S(1)} %get-tuple-element.84), channel_id=1, source_target_pairs={{0,6},{1,7},{2,4},{3,5},{4,2},{5,3},{6,0},{7,1},{8,14},{9,15},{10,... | collective-permute-start | bytes 196616 | tf_op jit(solution)/shard_map/ppermute | solution.py:238
  (22 other events, 78.7 us)

commit v4 on v3

--- a/solution.py
+++ b/solution.py
@@ -301,20 +301,23 @@
             pair_in, section * own_count + (part + parts - k) % parts, 0, keepdims=False
         )
         pairs.append(move_parts(crop, -k, width))
-    projs = from_sections(proj_weights[0], sections)
-    gains = from_sections(norm_gains[0], sections)
-    others = (out_weights[0], up_weights[0], down_weights[0])
-    *others, projs[-1] = lax.optimization_barrier((*others, projs[-1]))
-    others = [from_sections(w, sections) for w in others]
-    projs = [
-        (0.5 * w).astype(w.dtype).transpose(0, 2, 1).reshape(-1, channels)
-        for w in by_layer(projs, section)
-    ]
-    outs, ups, downs = [[w.T for w in by_layer(slots, section)] for slots in others]
-    gains = [
-        jnp.broadcast_to(g.astype(jnp.float32)[:, :, None], g.shape + (columns,))
-        for g in by_layer(gains, section)
-    ]
+    heads = from_sections(
+        jnp.concatenate((proj_weights[0].reshape(-1, channels), norm_gains[0])), sections
+    )
+    others = from_sections(
+        jnp.concatenate((out_weights[0].T, up_weights[0].T, down_weights[0])), sections
+    )
+    kinds = proj_weights.shape[1]
+
+    def head_of(slots, layer):
+        head = by_layer(slots, section)[layer]
+        proj = (0.5 * head[: kinds * channels]).astype(head.dtype)
+        proj = proj.reshape(kinds, channels, channels).transpose(0, 2, 1).reshape(-1, channels)
+        gain = head[kinds * channels :].astype(jnp.float32)[:, :, None]
+        return proj, jnp.broadcast_to(gain, (norm_gains.shape[1], channels, columns))
+
+    proj, gain = head_of(heads, 0)
+    projs, gains = [proj], [gain]
 
     mask_all = lax.dynamic_index_in_dim(
         crop_mask, section * own_count + part, 0, keepdims=False
@@ -335,7 +338,7 @@
     state_out = [
         ((rows, channels, columns), jnp.bfloat16), ((rows, channels, columns), jnp.bfloat16)
     ]
-    hidden = ups[0].shape[0]
+    hidden = up_weights.shape[2]
     points = rows * columns
     head_flops = 2 * points * 5 * channels * channels
     tail_flops = 2 * points * channels * (channels + 2 * hidden)
@@ -343,10 +346,19 @@
     for k in range(parts):
         *sent, pair, gate = call(
             functools.partial(first_kernel, half), edges_out + state_out, [scratch] * 2,
-            head_flops, here, pairs[k], masks[k], projs[0], gains[0],
+            head_flops, here, pairs[k], masks[k], proj, gain,
         )
         edges[k] = exchange(sent, width, groups)
         state[k] = (pair, gate)
+    heads, others, state[-1] = lax.optimization_barrier((heads, others, state[-1]))
+    for layer in range(1, sections):
+        proj, gain = head_of(heads, layer)
+        projs.append(proj)
+        gains.append(gain)
+    bodies = by_layer(others, section)
+    outs = [w[:channels] for w in bodies]
+    ups = [w[channels : channels + hidden] for w in bodies]
+    downs = [w[channels + hidden :].T for w in bodies]
     finished = [None] * parts
     for layer in range(sections):
         edges = [with_neighbour(edges[k]) for k in range(parts)]

time: 95.2 us -> 103 us (1.082)
  local copies, waits for them, and re-layouts: 4.26 us -> 10.1 us
  starting transfers between devices: 42.5 us -> 39.9 us
  Pallas kernels: 15.1 us -> 16.8 us
  waiting for transfers between devices: 31.6 us -> 33.2 us
    ppermute x2, waiting for transfers between devices: 0.01 us -> 4.73 us  [move_parts(): lax.ppermute(values, 'axial', [(j, (j + distance * width) % size) for j i...]
    unnamed x17 -> x23, local copies, waits for them, and re-layouts: 1.8 us -> 4.6 us
    ppermute x5 -> x2, waiting for transfers between devices: 2.32 us -> 0.01 us  [from_sections(): lax.ppermute(weight, 'section', [((i + shift) % sections, i) for i in ran...]
    ppermute x24, waiting for transfers between devices: 28 us -> 25.9 us  [exchange(): lax.ppermute(blocks[i], 'axial', [(j, j ^ 2 * i) for j in range(size)])]
    ppermute x5 -> x2, starting transfers between devices: 5.61 us -> 3.63 us  [from_sections(): lax.ppermute(weight, 'section', [((i + shift) % sections, i) for i in ran...]
    pallas_call x9, Pallas kernels: 15.1 us -> 16.8 us  [pallas(): pl.pallas_call(kernel, out_shape=[jax.ShapeDtypeStruct(shape, dtype) for...]
    slice x0 -> x6, local copies, waits for them, and re-layouts: none -> 1.39 us  [the longest x2 1.16 us: per_device(): ups = [w[channels:channels + hidden] for w in bodies]]
    ppermute x16, waiting for transfers between devices: 1.31 us -> 2.53 us  [with_neighbour(): return own + [lax.ppermute(piece, 'axial', swap) for piece in own]]
  transfers between devices with their start and end apart: 47 -> 44, of which waited for: 21 -> 20; matrix products, arithmetic and copies ran while one was open for 4% -> 5% of each run, Pallas kernels for 13% -> 10%
where the time goes in v4:
time: 103 us; the launch traced here: 102 us
  starting transfers between devices  39.9 us (39%)
  waiting for transfers between devices  33.2 us (32%)
  Pallas kernels  16.8 us (16%)
  local copies, waits for them, and re-layouts  10.1 us (10%)
  other arithmetic  2.04 us (2%)
    ppermute x24, starting transfers between devices, exchange(): lax.ppermute(blocks[i], 'axial', [(j, j ^ 2 * i) for j in range(size)])  28.3 us
    ppermute x24, waiting for transfers between devices, exchange(): lax.ppermute(blocks[i], 'axial', [(j, j ^ 2 * i) for j in range(size)])  25.9 us
    pallas_call x9, Pallas kernels, pallas(): pl.pallas_call(kernel, out_shape=[jax.ShapeDtypeStruct(shape, dtype) for...  16.8 us
    ppermute x2, starting transfers between devices, move_parts(): lax.ppermute(values, 'axial', [(j, (j + distance * width) % size) for j i...  5.73 us
    ppermute x2, waiting for transfers between devices, move_parts(): lax.ppermute(values, 'axial', [(j, (j + distance * width) % size) for j i...  4.73 us
    unnamed x23, local copies, waits for them, and re-layouts  4.6 us
    ppermute x2, starting transfers between devices, from_sections(): lax.ppermute(weight, 'section', [((i + shift) % sections, i) for i in ran...  3.63 us
    ppermute x16, waiting for transfers between devices, with_neighbour(): return own + [lax.ppermute(piece, 'axial', swap) for piece in own]  2.53 us
  transfers between devices with their start and end apart: 44, of which 20 were waited for; matrix products, arithmetic and copies ran while one was open for 5% of the time, Pallas kernels for 10%

profile of v4, /device:TPU:0, one launch (start us, length us, event | category | flops | bytes accessed | tf_op | source)
XLA Modules:
  0.0 102.3 jit_solution(18168491137636091479)
XLA Ops:
  1.6 3.0 %collective-permute-start = (bf16[643,128]{1,0:T(8,128)(2,1)S(1)}, bf16[643,128]{1,0:T(8,128)(2,1)S(1)}, u32[]{:S(2)}, u32[]{:S(2)}) collective-permute-start(bf16[643,128]{1,0:T(8,128)(2,1)S(1)} %pad_maximum_fusion.1), channel_id=1, source_target_pairs={{16,0},{0,16},{17,1},{1,17},{18,2},{2,18},{19,3},{3,19},{20,4},{4,... | collective-permute-start | bytes 493832 | tf_op jit(solution)/shard_map/ppermute | solution.py:265
  5.8 2.7 %collective-permute-start.8 = (bf16[8,128,128]{2,1,0:T(8,128)(2,1)S(1)}, bf16[8,128,128]{2,1,0:T(8,128)(2,1)S(1)}, u32[]{:S(2)}, u32[]{:S(2)}) collective-permute-start(bf16[8,128,128]{2,1,0:T(8,128)(2,1)S(1)} %get-tuple-element.97), channel_id=1, source_target_pairs={{0,8},{1,9},{2,10},{3,11},{4,12},{5,13},{6,14},{7,15},{8,0},{9,1},... | collective-permute-start | bytes 786440 | tf_op jit(solution)/shard_map/ppermute | solution.py:258
  11.9 1.6 %collective-permute-start.1 = (bf16[2,256,128]{2,1,0:T(8,128)(2,1)S(1)}, bf16[2,256,128]{2,1,0:T(8,128)(2,1)S(1)}, u32[]{:S(2)}, u32[]{:S(2)}) collective-permute-start(bf16[2,256,128]{2,1,0:T(8,128)(2,1)S(1)} %get-tuple-element.52), channel_id=1, source_target_pairs={{0,2},{1,3},{2,0},{3,1},{4,6},{5,7},{6,4},{7,5},{8,10},{9,11},{10,... | collective-permute-start | bytes 393224 | tf_op jit(solution)/shard_map/ppermute | solution.py:238
  13.5 1.6 %collective-permute-start.2 = (bf16[2,256,128]{2,1,0:T(8,128)(2,1)S(1)}, bf16[2,256,128]{2,1,0:T(8,128)(2,1)S(1)}, u32[]{:S(2)}, u32[]{:S(2)}) collective-permute-start(bf16[2,256,128]{2,1,0:T(8,128)(2,1)S(1)} %get-tuple-element.53), channel_id=1, source_target_pairs={{0,4},{1,5},{2,6},{3,7},{4,0},{5,1},{6,2},{7,3},{8,12},{9,13},{10,... | collective-permute-start | bytes 393224 | tf_op jit(solution)/shard_map/ppermute | solution.py:238
  15.5 4.7 %collective-permute-done.8.pair = bf16[8,128,128]{2,1,0:T(8,128)(2,1)S(1)} collective-permute-done((bf16[8,128,128]{2,1,0:T(8,128)(2,1)S(1)}, bf16[8,128,128]{2,1,0:T(8,128)(2,1)S(1)}, u32[]{:S(2)}, u32[]{:S(2)}) %collective-permute-start.8) | collective-permute-done | bytes 262176 | tf_op jit(solution)/shard_map/ppermute | solution.py:258
  21.5 1.6 %collective-permute-start.9 = (bf16[2,256,128]{2,1,0:T(8,128)(2,1)S(1)}, bf16[2,256,128]{2,1,0:T(8,128)(2,1)S(1)}, u32[]{:S(2)}, u32[]{:S(2)}) collective-permute-start(bf16[2,256,128]{2,1,0:T(8,128)(2,1)S(1)} %get-tuple-element.56), channel_id=1, source_target_pairs={{0,2},{1,3},{2,0},{3,1},{4,6},{5,7},{6,4},{7,5},{8,10},{9,11},{10,... | collective-permute-start | bytes 393224 | tf_op jit(solution)/shard_map/ppermute | solution.py:238
  26.5 1.4 %collective-permute-done.9.refs_9_ = bf16[2,256,128]{2,1,0:T(8,128)(2,1)S(1)} collective-permute-done((bf16[2,256,128]{2,1,0:T(8,128)(2,1)S(1)}, bf16[2,256,128]{2,1,0:T(8,128)(2,1)S(1)}, u32[]{:S(2)}, u32[]{:S(2)}) %collective-permute-start.9) | collective-permute-done | bytes 131104 | tf_op jit(solution)/shard_map/ppermute | solution.py:238
  28.0 2.4 %collective-permute-done.10.refs_10_ = bf16[2,256,128]{2,1,0:T(8,128)(2,1)S(1)} collective-permute-done((bf16[2,256,128]{2,1,0:T(8,128)(2,1)S(1)}, bf16[2,256,128]{2,1,0:T(8,128)(2,1)S(1)}, u32[]{:S(2)}, u32[]{:S(2)}) %collective-permute-start.10) | collective-permute-done | bytes 131104 | tf_op jit(solution)/shard_map/ppermute | solution.py:238
  30.4 2.0 %collective-permute-done.11.refs_11_ = bf16[2,256,128]{2,1,0:T(8,128)(2,1)S(1)} collective-permute-done((bf16[2,256,128]{2,1,0:T(8,128)(2,1)S(1)}, bf16[2,256,128]{2,1,0:T(8,128)(2,1)S(1)}, u32[]{:S(2)}, u32[]{:S(2)}) %collective-permute-start.11) | collective-permute-done | bytes 131104 | tf_op jit(solution)/shard_map/ppermute | solution.py:238
  34.3 1.5 %shard_map.75 = (bf16[256,128]{1,0:T(8,128)(2,1)S(1)}, bf16[256,128]{1,0:T(8,128)(2,1)S(1)}, bf16[256,128]{1,0:T(8,128)(2,1)S(1)}, bf16[256,128]{1,0:T(8,128)(2,...) custom-call(s32[3]{0:T(128)S(1)} %pad_add_fusion.here, ...), custom_call_target="tpu_custom_call" | custom-call | flops 67108864 | tf_op jit(solution)/shard_map/pallas_call | solution.py:217
  35.8 1.6 %collective-permute-start.16 = (bf16[256,128]{1,0:T(8,128)(2,1)S(1)}, bf16[256,128]{1,0:T(8,128)(2,1)S(1)}, u32[]{:S(2)}, u32[]{:S(2)}) collective-permute-start(bf16[256,128]{1,0:T(8,128)(2,1)S(1)} %get-tuple-element.60), channel_id=1, source_target_pairs={{0,2},{1,3},{2,0},{3,1},{4,6},{5,7},{6,4},{7,5},{8,10},{9,11},{10,... | collective-permute-start | bytes 196616 | tf_op jit(solution)/shard_map/ppermute | solution.py:238
  38.0 1.4 %collective-permute-start.18 = (bf16[256,128]{1,0:T(8,128)(2,1)S(1)}, bf16[256,128]{1,0:T(8,128)(2,1)S(1)}, u32[]{:S(2)}, u32[]{:S(2)}) collective-permute-start(bf16[256,128]{1,0:T(8,128)(2,1)S(1)} %get-tuple-element.62), channel_id=1, source_target_pairs={{0,6},{1,7},{2,4},{3,5},{4,2},{5,3},{6,0},{7,1},{8,14},{9,15},{10,... | collective-permute-start | bytes 196616 | tf_op jit(solution)/shard_map/ppermute | solution.py:238
  39.3 1.5 %collective-permute-start.27 = (bf16[256,128]{1,0:T(8,128)(2,1)S(1)}, bf16[256,128]{1,0:T(8,128)(2,1)S(1)}, u32[]{:S(2)}, u32[]{:S(2)}) collective-permute-start(bf16[256,128]{1,0:T(8,128)(2,1)S(1)} %get-tuple-element.76), channel_id=1, source_target_pairs={{0,2},{1,3},{2,0},{3,1},{4,6},{5,7},{6,4},{7,5},{8,10},{9,11},{10,... | collective-permute-start | bytes 196616 | tf_op jit(solution)/shard_map/ppermute | solution.py:238
  42.0 1.4 %collective-permute-done.18.refs_3_ = bf16[256,128]{1,0:T(8,128)(2,1)S(1)} collective-permute-done((bf16[256,128]{1,0:T(8,128)(2,1)S(1)}, bf16[256,128]{1,0:T(8,128)(2,1)S(1)}, u32[]{:S(2)}, u32[]{:S(2)}) %collective-permute-start.18) | collective-permute-done | bytes 65568 | tf_op jit(solution)/shard_map/ppermute | solution.py:238
  43.4 2.1 %shard_map.76 = (bf16[2,256,128]{2,1,0:T(8,128)(2,1)S(1)}, bf16[2,256,128]{2,1,0:T(8,128)(2,1)S(1)}, bf16[2,256,128]{2,1,0:T(8,128)(2,1)S(1)}, bf16[2,256,128]{2...) custom-call(s32[3]{0:T(128)S(1)} %pad_add_fusion.here, ...), custom_call_target="tpu_custom_call" | custom-call | flops 469762048 | tf_op jit(solution)/shard_map/pallas_call | solution.py:217
  47.5 1.6 %collective-permute-start.22 = (bf16[2,256,128]{2,1,0:T(8,128)(2,1)S(1)}, bf16[2,256,128]{2,1,0:T(8,128)(2,1)S(1)}, u32[]{:S(2)}, u32[]{:S(2)}) collective-permute-start(bf16[2,256,128]{2,1,0:T(8,128)(2,1)S(1)} %get-tuple-element.74), channel_id=1, source_target_pairs={{0,6},{1,7},{2,4},{3,5},{4,2},{5,3},{6,0},{7,1},{8,14},{9,15},{10,... | collective-permute-start | bytes 393224 | tf_op jit(solution)/shard_map/ppermute | solution.py:238
  51.1 4.3 %collective-permute-done.29.refs_3_ = bf16[256,128]{1,0:T(8,128)(2,1)S(1)} collective-permute-done((bf16[256,128]{1,0:T(8,128)(2,1)S(1)}, bf16[256,128]{1,0:T(8,128)(2,1)S(1)}, u32[]{:S(2)}, u32[]{:S(2)}) %collective-permute-start.29) | collective-permute-done | bytes 65568 | tf_op jit(solution)/shard_map/ppermute | solution.py:238
  56.2 2.1 %shard_map.77 = (bf16[2,256,128]{2,1,0:T(8,128)(2,1)S(1)}, bf16[2,256,128]{2,1,0:T(8,128)(2,1)S(1)}, bf16[2,256,128]{2,1,0:T(8,128)(2,1)S(1)}, bf16[2,256,128]{2...) custom-call(s32[3]{0:T(128)S(1)} %pad_add_fusion.here, ...), custom_call_target="tpu_custom_call" | custom-call | flops 469762048 | tf_op jit(solution)/shard_map/pallas_call | solution.py:217
  61.0 1.5 %collective-permute-start.32 = (bf16[2,256,128]{2,1,0:T(8,128)(2,1)S(1)}, bf16[2,256,128]{2,1,0:T(8,128)(2,1)S(1)}, u32[]{:S(2)}, u32[]{:S(2)}) collective-permute-start(bf16[2,256,128]{2,1,0:T(8,128)(2,1)S(1)} %get-tuple-element.84), channel_id=1, source_target_pairs={{0,6},{1,7},{2,4},{3,5},{4,2},{5,3},{6,0},{7,1},{8,14},{9,15},{10,... | collective-permute-start | bytes 393224 | tf_op jit(solution)/shard_map/ppermute | solution.py:238
  63.0 1.4 %collective-permute-done.30.refs_9_ = bf16[2,256,128]{2,1,0:T(8,128)(2,1)S(1)} collective-permute-done((bf16[2,256,128]{2,1,0:T(8,128)(2,1)S(1)}, bf16[2,256,128]{2,1,0:T(8,128)(2,1)S(1)}, u32[]{:S(2)}, u32[]{:S(2)}) %collective-permute-start.30) | collective-permute-done | bytes 131104 | tf_op jit(solution)/shard_map/ppermute | solution.py:238
  64.5 2.0 %collective-permute-done.31.refs_10_ = bf16[2,256,128]{2,1,0:T(8,128)(2,1)S(1)} collective-permute-done((bf16[2,256,128]{2,1,0:T(8,128)(2,1)S(1)}, bf16[2,256,128]{2,1,0:T(8,128)(2,1)S(1)}, u32[]{:S(2)}, u32[]{:S(2)}) %collective-permute-start.31) | collective-permute-done | bytes 131104 | tf_op jit(solution)/shard_map/ppermute | solution.py:238
  66.4 1.8 %collective-permute-done.32.refs_11_ = bf16[2,256,128]{2,1,0:T(8,128)(2,1)S(1)} collective-permute-done((bf16[2,256,128]{2,1,0:T(8,128)(2,1)S(1)}, bf16[2,256,128]{2,1,0:T(8,128)(2,1)S(1)}, u32[]{:S(2)}, u32[]{:S(2)}) %collective-permute-start.32) | collective-permute-done | bytes 131104 | tf_op jit(solution)/shard_map/ppermute | solution.py:238
  70.1 2.0 %shard_map.80 = (bf16[256,128]{1,0:T(8,128)(2,1)S(1)}, bf16[256,128]{1,0:T(8,128)(2,1)}, bf16[256,128]{1,0:T(8,128)(2,1)}, bf16[256,128]{1,0:T(8,128)(2,1)}) custom-call(s32[3]{0:T(128)S(1)} %pad_add_fusion.here, bf16[2,256,128]{2,1,0:T(8,128)(2,1)S(1)} %get-tuple-element.71.refs_0_, bf16[2,256,128]{2,1,0:T(8,128)(2,1)S(1)} %collective-permute-done.20.refs_1_, ...), custom_call_target="tpu_custom_call" | custom-call | flops 33554432 | tf_op jit(solution)/shard_map/pallas_call | solution.py:217
  74.1 1.5 %collective-permute-start.42 = (bf16[256,128]{1,0:T(8,128)(2,1)}, bf16[256,128]{1,0:T(8,128)(2,1)}, u32[]{:S(2)}, u32[]{:S(2)}) collective-permute-start(bf16[256,128]{1,0:T(8,128)(2,1)} %get-tuple-element.94), channel_id=1, source_target_pairs={{0,6},{1,7},{2,4},{3,5},{4,2},{5,3},{6,0},{7,1},{8,14},{9,15},{10,... | collective-permute-start | bytes 196616 | tf_op jit(solution)/shard_map/ppermute | solution.py:238
  78.1 1.5 %collective-permute-done.42.refs_3_ = bf16[256,128]{1,0:T(8,128)(2,1)} collective-permute-done((bf16[256,128]{1,0:T(8,128)(2,1)}, bf16[256,128]{1,0:T(8,128)(2,1)}, u32[]{:S(2)}, u32[]{:S(2)}) %collective-permute-start.42) | collective-permute-done | bytes 65568 | tf_op jit(solution)/shard_map/ppermute | solution.py:238
  80.5 2.7 %shard_map.81 = bf16[1,8,128,128]{3,2,1,0:T(8,128)(2,1)} custom-call(s32[3]{0:T(128)S(1)} %pad_add_fusion.here, bf16[256,128]{1,0:T(8,128)(2,1)S(1)} %get-tuple-element.91.refs_0_, bf16[256,128]{1,0:T(8,128)(2,1)S(1)} %collective-permute-done.40.refs_1_, bf16[256,128]{1,0:T(8,128)(2,1)} %collective-permute-done.41.refs_2_, ...), custom_call_target="tpu_custom_call" | custom-call | flops 301989888 | tf_op jit(solution)/shard_map/pallas_call | solution.py:217
  83.2 3.1 %collective-permute-start.43 = (bf16[1,8,128,128]{3,2,1,0:T(8,128)(2,1)}, bf16[1,8,128,128]{3,2,1,0:T(8,128)(2,1)}, u32[]{:S(2)}, u32[]{:S(2)}) collective-permute-start(bf16[1,8,128,128]{3,2,1,0:T(8,128)(2,1)} %shard_map.81), channel_id=1, source_target_pairs={{0,8},{1,9},{2,10},{3,11},{4,12},{5,13},{6,14},{7,15},{8,0},{9,1},... | collective-permute-start | bytes 786440 | tf_op jit(solution)/shard_map/ppermute | solution.py:258
  89.7 1.5 %collective-permute-start.39 = (bf16[256,128]{1,0:T(8,128)(2,1)S(1)}, bf16[256,128]{1,0:T(8,128)(2,1)S(1)}, u32[]{:S(2)}, u32[]{:S(2)}) collective-permute-start(bf16[256,128]{1,0:T(8,128)(2,1)S(1)} %get-tuple-element.88), channel_id=1, source_target_pairs={{0,6},{1,7},{2,4},{3,5},{4,2},{5,3},{6,0},{7,1},{8,14},{9,15},{10,... | collective-permute-start | bytes 196616 | tf_op jit(solution)/shard_map/ppermute | solution.py:238
  91.1 1.4 %collective-permute-done.37.refs_1_ = bf16[256,128]{1,0:T(8,128)(2,1)S(1)} collective-permute-done((bf16[256,128]{1,0:T(8,128)(2,1)S(1)}, bf16[256,128]{1,0:T(8,128)(2,1)S(1)}, u32[]{:S(2)}, u32[]{:S(2)}) %collective-permute-start.37) | collective-permute-done | bytes 65568 | tf_op jit(solution)/shard_map/ppermute | solution.py:238
  93.4 4.8 %collective-permute-done.39.refs_3_ = bf16[256,128]{1,0:T(8,128)(2,1)S(1)} collective-permute-done((bf16[256,128]{1,0:T(8,128)(2,1)S(1)}, bf16[256,128]{1,0:T(8,128)(2,1)S(1)}, u32[]{:S(2)}, u32[]{:S(2)}) %collective-permute-start.39) | collective-permute-done | bytes 65568 | tf_op jit(solution)/shard_map/ppermute | solution.py:238
  98.2 2.4 %shard_map.79 = bf16[2,8,128,128]{3,2,1,0:T(8,128)(2,1)} custom-call(s32[3]{0:T(128)S(1)} %pad_add_fusion.here, bf16[256,128]{1,0:T(8,128)(2,1)S(1)} %get-tuple-element.85.refs_0_, bf16[256,128]{1,0:T(8,128)(2,1)S(1)} %collective-permute-done.37.refs_1_, bf16[256,128]{1,0:T(8,128)(2,1)S(1)} %collective-permute-done.38.refs_2_, ...), custom_call_target="tpu_custom_call" | custom-call | flops 301989888 | tf_op jit(solution)/shard_map/pallas_call | solution.py:217
  100.7 1.7 %constant_dynamic-update-slice_fusion = bf16[2,8,128,128]{3,2,1,0:T(8,128)(2,1)} fusion(bf16[2,8,128,128]{3,2,1,0:T(8,128)(2,1)} %shard_map.79, bf16[1,8,128,128]{3,2,1,0:T(8,128)(2,1)} %collective-permute-done.43, s32[]{:T(128)S(6)} %select_n.113), kind=kLoop, calls=%fused_computation.14 | loop fusion | bytes 524292 | tf_op jit(solution)/shard_map/dynamic_update_slice | solution.py:397
  (116 shorter events, 34.4 us)
Async XLA Ops:
  1.6 8.6 %collective-permute-start = (bf16[643,128]{1,0:T(8,128)(2,1)S(1)}, bf16[643,128]{1,0:T(8,128)(2,1)S(1)}, u32[]{:S(2)}, u32[]{:S(2)}) collective-permute-start(bf16[643,128]{1,0:T(8,128)(2,1)S(1)} %pad_maximum_fusion.1), channel_id=1, source_target_pairs={{16,0},{0,16},{17,1},{1,17},{18,2},{2,18},{19,3},{3,19},{20,4},{4,... | collective-permute-start | bytes 493832 | tf_op jit(solution)/shard_map/ppermute | solution.py:265
  5.8 14.4 %collective-permute-start.8 = (bf16[8,128,128]{2,1,0:T(8,128)(2,1)S(1)}, bf16[8,128,128]{2,1,0:T(8,128)(2,1)S(1)}, u32[]{:S(2)}, u32[]{:S(2)}) collective-permute-start(bf16[8,128,128]{2,1,0:T(8,128)(2,1)S(1)} %get-tuple-element.97), channel_id=1, source_target_pairs={{0,8},{1,9},{2,10},{3,11},{4,12},{5,13},{6,14},{7,15},{8,0},{9,1},... | collective-permute-start | bytes 786440 | tf_op jit(solution)/shard_map/ppermute | solution.py:258
  8.6 12.9 %collective-permute-start.19 = (bf16[1152,128]{0,1:T(8,128)(2,1)S(1)}, bf16[1152,128]{0,1:T(8,128)(2,1)S(1)}, u32[]{:S(2)}, u32[]{:S(2)}) collective-permute-start(bf16[1152,128]{0,1:T(8,128)(2,1)S(1)} %pad_maximum_fusion), channel_id=1, source_target_pairs={{16,0},{0,16},{17,1},{1,17},{18,2},{2,18},{19,3},{3,19},{20,4},{4,... | collective-permute-start | bytes 884744 | tf_op jit(solution)/shard_map/ppermute | solution.py:265
  11.9 12.0 %collective-permute-start.1 = (bf16[2,256,128]{2,1,0:T(8,128)(2,1)S(1)}, bf16[2,256,128]{2,1,0:T(8,128)(2,1)S(1)}, u32[]{:S(2)}, u32[]{:S(2)}) collective-permute-start(bf16[2,256,128]{2,1,0:T(8,128)(2,1)S(1)} %get-tuple-element.52), channel_id=1, source_target_pairs={{0,2},{1,3},{2,0},{3,1},{4,6},{5,7},{6,4},{7,5},{8,10},{9,11},{10,... | collective-permute-start | bytes 393224 | tf_op jit(solution)/shard_map/ppermute | solution.py:238
  13.5 11.1 %collective-permute-start.2 = (bf16[2,256,128]{2,1,0:T(8,128)(2,1)S(1)}, bf16[2,256,128]{2,1,0:T(8,128)(2,1)S(1)}, u32[]{:S(2)}, u32[]{:S(2)}) collective-permute-start(bf16[2,256,128]{2,1,0:T(8,128)(2,1)S(1)} %get-tuple-element.53), channel_id=1, source_target_pairs={{0,4},{1,5},{2,6},{3,7},{4,0},{5,1},{6,2},{7,3},{8,12},{9,13},{10,... | collective-permute-start | bytes 393224 | tf_op jit(solution)/shard_map/ppermute | solution.py:238
  15.1 10.9 %collective-permute-start.3 = (bf16[2,256,128]{2,1,0:T(8,128)(2,1)S(1)}, bf16[2,256,128]{2,1,0:T(8,128)(2,1)S(1)}, u32[]{:S(2)}, u32[]{:S(2)}) collective-permute-start(bf16[2,256,128]{2,1,0:T(8,128)(2,1)S(1)} %get-tuple-element.54), channel_id=1, source_target_pairs={{0,6},{1,7},{2,4},{3,5},{4,2},{5,3},{6,0},{7,1},{8,14},{9,15},{10,... | collective-permute-start | bytes 393224 | tf_op jit(solution)/shard_map/ppermute | solution.py:238
  20.2 5.8 %collective-permute-start.4 = (bf16[2,256,128]{2,1,0:T(8,128)(2,1)S(1)}, bf16[2,256,128]{2,1,0:T(8,128)(2,1)S(1)}, u32[]{:S(2)}, u32[]{:S(2)}) collective-permute-start(bf16[2,256,128]{2,1,0:T(8,128)(2,1)S(1)} %get-tuple-element.51.refs_0_), channel_id=1, source_target_pairs={{0,1},{1,0},{2,3},{3,2},{4,5},{5,4},{6,7},{7,6},{8,9},{9,8},{10,11... | collective-permute-start | bytes 393224 | tf_op jit(solution)/shard_map/ppermute | solution.py:247
  21.5 6.4 %collective-permute-start.9 = (bf16[2,256,128]{2,1,0:T(8,128)(2,1)S(1)}, bf16[2,256,128]{2,1,0:T(8,128)(2,1)S(1)}, u32[]{:S(2)}, u32[]{:S(2)}) collective-permute-start(bf16[2,256,128]{2,1,0:T(8,128)(2,1)S(1)} %get-tuple-element.56), channel_id=1, source_target_pairs={{0,2},{1,3},{2,0},{3,1},{4,6},{5,7},{6,4},{7,5},{8,10},{9,11},{10,... | collective-permute-start | bytes 393224 | tf_op jit(solution)/shard_map/ppermute | solution.py:238
  24.0 6.4 %collective-permute-start.10 = (bf16[2,256,128]{2,1,0:T(8,128)(2,1)S(1)}, bf16[2,256,128]{2,1,0:T(8,128)(2,1)S(1)}, u32[]{:S(2)}, u32[]{:S(2)}) collective-permute-start(bf16[2,256,128]{2,1,0:T(8,128)(2,1)S(1)} %get-tuple-element.57), channel_id=1, source_target_pairs={{0,4},{1,5},{2,6},{3,7},{4,0},{5,1},{6,2},{7,3},{8,12},{9,13},{10,... | collective-permute-start | bytes 393224 | tf_op jit(solution)/shard_map/ppermute | solution.py:238
  24.7 7.7 %collective-permute-start.11 = (bf16[2,256,128]{2,1,0:T(8,128)(2,1)S(1)}, bf16[2,256,128]{2,1,0:T(8,128)(2,1)S(1)}, u32[]{:S(2)}, u32[]{:S(2)}) collective-permute-start(bf16[2,256,128]{2,1,0:T(8,128)(2,1)S(1)} %get-tuple-element.58), channel_id=1, source_target_pairs={{0,6},{1,7},{2,4},{3,5},{4,2},{5,3},{6,0},{7,1},{8,14},{9,15},{10,... | collective-permute-start | bytes 393224 | tf_op jit(solution)/shard_map/ppermute | solution.py:238
  26.0 6.4 %collective-permute-start.12 = (bf16[2,256,128]{2,1,0:T(8,128)(2,1)S(1)}, bf16[2,256,128]{2,1,0:T(8,128)(2,1)S(1)}, u32[]{:S(2)}, u32[]{:S(2)}) collective-permute-start(bf16[2,256,128]{2,1,0:T(8,128)(2,1)S(1)} %get-tuple-element.55.refs_8_), channel_id=1, source_target_pairs={{0,1},{1,0},{2,3},{3,2},{4,5},{5,4},{6,7},{7,6},{8,9},{9,8},{10,11... | collective-permute-start | bytes 393224 | tf_op jit(solution)/shard_map/ppermute | solution.py:247
  26.0 6.9 %collective-permute-start.5 = (bf16[2,256,128]{2,1,0:T(8,128)(2,1)S(1)}, bf16[2,256,128]{2,1,0:T(8,128)(2,1)S(1)}, u32[]{:S(2)}, u32[]{:S(2)}) collective-permute-start(bf16[2,256,128]{2,1,0:T(8,128)(2,1)S(1)} %collective-permute-done.1.refs_1_), channel_id=1, source_target_pairs={{0,1},{1,0},{2,3},{3,2},{4,5},{5,4},{6,7},{7,6},{8,9},{9,8},{10,11... | collective-permute-start | bytes 393224 | tf_op jit(solution)/shard_map/ppermute | solution.py:247
  27.9 5.1 %collective-permute-start.6 = (bf16[2,256,128]{2,1,0:T(8,128)(2,1)S(1)}, bf16[2,256,128]{2,1,0:T(8,128)(2,1)S(1)}, u32[]{:S(2)}, u32[]{:S(2)}) collective-permute-start(bf16[2,256,128]{2,1,0:T(8,128)(2,1)S(1)} %collective-permute-done.2.refs_2_), channel_id=1, source_target_pairs={{0,1},{1,0},{2,3},{3,2},{4,5},{5,4},{6,7},{7,6},{8,9},{9,8},{10,11... | collective-permute-start | bytes 393224 | tf_op jit(solution)/shard_map/ppermute | solution.py:247
  35.8 6.2 %collective-permute-start.16 = (bf16[256,128]{1,0:T(8,128)(2,1)S(1)}, bf16[256,128]{1,0:T(8,128)(2,1)S(1)}, u32[]{:S(2)}, u32[]{:S(2)}) collective-permute-start(bf16[256,128]{1,0:T(8,128)(2,1)S(1)} %get-tuple-element.60), channel_id=1, source_target_pairs={{0,2},{1,3},{2,0},{3,1},{4,6},{5,7},{6,4},{7,5},{8,10},{9,11},{10,... | collective-permute-start | bytes 196616 | tf_op jit(solution)/shard_map/ppermute | solution.py:238
  38.0 5.4 %collective-permute-start.18 = (bf16[256,128]{1,0:T(8,128)(2,1)S(1)}, bf16[256,128]{1,0:T(8,128)(2,1)S(1)}, u32[]{:S(2)}, u32[]{:S(2)}) collective-permute-start(bf16[256,128]{1,0:T(8,128)(2,1)S(1)} %get-tuple-element.62), channel_id=1, source_target_pairs={{0,6},{1,7},{2,4},{3,5},{4,2},{5,3},{6,0},{7,1},{8,14},{9,15},{10,... | collective-permute-start | bytes 196616 | tf_op jit(solution)/shard_map/ppermute | solution.py:238
  39.3 9.8 %collective-permute-start.27 = (bf16[256,128]{1,0:T(8,128)(2,1)S(1)}, bf16[256,128]{1,0:T(8,128)(2,1)S(1)}, u32[]{:S(2)}, u32[]{:S(2)}) collective-permute-start(bf16[256,128]{1,0:T(8,128)(2,1)S(1)} %get-tuple-element.76), channel_id=1, source_target_pairs={{0,2},{1,3},{2,0},{3,1},{4,6},{5,7},{6,4},{7,5},{8,10},{9,11},{10,... | collective-permute-start | bytes 196616 | tf_op jit(solution)/shard_map/ppermute | solution.py:238
  41.3 8.5 %collective-permute-start.28 = (bf16[256,128]{1,0:T(8,128)(2,1)S(1)}, bf16[256,128]{1,0:T(8,128)(2,1)S(1)}, u32[]{:S(2)}, u32[]{:S(2)}) collective-permute-start(bf16[256,128]{1,0:T(8,128)(2,1)S(1)} %get-tuple-element.77), channel_id=1, source_target_pairs={{0,4},{1,5},{2,6},{3,7},{4,0},{5,1},{6,2},{7,3},{8,12},{9,13},{10,... | collective-permute-start | bytes 196616 | tf_op jit(solution)/shard_map/ppermute | solution.py:238
  45.6 14.7 %collective-permute-start.20 = (bf16[2,256,128]{2,1,0:T(8,128)(2,1)S(1)}, bf16[2,256,128]{2,1,0:T(8,128)(2,1)S(1)}, u32[]{:S(2)}, u32[]{:S(2)}) collective-permute-start(bf16[2,256,128]{2,1,0:T(8,128)(2,1)S(1)} %get-tuple-element.72), channel_id=1, source_target_pairs={{0,2},{1,3},{2,0},{3,1},{4,6},{5,7},{6,4},{7,5},{8,10},{9,11},{10,... | collective-permute-start | bytes 393224 | tf_op jit(solution)/shard_map/ppermute | solution.py:238
  46.5 14.5 %collective-permute-start.21 = (bf16[2,256,128]{2,1,0:T(8,128)(2,1)S(1)}, bf16[2,256,128]{2,1,0:T(8,128)(2,1)S(1)}, u32[]{:S(2)}, u32[]{:S(2)}) collective-permute-start(bf16[2,256,128]{2,1,0:T(8,128)(2,1)S(1)} %get-tuple-element.73), channel_id=1, source_target_pairs={{0,4},{1,5},{2,6},{3,7},{4,0},{5,1},{6,2},{7,3},{8,12},{9,13},{10,... | collective-permute-start | bytes 393224 | tf_op jit(solution)/shard_map/ppermute | solution.py:238
  47.5 15.0 %collective-permute-start.22 = (bf16[2,256,128]{2,1,0:T(8,128)(2,1)S(1)}, bf16[2,256,128]{2,1,0:T(8,128)(2,1)S(1)}, u32[]{:S(2)}, u32[]{:S(2)}) collective-permute-start(bf16[2,256,128]{2,1,0:T(8,128)(2,1)S(1)} %get-tuple-element.74), channel_id=1, source_target_pairs={{0,6},{1,7},{2,4},{3,5},{4,2},{5,3},{6,0},{7,1},{8,14},{9,15},{10,... | collective-permute-start | bytes 393224 | tf_op jit(solution)/shard_map/ppermute | solution.py:238
  49.8 12.7 %collective-permute-start.23 = (bf16[2,256,128]{2,1,0:T(8,128)(2,1)S(1)}, bf16[2,256,128]{2,1,0:T(8,128)(2,1)S(1)}, u32[]{:S(2)}, u32[]{:S(2)}) collective-permute-start(bf16[2,256,128]{2,1,0:T(8,128)(2,1)S(1)} %get-tuple-element.71.refs_0_), channel_id=1, source_target_pairs={{0,1},{1,0},{2,3},{3,2},{4,5},{5,4},{6,7},{7,6},{8,9},{9,8},{10,11... | collective-permute-start | bytes 393224 | tf_op jit(solution)/shard_map/ppermute | solution.py:247
  49.8 5.6 %collective-permute-start.29 = (bf16[256,128]{1,0:T(8,128)(2,1)S(1)}, bf16[256,128]{1,0:T(8,128)(2,1)S(1)}, u32[]{:S(2)}, u32[]{:S(2)}) collective-permute-start(bf16[256,128]{1,0:T(8,128)(2,1)S(1)} %get-tuple-element.78), channel_id=1, source_target_pairs={{0,6},{1,7},{2,4},{3,5},{4,2},{5,3},{6,0},{7,1},{8,14},{9,15},{10,... | collective-permute-start | bytes 196616 | tf_op jit(solution)/shard_map/ppermute | solution.py:238
  59.0 5.5 %collective-permute-start.30 = (bf16[2,256,128]{2,1,0:T(8,128)(2,1)S(1)}, bf16[2,256,128]{2,1,0:T(8,128)(2,1)S(1)}, u32[]{:S(2)}, u32[]{:S(2)}) collective-permute-start(bf16[2,256,128]{2,1,0:T(8,128)(2,1)S(1)} %get-tuple-element.82), channel_id=1, source_target_pairs={{0,2},{1,3},{2,0},{3,1},{4,6},{5,7},{6,4},{7,5},{8,10},{9,11},{10,... | collective-permute-start | bytes 393224 | tf_op jit(solution)/shard_map/ppermute | solution.py:238
  60.2 6.2 %collective-permute-start.31 = (bf16[2,256,128]{2,1,0:T(8,128)(2,1)S(1)}, bf16[2,256,128]{2,1,0:T(8,128)(2,1)S(1)}, u32[]{:S(2)}, u32[]{:S(2)}) collective-permute-start(bf16[2,256,128]{2,1,0:T(8,128)(2,1)S(1)} %get-tuple-element.83), channel_id=1, source_target_pairs={{0,4},{1,5},{2,6},{3,7},{4,0},{5,1},{6,2},{7,3},{8,12},{9,13},{10,... | collective-permute-start | bytes 393224 | tf_op jit(solution)/shard_map/ppermute | solution.py:238
  61.0 7.2 %collective-permute-start.32 = (bf16[2,256,128]{2,1,0:T(8,128)(2,1)S(1)}, bf16[2,256,128]{2,1,0:T(8,128)(2,1)S(1)}, u32[]{:S(2)}, u32[]{:S(2)}) collective-permute-start(bf16[2,256,128]{2,1,0:T(8,128)(2,1)S(1)} %get-tuple-element.84), channel_id=1, source_target_pairs={{0,6},{1,7},{2,4},{3,5},{4,2},{5,3},{6,0},{7,1},{8,14},{9,15},{10,... | collective-permute-start | bytes 393224 | tf_op jit(solution)/shard_map/ppermute | solution.py:238
  62.5 5.7 %collective-permute-start.33 = (bf16[2,256,128]{2,1,0:T(8,128)(2,1)S(1)}, bf16[2,256,128]{2,1,0:T(8,128)(2,1)S(1)}, u32[]{:S(2)}, u32[]{:S(2)}) collective-permute-start(bf16[2,256,128]{2,1,0:T(8,128)(2,1)S(1)} %get-tuple-element.81.refs_8_), channel_id=1, source_target_pairs={{0,1},{1,0},{2,3},{3,2},{4,5},{5,4},{6,7},{7,6},{8,9},{9,8},{10,11... | collective-permute-start | bytes 393224 | tf_op jit(solution)/shard_map/ppermute | solution.py:247
  62.5 6.2 %collective-permute-start.24 = (bf16[2,256,128]{2,1,0:T(8,128)(2,1)S(1)}, bf16[2,256,128]{2,1,0:T(8,128)(2,1)S(1)}, u32[]{:S(2)}, u32[]{:S(2)}) collective-permute-start(bf16[2,256,128]{2,1,0:T(8,128)(2,1)S(1)} %collective-permute-done.20.refs_1_), channel_id=1, source_target_pairs={{0,1},{1,0},{2,3},{3,2},{4,5},{5,4},{6,7},{7,6},{8,9},{9,8},{10,11... | collective-permute-start | bytes 393224 | tf_op jit(solution)/shard_map/ppermute | solution.py:247
  72.1 5.3 %collective-permute-start.40 = (bf16[256,128]{1,0:T(8,128)(2,1)}, bf16[256,128]{1,0:T(8,128)(2,1)S(1)}, u32[]{:S(2)}, u32[]{:S(2)}) collective-permute-start(bf16[256,128]{1,0:T(8,128)(2,1)} %get-tuple-element.92), channel_id=1, source_target_pairs={{0,2},{1,3},{2,0},{3,1},{4,6},{5,7},{6,4},{7,5},{8,10},{9,11},{10,... | collective-permute-start | bytes 196616 | tf_op jit(solution)/shard_map/ppermute | solution.py:238
  74.1 5.5 %collective-permute-start.42 = (bf16[256,128]{1,0:T(8,128)(2,1)}, bf16[256,128]{1,0:T(8,128)(2,1)}, u32[]{:S(2)}, u32[]{:S(2)}) collective-permute-start(bf16[256,128]{1,0:T(8,128)(2,1)} %get-tuple-element.94), channel_id=1, source_target_pairs={{0,6},{1,7},{2,4},{3,5},{4,2},{5,3},{6,0},{7,1},{8,14},{9,15},{10,... | collective-permute-start | bytes 196616 | tf_op jit(solution)/shard_map/ppermute | solution.py:238
  83.2 17.5 %collective-permute-start.43 = (bf16[1,8,128,128]{3,2,1,0:T(8,128)(2,1)}, bf16[1,8,128,128]{3,2,1,0:T(8,128)(2,1)}, u32[]{:S(2)}, u32[]{:S(2)}) collective-permute-start(bf16[1,8,128,128]{3,2,1,0:T(8,128)(2,1)} %shard_map.81), channel_id=1, source_target_pairs={{0,8},{1,9},{2,10},{3,11},{4,12},{5,13},{6,14},{7,15},{8,0},{9,1},... | collective-permute-start | bytes 786440 | tf_op jit(solution)/shard_map/ppermute | solution.py:258
  88.3 5.1 %collective-permute-start.38 = (bf16[256,128]{1,0:T(8,128)(2,1)S(1)}, bf16[256,128]{1,0:T(8,128)(2,1)S(1)}, u32[]{:S(2)}, u32[]{:S(2)}) collective-permute-start(bf16[256,128]{1,0:T(8,128)(2,1)S(1)} %get-tuple-element.87), channel_id=1, source_target_pairs={{0,4},{1,5},{2,6},{3,7},{4,0},{5,1},{6,2},{7,3},{8,12},{9,13},{10,... | collective-permute-start | bytes 196616 | tf_op jit(solution)/shard_map/ppermute | solution.py:238
  89.7 8.6 %collective-permute-start.39 = (bf16[256,128]{1,0:T(8,128)(2,1)S(1)}, bf16[256,128]{1,0:T(8,128)(2,1)S(1)}, u32[]{:S(2)}, u32[]{:S(2)}) collective-permute-start(bf16[256,128]{1,0:T(8,128)(2,1)S(1)} %get-tuple-element.88), channel_id=1, source_target_pairs={{0,6},{1,7},{2,4},{3,5},{4,2},{5,3},{6,0},{7,1},{8,14},{9,15},{10,... | collective-permute-start | bytes 196616 | tf_op jit(solution)/shard_map/ppermute | solution.py:238
  (23 other events, 61.0 us)

commit v5 on v4

--- a/solution.py
+++ b/solution.py
@@ -206,6 +206,24 @@
         return carry
 
     lax.fori_loop(0, rows // count, step, 0)
+
+
+def fetch_kernel(index, source, target, arrived):
+    copy = pltpu.make_async_copy(source.at[index[0]], target, arrived)
+    copy.start()
+    copy.wait()
+
+
+def fetch(source, index):
+    return pl.pallas_call(
+        fetch_kernel,
+        out_shape=jax.ShapeDtypeStruct(source.shape[1:], source.dtype),
+        in_specs=[
+            pl.BlockSpec(memory_space=pltpu.SMEM), pl.BlockSpec(memory_space=pl.ANY)
+        ],
+        out_specs=pl.BlockSpec(memory_space=pltpu.VMEM),
+        scratch_shapes=[pltpu.SemaphoreType.DMA],
+    )(index.astype(jnp.int32).reshape(1), source)
 
 
 def call(kernel, outs, scratch, flops, here, *operands):
@@ -297,16 +315,16 @@
 
     pairs = []
     for k in range(parts):
-        crop = lax.dynamic_index_in_dim(
-            pair_in, section * own_count + (part + parts - k) % parts, 0, keepdims=False
-        )
-        pairs.append(move_parts(crop, -k, width))
+        crop = section * own_count + (part + parts - k) % parts
+        if k == 0:
+            pairs.append(fetch(pair_in, crop))
+            continue
+        sent = lax.dynamic_index_in_dim(pair_in, crop, 0, keepdims=False)
+        pairs.append(move_parts(sent, -k, width))
     heads = from_sections(
         jnp.concatenate((proj_weights[0].reshape(-1, channels), norm_gains[0])), sections
     )
-    others = from_sections(
-        jnp.concatenate((out_weights[0].T, up_weights[0].T, down_weights[0])), sections
-    )
+    others = [from_sections(w[0], sections) for w in (out_weights, up_weights, down_weights)]
     kinds = proj_weights.shape[1]
 
     def head_of(slots, layer):
@@ -355,10 +373,7 @@
         proj, gain = head_of(heads, layer)
         projs.append(proj)
         gains.append(gain)
-    bodies = by_layer(others, section)
-    outs = [w[:channels] for w in bodies]
-    ups = [w[channels : channels + hidden] for w in bodies]
-    downs = [w[channels + hidden :].T for w in bodies]
+    outs, ups, downs = [[w.T for w in by_layer(slots, section)] for slots in others]
     finished = [None] * parts
     for layer in range(sections):
         edges = [with_neighbour(edges[k]) for k in range(parts)]

time: 103 us -> 99.5 us (0.966)
  local copies, waits for them, and re-layouts: 10.1 us -> 4.73 us
  starting transfers between devices: 39.9 us -> 43.7 us
    ppermute x2, waiting for transfers between devices: 4.73 us -> 1.84 us  [move_parts(): lax.ppermute(values, 'axial', [(j, (j + distance * width) % size) for j i...]
    unnamed x23 -> x17, local copies, waits for them, and re-layouts: 4.6 us -> 2.37 us
    ppermute x2 -> x4, starting transfers between devices: 3.63 us -> 5.79 us  [from_sections(): lax.ppermute(weight, 'section', [((i + shift) % sections, i) for i in ran...]
    ppermute x24, waiting for transfers between devices: 25.9 us -> 28 us  [exchange(): lax.ppermute(blocks[i], 'axial', [(j, j ^ 2 * i) for j in range(size)])]
    pallas_call x9, Pallas kernels: 16.8 us -> 15.1 us  [pallas(): pl.pallas_call(kernel, out_shape=[jax.ShapeDtypeStruct(shape, dtype) for...]
    pallas_call x0 -> x1, Pallas kernels: none -> 1.7 us  [fetch(): pl.pallas_call(fetch_kernel, out_shape=jax.ShapeDtypeStruct(source.shape[...]
    ppermute x24, starting transfers between devices: 28.3 us -> 29.7 us  [exchange(): lax.ppermute(blocks[i], 'axial', [(j, j ^ 2 * i) for j in range(size)])]
    slice x6 -> x0, local copies, waits for them, and re-layouts: 1.39 us -> none  [the longest x2 1.16 us: per_device(): ups = [w[channels:channels + hidden] for w in bodies]]
  transfers between devices with their start and end apart: 44 -> 46, of which waited for: 20 -> 21; matrix products, arithmetic and copies ran while one was open for 5% -> 2% of each run, Pallas kernels for 10% -> 12%
where the time goes in v5:
time: 99.5 us; the launch traced here: 99.2 us
  starting transfers between devices  43.7 us (44%)
  waiting for transfers between devices  32.4 us (33%)
  Pallas kernels  16.8 us (17%)
  local copies, waits for them, and re-layouts  4.73 us (5%)
  other arithmetic  1.29 us (1%)
    ppermute x24, starting transfers between devices, exchange(): lax.ppermute(blocks[i], 'axial', [(j, j ^ 2 * i) for j in range(size)])  29.7 us
    ppermute x24, waiting for transfers between devices, exchange(): lax.ppermute(blocks[i], 'axial', [(j, j ^ 2 * i) for j in range(size)])  28 us
    pallas_call x9, Pallas kernels, pallas(): pl.pallas_call(kernel, out_shape=[jax.ShapeDtypeStruct(shape, dtype) for...  15.1 us
    ppermute x4, starting transfers between devices, from_sections(): lax.ppermute(weight, 'section', [((i + shift) % sections, i) for i in ran...  5.79 us
    ppermute x2, starting transfers between devices, move_parts(): lax.ppermute(values, 'axial', [(j, (j + distance * width) % size) for j i...  5.56 us
    ppermute x16, starting transfers between devices, with_neighbour(): return own + [lax.ppermute(piece, 'axial', swap) for piece in own]  2.7 us
    ppermute x16, waiting for transfers between devices, with_neighbour(): return own + [lax.ppermute(piece, 'axial', swap) for piece in own]  2.54 us
    unnamed x17, local copies, waits for them, and re-layouts  2.37 us
  transfers between devices with their start and end apart: 46, of which 21 were waited for; matrix products, arithmetic and copies ran while one was open for 2% of the time, Pallas kernels for 12%

profile of v5, /device:TPU:0, one launch (start us, length us, event | category | flops | bytes accessed | tf_op | source)
XLA Modules:
  0.0 99.2 jit_solution(6463088856413641248)
XLA Ops:
  1.6 3.0 %collective-permute-start = (bf16[643,128]{1,0:T(8,128)(2,1)S(1)}, bf16[643,128]{1,0:T(8,128)(2,1)S(1)}, u32[]{:S(2)}, u32[]{:S(2)}) collective-permute-start(bf16[643,128]{1,0:T(8,128)(2,1)S(1)} %pad_maximum_fusion), channel_id=1, source_target_pairs={{16,0},{0,16},{17,1},{1,17},{18,2},{2,18},{19,3},{3,19},{20,4},{4,... | collective-permute-start | bytes 493832 | tf_op jit(solution)/shard_map/ppermute | solution.py:283
  5.7 2.7 %collective-permute-start.8 = (bf16[8,128,128]{2,1,0:T(8,128)(2,1)S(1)}, bf16[8,128,128]{2,1,0:T(8,128)(2,1)S(1)}, u32[]{:S(2)}, u32[]{:S(2)}) collective-permute-start(bf16[8,128,128]{2,1,0:T(8,128)(2,1)S(1)} %dynamic-slice_bitcast_fusion), channel_id=1, source_target_pairs={{0,8},{1,9},{2,10},{3,11},{4,12},{5,13},{6,14},{7,15},{8,0},{9,1},... | collective-permute-start | bytes 786440 | tf_op jit(solution)/shard_map/ppermute | solution.py:276
  9.2 1.6 %collective-permute-start.20 = (bf16[128,512]{0,1:T(8,128)(2,1)S(1)}, bf16[128,512]{0,1:T(8,128)(2,1)S(1)}, u32[]{:S(2)}, u32[]{:S(2)}) collective-permute-start(bf16[128,512]{0,1:T(8,128)(2,1)S(1)} %bitcast.45), channel_id=1, source_target_pairs={{16,0},{0,16},{17,1},{1,17},{18,2},{2,18},{19,3},{3,19},{20,4},{4,... | collective-permute-start | bytes 393224 | tf_op jit(solution)/shard_map/ppermute | solution.py:283
  12.4 1.7 %shard_map.73.pair = bf16[8,128,128]{2,1,0:T(8,128)(2,1)} custom-call(s32[1]{0:T(128)} %bitcast.3.index, bf16[4,8,128,128]{3,2,1,0:T(8,128)(2,1)} %source.1), custom_call_target="tpu_custom_call" | custom-call | tf_op jit(solution)/shard_map/pallas_call | solution.py:218
  16.6 1.6 %collective-permute-start.1 = (bf16[2,256,128]{2,1,0:T(8,128)(2,1)S(1)}, bf16[2,256,128]{2,1,0:T(8,128)(2,1)S(1)}, u32[]{:S(2)}, u32[]{:S(2)}) collective-permute-start(bf16[2,256,128]{2,1,0:T(8,128)(2,1)S(1)} %get-tuple-element.56), channel_id=1, source_target_pairs={{0,2},{1,3},{2,0},{3,1},{4,6},{5,7},{6,4},{7,5},{8,10},{9,11},{10,... | collective-permute-start | bytes 393224 | tf_op jit(solution)/shard_map/ppermute | solution.py:256
  18.2 1.8 %collective-permute-done.8.pair = bf16[8,128,128]{2,1,0:T(8,128)(2,1)S(1)} collective-permute-done((bf16[8,128,128]{2,1,0:T(8,128)(2,1)S(1)}, bf16[8,128,128]{2,1,0:T(8,128)(2,1)S(1)}, u32[]{:S(2)}, u32[]{:S(2)}) %collective-permute-start.8) | collective-permute-done | bytes 262176 | tf_op jit(solution)/shard_map/ppermute | solution.py:276
  22.0 2.4 %collective-permute-start.3 = (bf16[2,256,128]{2,1,0:T(8,128)(2,1)S(1)}, bf16[2,256,128]{2,1,0:T(8,128)(2,1)S(1)}, u32[]{:S(2)}, u32[]{:S(2)}) collective-permute-start(bf16[2,256,128]{2,1,0:T(8,128)(2,1)S(1)} %get-tuple-element.58), channel_id=1, source_target_pairs={{0,6},{1,7},{2,4},{3,5},{4,2},{5,3},{6,0},{7,1},{8,14},{9,15},{10,... | collective-permute-start | bytes 393224 | tf_op jit(solution)/shard_map/ppermute | solution.py:256
  25.8 2.3 %collective-permute-start.11 = (bf16[2,256,128]{2,1,0:T(8,128)(2,1)S(1)}, bf16[2,256,128]{2,1,0:T(8,128)(2,1)S(1)}, u32[]{:S(2)}, u32[]{:S(2)}) collective-permute-start(bf16[2,256,128]{2,1,0:T(8,128)(2,1)S(1)} %get-tuple-element.62), channel_id=1, source_target_pairs={{0,6},{1,7},{2,4},{3,5},{4,2},{5,3},{6,0},{7,1},{8,14},{9,15},{10,... | collective-permute-start | bytes 393224 | tf_op jit(solution)/shard_map/ppermute | solution.py:256
  29.4 2.9 %collective-permute-done.9.refs_9_ = bf16[2,256,128]{2,1,0:T(8,128)(2,1)S(1)} collective-permute-done((bf16[2,256,128]{2,1,0:T(8,128)(2,1)S(1)}, bf16[2,256,128]{2,1,0:T(8,128)(2,1)S(1)}, u32[]{:S(2)}, u32[]{:S(2)}) %collective-permute-start.9) | collective-permute-done | bytes 131104 | tf_op jit(solution)/shard_map/ppermute | solution.py:256
  32.8 1.7 %collective-permute-done.11.refs_11_ = bf16[2,256,128]{2,1,0:T(8,128)(2,1)S(1)} collective-permute-done((bf16[2,256,128]{2,1,0:T(8,128)(2,1)S(1)}, bf16[2,256,128]{2,1,0:T(8,128)(2,1)S(1)}, u32[]{:S(2)}, u32[]{:S(2)}) %collective-permute-start.11) | collective-permute-done | bytes 131104 | tf_op jit(solution)/shard_map/ppermute | solution.py:256
  36.3 1.5 %shard_map.76 = (bf16[256,128]{1,0:T(8,128)(2,1)S(1)}, bf16[256,128]{1,0:T(8,128)(2,1)S(1)}, bf16[256,128]{1,0:T(8,128)(2,1)S(1)}, bf16[256,128]{1,0:T(8,128)(2,...) custom-call(s32[3]{0:T(128)S(1)} %pad_add_fusion.here, ...), custom_call_target="tpu_custom_call" | custom-call | flops 67108864 | tf_op jit(solution)/shard_map/pallas_call | solution.py:235
  39.8 1.5 %collective-permute-start.18 = (bf16[256,128]{1,0:T(8,128)(2,1)S(1)}, bf16[256,128]{1,0:T(8,128)(2,1)S(1)}, u32[]{:S(2)}, u32[]{:S(2)}) collective-permute-start(bf16[256,128]{1,0:T(8,128)(2,1)S(1)} %get-tuple-element.66), channel_id=1, source_target_pairs={{0,6},{1,7},{2,4},{3,5},{4,2},{5,3},{6,0},{7,1},{8,14},{9,15},{10,... | collective-permute-start | bytes 196616 | tf_op jit(solution)/shard_map/ppermute | solution.py:256
  43.6 1.7 %collective-permute-done.18.refs_3_ = bf16[256,128]{1,0:T(8,128)(2,1)S(1)} collective-permute-done((bf16[256,128]{1,0:T(8,128)(2,1)S(1)}, bf16[256,128]{1,0:T(8,128)(2,1)S(1)}, u32[]{:S(2)}, u32[]{:S(2)}) %collective-permute-start.18) | collective-permute-done | bytes 65568 | tf_op jit(solution)/shard_map/ppermute | solution.py:256
  45.4 2.1 %shard_map.77 = (bf16[2,256,128]{2,1,0:T(8,128)(2,1)S(1)}, bf16[2,256,128]{2,1,0:T(8,128)(2,1)S(1)}, bf16[2,256,128]{2,1,0:T(8,128)(2,1)S(1)}, bf16[2,256,128]{2...) custom-call(s32[3]{0:T(128)S(1)} %pad_add_fusion.here, ...), custom_call_target="tpu_custom_call" | custom-call | flops 469762048 | tf_op jit(solution)/shard_map/pallas_call | solution.py:235
  47.6 1.4 %collective-permute-start.22 = (bf16[2,256,128]{2,1,0:T(8,128)(2,1)S(1)}, bf16[2,256,128]{2,1,0:T(8,128)(2,1)S(1)}, u32[]{:S(2)}, u32[]{:S(2)}) collective-permute-start(bf16[2,256,128]{2,1,0:T(8,128)(2,1)S(1)} %get-tuple-element.80), channel_id=1, source_target_pairs={{0,2},{1,3},{2,0},{3,1},{4,6},{5,7},{6,4},{7,5},{8,10},{9,11},{10,... | collective-permute-start | bytes 393224 | tf_op jit(solution)/shard_map/ppermute | solution.py:256
  51.1 1.7 %collective-permute-start.31 = (bf16[256,128]{1,0:T(8,128)(2,1)S(1)}, bf16[256,128]{1,0:T(8,128)(2,1)S(1)}, u32[]{:S(2)}, u32[]{:S(2)}) collective-permute-start(bf16[256,128]{1,0:T(8,128)(2,1)S(1)} %get-tuple-element.86), channel_id=1, source_target_pairs={{0,6},{1,7},{2,4},{3,5},{4,2},{5,3},{6,0},{7,1},{8,14},{9,15},{10,... | collective-permute-start | bytes 196616 | tf_op jit(solution)/shard_map/ppermute | solution.py:256
  52.8 4.7 %collective-permute-done.31.refs_3_ = bf16[256,128]{1,0:T(8,128)(2,1)S(1)} collective-permute-done((bf16[256,128]{1,0:T(8,128)(2,1)S(1)}, bf16[256,128]{1,0:T(8,128)(2,1)S(1)}, u32[]{:S(2)}, u32[]{:S(2)}) %collective-permute-start.31) | collective-permute-done | bytes 65568 | tf_op jit(solution)/shard_map/ppermute | solution.py:256
  57.6 2.1 %shard_map.78 = (bf16[2,256,128]{2,1,0:T(8,128)(2,1)S(1)}, bf16[2,256,128]{2,1,0:T(8,128)(2,1)S(1)}, bf16[2,256,128]{2,1,0:T(8,128)(2,1)S(1)}, bf16[2,256,128]{2...) custom-call(s32[3]{0:T(128)S(1)} %pad_add_fusion.here, ...), custom_call_target="tpu_custom_call" | custom-call | flops 469762048 | tf_op jit(solution)/shard_map/pallas_call | solution.py:235
  61.6 1.6 %collective-permute-start.34 = (bf16[2,256,128]{2,1,0:T(8,128)(2,1)S(1)}, bf16[2,256,128]{2,1,0:T(8,128)(2,1)S(1)}, u32[]{:S(2)}, u32[]{:S(2)}) collective-permute-start(bf16[2,256,128]{2,1,0:T(8,128)(2,1)S(1)} %get-tuple-element.92), channel_id=1, source_target_pairs={{0,6},{1,7},{2,4},{3,5},{4,2},{5,3},{6,0},{7,1},{8,14},{9,15},{10,... | collective-permute-start | bytes 393224 | tf_op jit(solution)/shard_map/ppermute | solution.py:256
  63.8 2.4 %collective-permute-done.32.refs_9_ = bf16[2,256,128]{2,1,0:T(8,128)(2,1)S(1)} collective-permute-done((bf16[2,256,128]{2,1,0:T(8,128)(2,1)S(1)}, bf16[2,256,128]{2,1,0:T(8,128)(2,1)S(1)}, u32[]{:S(2)}, u32[]{:S(2)}) %collective-permute-start.32) | collective-permute-done | bytes 131104 | tf_op jit(solution)/shard_map/ppermute | solution.py:256
  66.7 1.5 %collective-permute-done.34.refs_11_ = bf16[2,256,128]{2,1,0:T(8,128)(2,1)S(1)} collective-permute-done((bf16[2,256,128]{2,1,0:T(8,128)(2,1)S(1)}, bf16[2,256,128]{2,1,0:T(8,128)(2,1)S(1)}, u32[]{:S(2)}, u32[]{:S(2)}) %collective-permute-start.34) | collective-permute-done | bytes 131104 | tf_op jit(solution)/shard_map/ppermute | solution.py:256
  70.1 1.3 %shard_map.81 = (bf16[256,128]{1,0:T(8,128)(2,1)S(1)}, bf16[256,128]{1,0:T(8,128)(2,1)S(1)}, bf16[256,128]{1,0:T(8,128)(2,1)S(1)}, bf16[256,128]{1,0:T(8,128)(2,1)S(1)}) custom-call(s32[3]{0:T(128)S(1)} %pad_add_fusion.here, bf16[2,256,128]{2,1,0:T(8,128)(2,1)S(1)} %get-tuple-element.79.refs_0_, bf16[2,256,128]{2,1,0:T(8,128)(2,1)S(1)} %collective-permute-done.22.refs_1_, ...), custom_call_target="tpu_custom_call" | custom-call | flops 33554432 | tf_op jit(solution)/shard_map/pallas_call | solution.py:235
  71.4 1.4 %collective-permute-start.42 = (bf16[256,128]{1,0:T(8,128)(2,1)S(1)}, bf16[256,128]{1,0:T(8,128)(2,1)S(1)}, u32[]{:S(2)}, u32[]{:S(2)}) collective-permute-start(bf16[256,128]{1,0:T(8,128)(2,1)S(1)} %get-tuple-element.100), channel_id=1, source_target_pairs={{0,2},{1,3},{2,0},{3,1},{4,6},{5,7},{6,4},{7,5},{8,10},{9,11},{10,... | collective-permute-start | bytes 196616 | tf_op jit(solution)/shard_map/ppermute | solution.py:256
  75.7 2.0 %collective-permute-done.43.refs_2_ = bf16[256,128]{1,0:T(8,128)(2,1)S(1)} collective-permute-done((bf16[256,128]{1,0:T(8,128)(2,1)S(1)}, bf16[256,128]{1,0:T(8,128)(2,1)S(1)}, u32[]{:S(2)}, u32[]{:S(2)}) %collective-permute-start.43) | collective-permute-done | bytes 65568 | tf_op jit(solution)/shard_map/ppermute | solution.py:256
  78.9 1.6 %shard_map.82 = bf16[1,8,128,128]{3,2,1,0:T(8,128)(2,1)S(1)} custom-call(s32[3]{0:T(128)S(1)} %pad_add_fusion.here, bf16[256,128]{1,0:T(8,128)(2,1)S(1)} %get-tuple-element.99.refs_0_, bf16[256,128]{1,0:T(8,128)(2,1)S(1)} %collective-permute-done.42.refs_1_, bf16[256,128]{1,0:T(8,128)(2,1)S(1)} %collective-permute-done.43.refs_2_, ...), custom_call_target="tpu_custom_call" | custom-call | flops 301989888 | tf_op jit(solution)/shard_map/pallas_call | solution.py:235
  80.5 2.9 %collective-permute-start.45 = (bf16[1,8,128,128]{3,2,1,0:T(8,128)(2,1)S(1)}, bf16[1,8,128,128]{3,2,1,0:T(8,128)(2,1)S(1)}, u32[]{:S(2)}, u32[]{:S(2)}) collective-permute-start(bf16[1,8,128,128]{3,2,1,0:T(8,128)(2,1)S(1)} %shard_map.82), channel_id=1, source_target_pairs={{0,8},{1,9},{2,10},{3,11},{4,12},{5,13},{6,14},{7,15},{8,0},{9,1},... | collective-permute-start | bytes 786440 | tf_op jit(solution)/shard_map/ppermute | solution.py:276
  83.4 1.3 %shard_map.79 = (bf16[256,128]{1,0:T(8,128)(2,1)S(1)}, bf16[256,128]{1,0:T(8,128)(2,1)S(1)}, bf16[256,128]{1,0:T(8,128)(2,1)S(1)}, bf16[256,128]{1,0:T(8,128)(2,1)S(1)}) custom-call(s32[3]{0:T(128)S(1)} %pad_add_fusion.here, bf16[2,256,128]{2,1,0:T(8,128)(2,1)S(1)} %get-tuple-element.79.refs_0_, bf16[2,256,128]{2,1,0:T(8,128)(2,1)S(1)} %collective-permute-done.22.refs_1_, ...), custom_call_target="tpu_custom_call" | custom-call | flops 33554432 | tf_op jit(solution)/shard_map/pallas_call | solution.py:235
  84.7 1.6 %collective-permute-start.39 = (bf16[256,128]{1,0:T(8,128)(2,1)S(1)}, bf16[256,128]{1,0:T(8,128)(2,1)S(1)}, u32[]{:S(2)}, u32[]{:S(2)}) collective-permute-start(bf16[256,128]{1,0:T(8,128)(2,1)S(1)} %get-tuple-element.94), channel_id=1, source_target_pairs={{0,2},{1,3},{2,0},{3,1},{4,6},{5,7},{6,4},{7,5},{8,10},{9,11},{10,... | collective-permute-start | bytes 196616 | tf_op jit(solution)/shard_map/ppermute | solution.py:256
  88.3 1.4 %collective-permute-done.39.refs_1_ = bf16[256,128]{1,0:T(8,128)(2,1)S(1)} collective-permute-done((bf16[256,128]{1,0:T(8,128)(2,1)S(1)}, bf16[256,128]{1,0:T(8,128)(2,1)S(1)}, u32[]{:S(2)}, u32[]{:S(2)}) %collective-permute-start.39) | collective-permute-done | bytes 65568 | tf_op jit(solution)/shard_map/ppermute | solution.py:256
  89.6 1.5 %collective-permute-done.40.refs_2_ = bf16[256,128]{1,0:T(8,128)(2,1)S(1)} collective-permute-done((bf16[256,128]{1,0:T(8,128)(2,1)S(1)}, bf16[256,128]{1,0:T(8,128)(2,1)S(1)}, u32[]{:S(2)}, u32[]{:S(2)}) %collective-permute-start.40) | collective-permute-done | bytes 65568 | tf_op jit(solution)/shard_map/ppermute | solution.py:256
  91.1 5.0 %collective-permute-done.41.refs_3_ = bf16[256,128]{1,0:T(8,128)(2,1)S(1)} collective-permute-done((bf16[256,128]{1,0:T(8,128)(2,1)S(1)}, bf16[256,128]{1,0:T(8,128)(2,1)S(1)}, u32[]{:S(2)}, u32[]{:S(2)}) %collective-permute-start.41) | collective-permute-done | bytes 65568 | tf_op jit(solution)/shard_map/ppermute | solution.py:256
  96.1 2.4 %shard_map.80 = bf16[2,8,128,128]{3,2,1,0:T(8,128)(2,1)} custom-call(s32[3]{0:T(128)S(1)} %pad_add_fusion.here, bf16[256,128]{1,0:T(8,128)(2,1)S(1)} %get-tuple-element.93.refs_0_, bf16[256,128]{1,0:T(8,128)(2,1)S(1)} %collective-permute-done.39.refs_1_, bf16[256,128]{1,0:T(8,128)(2,1)S(1)} %collective-permute-done.40.refs_2_, ...), custom_call_target="tpu_custom_call" | custom-call | flops 301989888 | tf_op jit(solution)/shard_map/pallas_call | solution.py:235
  (108 shorter events, 32.4 us)
Async XLA Ops:
  1.6 12.6 %collective-permute-start = (bf16[643,128]{1,0:T(8,128)(2,1)S(1)}, bf16[643,128]{1,0:T(8,128)(2,1)S(1)}, u32[]{:S(2)}, u32[]{:S(2)}) collective-permute-start(bf16[643,128]{1,0:T(8,128)(2,1)S(1)} %pad_maximum_fusion), channel_id=1, source_target_pairs={{16,0},{0,16},{17,1},{1,17},{18,2},{2,18},{19,3},{3,19},{20,4},{4,... | collective-permute-start | bytes 493832 | tf_op jit(solution)/shard_map/ppermute | solution.py:283
  5.7 14.3 %collective-permute-start.8 = (bf16[8,128,128]{2,1,0:T(8,128)(2,1)S(1)}, bf16[8,128,128]{2,1,0:T(8,128)(2,1)S(1)}, u32[]{:S(2)}, u32[]{:S(2)}) collective-permute-start(bf16[8,128,128]{2,1,0:T(8,128)(2,1)S(1)} %dynamic-slice_bitcast_fusion), channel_id=1, source_target_pairs={{0,8},{1,9},{2,10},{3,11},{4,12},{5,13},{6,14},{7,15},{8,0},{9,1},... | collective-permute-start | bytes 786440 | tf_op jit(solution)/shard_map/ppermute | solution.py:276
  8.4 13.5 %collective-permute-start.19 = (bf16[128,128]{0,1:T(8,128)(2,1)S(1)}, bf16[128,128]{0,1:T(8,128)(2,1)S(1)}, u32[]{:S(2)}, u32[]{:S(2)}) collective-permute-start(bf16[128,128]{0,1:T(8,128)(2,1)S(1)} %bitcast.49), channel_id=1, source_target_pairs={{16,0},{0,16},{17,1},{1,17},{18,2},{2,18},{19,3},{3,19},{20,4},{4,... | collective-permute-start | bytes 98312 | tf_op jit(solution)/shard_map/ppermute | solution.py:283
  9.2 15.2 %collective-permute-start.20 = (bf16[128,512]{0,1:T(8,128)(2,1)S(1)}, bf16[128,512]{0,1:T(8,128)(2,1)S(1)}, u32[]{:S(2)}, u32[]{:S(2)}) collective-permute-start(bf16[128,512]{0,1:T(8,128)(2,1)S(1)} %bitcast.45), channel_id=1, source_target_pairs={{16,0},{0,16},{17,1},{1,17},{18,2},{2,18},{19,3},{3,19},{20,4},{4,... | collective-permute-start | bytes 393224 | tf_op jit(solution)/shard_map/ppermute | solution.py:283
  10.8 13.5 %collective-permute-start.21 = (bf16[512,128]{0,1:T(8,128)(2,1)S(1)}, bf16[512,128]{0,1:T(8,128)(2,1)S(1)}, u32[]{:S(2)}, u32[]{:S(2)}) collective-permute-start(bf16[512,128]{0,1:T(8,128)(2,1)S(1)} %bitcast.47), channel_id=1, source_target_pairs={{16,0},{0,16},{17,1},{1,17},{18,2},{2,18},{19,3},{3,19},{20,4},{4,... | collective-permute-start | bytes 393224 | tf_op jit(solution)/shard_map/ppermute | solution.py:283
  16.6 8.5 %collective-permute-start.1 = (bf16[2,256,128]{2,1,0:T(8,128)(2,1)S(1)}, bf16[2,256,128]{2,1,0:T(8,128)(2,1)S(1)}, u32[]{:S(2)}, u32[]{:S(2)}) collective-permute-start(bf16[2,256,128]{2,1,0:T(8,128)(2,1)S(1)} %get-tuple-element.56), channel_id=1, source_target_pairs={{0,2},{1,3},{2,0},{3,1},{4,6},{5,7},{6,4},{7,5},{8,10},{9,11},{10,... | collective-permute-start | bytes 393224 | tf_op jit(solution)/shard_map/ppermute | solution.py:256
  20.0 5.8 %collective-permute-start.2 = (bf16[2,256,128]{2,1,0:T(8,128)(2,1)S(1)}, bf16[2,256,128]{2,1,0:T(8,128)(2,1)S(1)}, u32[]{:S(2)}, u32[]{:S(2)}) collective-permute-start(bf16[2,256,128]{2,1,0:T(8,128)(2,1)S(1)} %get-tuple-element.57), channel_id=1, source_target_pairs={{0,4},{1,5},{2,6},{3,7},{4,0},{5,1},{6,2},{7,3},{8,12},{9,13},{10,... | collective-permute-start | bytes 393224 | tf_op jit(solution)/shard_map/ppermute | solution.py:256
  22.0 6.8 %collective-permute-start.3 = (bf16[2,256,128]{2,1,0:T(8,128)(2,1)S(1)}, bf16[2,256,128]{2,1,0:T(8,128)(2,1)S(1)}, u32[]{:S(2)}, u32[]{:S(2)}) collective-permute-start(bf16[2,256,128]{2,1,0:T(8,128)(2,1)S(1)} %get-tuple-element.58), channel_id=1, source_target_pairs={{0,6},{1,7},{2,4},{3,5},{4,2},{5,3},{6,0},{7,1},{8,14},{9,15},{10,... | collective-permute-start | bytes 393224 | tf_op jit(solution)/shard_map/ppermute | solution.py:256
  24.4 7.9 %collective-permute-start.9 = (bf16[2,256,128]{2,1,0:T(8,128)(2,1)S(1)}, bf16[2,256,128]{2,1,0:T(8,128)(2,1)S(1)}, u32[]{:S(2)}, u32[]{:S(2)}) collective-permute-start(bf16[2,256,128]{2,1,0:T(8,128)(2,1)S(1)} %get-tuple-element.60), channel_id=1, source_target_pairs={{0,2},{1,3},{2,0},{3,1},{4,6},{5,7},{6,4},{7,5},{8,10},{9,11},{10,... | collective-permute-start | bytes 393224 | tf_op jit(solution)/shard_map/ppermute | solution.py:256
  25.1 7.2 %collective-permute-start.10 = (bf16[2,256,128]{2,1,0:T(8,128)(2,1)S(1)}, bf16[2,256,128]{2,1,0:T(8,128)(2,1)S(1)}, u32[]{:S(2)}, u32[]{:S(2)}) collective-permute-start(bf16[2,256,128]{2,1,0:T(8,128)(2,1)S(1)} %get-tuple-element.61), channel_id=1, source_target_pairs={{0,4},{1,5},{2,6},{3,7},{4,0},{5,1},{6,2},{7,3},{8,12},{9,13},{10,... | collective-permute-start | bytes 393224 | tf_op jit(solution)/shard_map/ppermute | solution.py:256
  25.8 8.7 %collective-permute-start.11 = (bf16[2,256,128]{2,1,0:T(8,128)(2,1)S(1)}, bf16[2,256,128]{2,1,0:T(8,128)(2,1)S(1)}, u32[]{:S(2)}, u32[]{:S(2)}) collective-permute-start(bf16[2,256,128]{2,1,0:T(8,128)(2,1)S(1)} %get-tuple-element.62), channel_id=1, source_target_pairs={{0,6},{1,7},{2,4},{3,5},{4,2},{5,3},{6,0},{7,1},{8,14},{9,15},{10,... | collective-permute-start | bytes 393224 | tf_op jit(solution)/shard_map/ppermute | solution.py:256
  28.8 5.6 %collective-permute-start.12 = (bf16[2,256,128]{2,1,0:T(8,128)(2,1)S(1)}, bf16[2,256,128]{2,1,0:T(8,128)(2,1)S(1)}, u32[]{:S(2)}, u32[]{:S(2)}) collective-permute-start(bf16[2,256,128]{2,1,0:T(8,128)(2,1)S(1)} %get-tuple-element.59.refs_8_), channel_id=1, source_target_pairs={{0,1},{1,0},{2,3},{3,2},{4,5},{5,4},{6,7},{7,6},{8,9},{9,8},{10,11... | collective-permute-start | bytes 393224 | tf_op jit(solution)/shard_map/ppermute | solution.py:265
  28.8 6.1 %collective-permute-start.5 = (bf16[2,256,128]{2,1,0:T(8,128)(2,1)S(1)}, bf16[2,256,128]{2,1,0:T(8,128)(2,1)S(1)}, u32[]{:S(2)}, u32[]{:S(2)}) collective-permute-start(bf16[2,256,128]{2,1,0:T(8,128)(2,1)S(1)} %collective-permute-done.1.refs_1_), channel_id=1, source_target_pairs={{0,1},{1,0},{2,3},{3,2},{4,5},{5,4},{6,7},{7,6},{8,9},{9,8},{10,11... | collective-permute-start | bytes 393224 | tf_op jit(solution)/shard_map/ppermute | solution.py:265
  37.8 5.7 %collective-permute-start.16 = (bf16[256,128]{1,0:T(8,128)(2,1)S(1)}, bf16[256,128]{1,0:T(8,128)(2,1)S(1)}, u32[]{:S(2)}, u32[]{:S(2)}) collective-permute-start(bf16[256,128]{1,0:T(8,128)(2,1)S(1)} %get-tuple-element.64), channel_id=1, source_target_pairs={{0,2},{1,3},{2,0},{3,1},{4,6},{5,7},{6,4},{7,5},{8,10},{9,11},{10,... | collective-permute-start | bytes 196616 | tf_op jit(solution)/shard_map/ppermute | solution.py:256
  38.7 4.9 %collective-permute-start.17 = (bf16[256,128]{1,0:T(8,128)(2,1)S(1)}, bf16[256,128]{1,0:T(8,128)(2,1)S(1)}, u32[]{:S(2)}, u32[]{:S(2)}) collective-permute-start(bf16[256,128]{1,0:T(8,128)(2,1)S(1)} %get-tuple-element.65), channel_id=1, source_target_pairs={{0,4},{1,5},{2,6},{3,7},{4,0},{5,1},{6,2},{7,3},{8,12},{9,13},{10,... | collective-permute-start | bytes 196616 | tf_op jit(solution)/shard_map/ppermute | solution.py:256
  39.8 5.5 %collective-permute-start.18 = (bf16[256,128]{1,0:T(8,128)(2,1)S(1)}, bf16[256,128]{1,0:T(8,128)(2,1)S(1)}, u32[]{:S(2)}, u32[]{:S(2)}) collective-permute-start(bf16[256,128]{1,0:T(8,128)(2,1)S(1)} %get-tuple-element.66), channel_id=1, source_target_pairs={{0,6},{1,7},{2,4},{3,5},{4,2},{5,3},{6,0},{7,1},{8,14},{9,15},{10,... | collective-permute-start | bytes 196616 | tf_op jit(solution)/shard_map/ppermute | solution.py:256
  41.4 9.7 %collective-permute-start.29 = (bf16[256,128]{1,0:T(8,128)(2,1)S(1)}, bf16[256,128]{1,0:T(8,128)(2,1)S(1)}, u32[]{:S(2)}, u32[]{:S(2)}) collective-permute-start(bf16[256,128]{1,0:T(8,128)(2,1)S(1)} %get-tuple-element.84), channel_id=1, source_target_pairs={{0,2},{1,3},{2,0},{3,1},{4,6},{5,7},{6,4},{7,5},{8,10},{9,11},{10,... | collective-permute-start | bytes 196616 | tf_op jit(solution)/shard_map/ppermute | solution.py:256
  42.3 8.8 %collective-permute-start.30 = (bf16[256,128]{1,0:T(8,128)(2,1)S(1)}, bf16[256,128]{1,0:T(8,128)(2,1)S(1)}, u32[]{:S(2)}, u32[]{:S(2)}) collective-permute-start(bf16[256,128]{1,0:T(8,128)(2,1)S(1)} %get-tuple-element.85), channel_id=1, source_target_pairs={{0,4},{1,5},{2,6},{3,7},{4,0},{5,1},{6,2},{7,3},{8,12},{9,13},{10,... | collective-permute-start | bytes 196616 | tf_op jit(solution)/shard_map/ppermute | solution.py:256
  47.6 12.9 %collective-permute-start.22 = (bf16[2,256,128]{2,1,0:T(8,128)(2,1)S(1)}, bf16[2,256,128]{2,1,0:T(8,128)(2,1)S(1)}, u32[]{:S(2)}, u32[]{:S(2)}) collective-permute-start(bf16[2,256,128]{2,1,0:T(8,128)(2,1)S(1)} %get-tuple-element.80), channel_id=1, source_target_pairs={{0,2},{1,3},{2,0},{3,1},{4,6},{5,7},{6,4},{7,5},{8,10},{9,11},{10,... | collective-permute-start | bytes 393224 | tf_op jit(solution)/shard_map/ppermute | solution.py:256
  49.0 12.6 %collective-permute-start.23 = (bf16[2,256,128]{2,1,0:T(8,128)(2,1)S(1)}, bf16[2,256,128]{2,1,0:T(8,128)(2,1)S(1)}, u32[]{:S(2)}, u32[]{:S(2)}) collective-permute-start(bf16[2,256,128]{2,1,0:T(8,128)(2,1)S(1)} %get-tuple-element.81), channel_id=1, source_target_pairs={{0,4},{1,5},{2,6},{3,7},{4,0},{5,1},{6,2},{7,3},{8,12},{9,13},{10,... | collective-permute-start | bytes 393224 | tf_op jit(solution)/shard_map/ppermute | solution.py:256
  49.8 13.4 %collective-permute-start.24 = (bf16[2,256,128]{2,1,0:T(8,128)(2,1)S(1)}, bf16[2,256,128]{2,1,0:T(8,128)(2,1)S(1)}, u32[]{:S(2)}, u32[]{:S(2)}) collective-permute-start(bf16[2,256,128]{2,1,0:T(8,128)(2,1)S(1)} %get-tuple-element.82), channel_id=1, source_target_pairs={{0,6},{1,7},{2,4},{3,5},{4,2},{5,3},{6,0},{7,1},{8,14},{9,15},{10,... | collective-permute-start | bytes 393224 | tf_op jit(solution)/shard_map/ppermute | solution.py:256
  51.1 12.1 %collective-permute-start.25 = (bf16[2,256,128]{2,1,0:T(8,128)(2,1)S(1)}, bf16[2,256,128]{2,1,0:T(8,128)(2,1)S(1)}, u32[]{:S(2)}, u32[]{:S(2)}) collective-permute-start(bf16[2,256,128]{2,1,0:T(8,128)(2,1)S(1)} %get-tuple-element.79.refs_0_), channel_id=1, source_target_pairs={{0,1},{1,0},{2,3},{3,2},{4,5},{5,4},{6,7},{7,6},{8,9},{9,8},{10,11... | collective-permute-start | bytes 393224 | tf_op jit(solution)/shard_map/ppermute | solution.py:265
  51.1 6.4 %collective-permute-start.31 = (bf16[256,128]{1,0:T(8,128)(2,1)S(1)}, bf16[256,128]{1,0:T(8,128)(2,1)S(1)}, u32[]{:S(2)}, u32[]{:S(2)}) collective-permute-start(bf16[256,128]{1,0:T(8,128)(2,1)S(1)} %get-tuple-element.86), channel_id=1, source_target_pairs={{0,6},{1,7},{2,4},{3,5},{4,2},{5,3},{6,0},{7,1},{8,14},{9,15},{10,... | collective-permute-start | bytes 196616 | tf_op jit(solution)/shard_map/ppermute | solution.py:256
  59.7 6.4 %collective-permute-start.32 = (bf16[2,256,128]{2,1,0:T(8,128)(2,1)S(1)}, bf16[2,256,128]{2,1,0:T(8,128)(2,1)S(1)}, u32[]{:S(2)}, u32[]{:S(2)}) collective-permute-start(bf16[2,256,128]{2,1,0:T(8,128)(2,1)S(1)} %get-tuple-element.90), channel_id=1, source_target_pairs={{0,2},{1,3},{2,0},{3,1},{4,6},{5,7},{6,4},{7,5},{8,10},{9,11},{10,... | collective-permute-start | bytes 393224 | tf_op jit(solution)/shard_map/ppermute | solution.py:256
  60.4 6.3 %collective-permute-start.33 = (bf16[2,256,128]{2,1,0:T(8,128)(2,1)S(1)}, bf16[2,256,128]{2,1,0:T(8,128)(2,1)S(1)}, u32[]{:S(2)}, u32[]{:S(2)}) collective-permute-start(bf16[2,256,128]{2,1,0:T(8,128)(2,1)S(1)} %get-tuple-element.91), channel_id=1, source_target_pairs={{0,4},{1,5},{2,6},{3,7},{4,0},{5,1},{6,2},{7,3},{8,12},{9,13},{10,... | collective-permute-start | bytes 393224 | tf_op jit(solution)/shard_map/ppermute | solution.py:256
  61.6 6.6 %collective-permute-start.34 = (bf16[2,256,128]{2,1,0:T(8,128)(2,1)S(1)}, bf16[2,256,128]{2,1,0:T(8,128)(2,1)S(1)}, u32[]{:S(2)}, u32[]{:S(2)}) collective-permute-start(bf16[2,256,128]{2,1,0:T(8,128)(2,1)S(1)} %get-tuple-element.92), channel_id=1, source_target_pairs={{0,6},{1,7},{2,4},{3,5},{4,2},{5,3},{6,0},{7,1},{8,14},{9,15},{10,... | collective-permute-start | bytes 393224 | tf_op jit(solution)/shard_map/ppermute | solution.py:256
  63.3 5.0 %collective-permute-start.35 = (bf16[2,256,128]{2,1,0:T(8,128)(2,1)S(1)}, bf16[2,256,128]{2,1,0:T(8,128)(2,1)S(1)}, u32[]{:S(2)}, u32[]{:S(2)}) collective-permute-start(bf16[2,256,128]{2,1,0:T(8,128)(2,1)S(1)} %get-tuple-element.89.refs_8_), channel_id=1, source_target_pairs={{0,1},{1,0},{2,3},{3,2},{4,5},{5,4},{6,7},{7,6},{8,9},{9,8},{10,11... | collective-permute-start | bytes 393224 | tf_op jit(solution)/shard_map/ppermute | solution.py:265
  63.3 5.5 %collective-permute-start.26 = (bf16[2,256,128]{2,1,0:T(8,128)(2,1)S(1)}, bf16[2,256,128]{2,1,0:T(8,128)(2,1)S(1)}, u32[]{:S(2)}, u32[]{:S(2)}) collective-permute-start(bf16[2,256,128]{2,1,0:T(8,128)(2,1)S(1)} %collective-permute-done.22.refs_1_), channel_id=1, source_target_pairs={{0,1},{1,0},{2,3},{3,2},{4,5},{5,4},{6,7},{7,6},{8,9},{9,8},{10,11... | collective-permute-start | bytes 393224 | tf_op jit(solution)/shard_map/ppermute | solution.py:265
  73.7 5.2 %collective-permute-start.44 = (bf16[256,128]{1,0:T(8,128)(2,1)S(1)}, bf16[256,128]{1,0:T(8,128)(2,1)S(1)}, u32[]{:S(2)}, u32[]{:S(2)}) collective-permute-start(bf16[256,128]{1,0:T(8,128)(2,1)S(1)} %get-tuple-element.102), channel_id=1, source_target_pairs={{0,6},{1,7},{2,4},{3,5},{4,2},{5,3},{6,0},{7,1},{8,14},{9,15},{10,... | collective-permute-start | bytes 196616 | tf_op jit(solution)/shard_map/ppermute | solution.py:256
  80.5 18.0 %collective-permute-start.45 = (bf16[1,8,128,128]{3,2,1,0:T(8,128)(2,1)S(1)}, bf16[1,8,128,128]{3,2,1,0:T(8,128)(2,1)S(1)}, u32[]{:S(2)}, u32[]{:S(2)}) collective-permute-start(bf16[1,8,128,128]{3,2,1,0:T(8,128)(2,1)S(1)} %shard_map.82), channel_id=1, source_target_pairs={{0,8},{1,9},{2,10},{3,11},{4,12},{5,13},{6,14},{7,15},{8,0},{9,1},... | collective-permute-start | bytes 786440 | tf_op jit(solution)/shard_map/ppermute | solution.py:276
  84.7 4.9 %collective-permute-start.39 = (bf16[256,128]{1,0:T(8,128)(2,1)S(1)}, bf16[256,128]{1,0:T(8,128)(2,1)S(1)}, u32[]{:S(2)}, u32[]{:S(2)}) collective-permute-start(bf16[256,128]{1,0:T(8,128)(2,1)S(1)} %get-tuple-element.94), channel_id=1, source_target_pairs={{0,2},{1,3},{2,0},{3,1},{4,6},{5,7},{6,4},{7,5},{8,10},{9,11},{10,... | collective-permute-start | bytes 196616 | tf_op jit(solution)/shard_map/ppermute | solution.py:256
  86.9 9.1 %collective-permute-start.41 = (bf16[256,128]{1,0:T(8,128)(2,1)S(1)}, bf16[256,128]{1,0:T(8,128)(2,1)S(1)}, u32[]{:S(2)}, u32[]{:S(2)}) collective-permute-start(bf16[256,128]{1,0:T(8,128)(2,1)S(1)} %get-tuple-element.96), channel_id=1, source_target_pairs={{0,6},{1,7},{2,4},{3,5},{4,2},{5,3},{6,0},{7,1},{8,14},{9,15},{10,... | collective-permute-start | bytes 196616 | tf_op jit(solution)/shard_map/ppermute | solution.py:256
  (21 other events, 51.8 us)

commit v6 on v4

--- a/solution.py
+++ b/solution.py
@@ -304,9 +304,7 @@
     heads = from_sections(
         jnp.concatenate((proj_weights[0].reshape(-1, channels), norm_gains[0])), sections
     )
-    others = from_sections(
-        jnp.concatenate((out_weights[0].T, up_weights[0].T, down_weights[0])), sections
-    )
+    others = [from_sections(w[0], sections) for w in (out_weights, up_weights, down_weights)]
     kinds = proj_weights.shape[1]
 
     def head_of(slots, layer):
@@ -355,17 +353,14 @@
         proj, gain = head_of(heads, layer)
         projs.append(proj)
         gains.append(gain)
-    bodies = by_layer(others, section)
-    outs = [w[:channels] for w in bodies]
-    ups = [w[channels : channels + hidden] for w in bodies]
-    downs = [w[channels + hidden :].T for w in bodies]
+    outs, ups, downs = [[w.T for w in by_layer(slots, section)] for slots in others]
     finished = [None] * parts
     for layer in range(sections):
         edges = [with_neighbour(edges[k]) for k in range(parts)]
         last = layer == sections - 1
         order = range(parts - 1, -1, -1) if last else range(parts)
         tri = {}
-        for taken in [(k,) for k in order] if last else [tuple(order)]:
+        for taken in [tuple(order)]:
             sides = [(n * half, block, columns) for n in (len(taken), 2 * parts, len(taken))]
             products = call(
                 functools.partial(triangle_kernel, half, parts, taken),

time: 103 us -> 95.7 us (0.929)
  local copies, waits for them, and re-layouts: 10.1 us -> 4.17 us
  starting transfers between devices: 39.9 us -> 43.7 us
  Pallas kernels: 16.8 us -> 13.9 us
  waiting for transfers between devices: 33.2 us -> 32.1 us
    pallas_call x9 -> x8, Pallas kernels: 16.8 us -> 13.9 us  [pallas(): pl.pallas_call(kernel, out_shape=[jax.ShapeDtypeStruct(shape, dtype) for...]
    unnamed x23 -> x15, local copies, waits for them, and re-layouts: 4.6 us -> 1.72 us
    ppermute x2 -> x4, starting transfers between devices: 3.63 us -> 5.79 us  [from_sections(): lax.ppermute(weight, 'section', [((i + shift) % sections, i) for i in ran...]
    ppermute x24, waiting for transfers between devices: 25.9 us -> 24.4 us  [exchange(): lax.ppermute(blocks[i], 'axial', [(j, j ^ 2 * i) for j in range(size)])]
    ppermute x24, starting transfers between devices: 28.3 us -> 29.7 us  [exchange(): lax.ppermute(blocks[i], 'axial', [(j, j ^ 2 * i) for j in range(size)])]
    slice x6 -> x0, local copies, waits for them, and re-layouts: 1.39 us -> none  [the longest x2 1.16 us: per_device(): ups = [w[channels:channels + hidden] for w in bodies]]
  transfers between devices with their start and end apart: 44 -> 46, of which waited for: 20 -> 22; matrix products, arithmetic and copies ran while one was open for 5% -> 3% of each run, Pallas kernels for 10% -> 10%
where the time goes in v6:
time: 95.7 us; the launch traced here: 95.5 us
  starting transfers between devices  43.7 us (46%)
  waiting for transfers between devices  32.1 us (34%)
  Pallas kernels  13.9 us (15%)
  local copies, waits for them, and re-layouts  4.17 us (4%)
  other arithmetic  1.29 us (1%)
    ppermute x24, starting transfers between devices, exchange(): lax.ppermute(blocks[i], 'axial', [(j, j ^ 2 * i) for j in range(size)])  29.7 us
    ppermute x24, waiting for transfers between devices, exchange(): lax.ppermute(blocks[i], 'axial', [(j, j ^ 2 * i) for j in range(size)])  24.4 us
    pallas_call x8, Pallas kernels, pallas(): pl.pallas_call(kernel, out_shape=[jax.ShapeDtypeStruct(shape, dtype) for...  13.9 us
    ppermute x4, starting transfers between devices, from_sections(): lax.ppermute(weight, 'section', [((i + shift) % sections, i) for i in ran...  5.79 us
    ppermute x2, starting transfers between devices, move_parts(): lax.ppermute(values, 'axial', [(j, (j + distance * width) % size) for j i...  5.56 us
    ppermute x2, waiting for transfers between devices, move_parts(): lax.ppermute(values, 'axial', [(j, (j + distance * width) % size) for j i...  5.18 us
    ppermute x16, starting transfers between devices, with_neighbour(): return own + [lax.ppermute(piece, 'axial', swap) for piece in own]  2.7 us
    ppermute x16, waiting for transfers between devices, with_neighbour(): return own + [lax.ppermute(piece, 'axial', swap) for piece in own]  2.54 us
  transfers between devices with their start and end apart: 46, of which 22 were waited for; matrix products, arithmetic and copies ran while one was open for 3% of the time, Pallas kernels for 10%

profile of v6, /device:TPU:0, one launch (start us, length us, event | category | flops | bytes accessed | tf_op | source)
XLA Modules:
  0.0 95.5 jit_solution(15217652372530976377)
XLA Ops:
  1.6 3.0 %collective-permute-start = (bf16[643,128]{1,0:T(8,128)(2,1)S(1)}, bf16[643,128]{1,0:T(8,128)(2,1)S(1)}, u32[]{:S(2)}, u32[]{:S(2)}) collective-permute-start(bf16[643,128]{1,0:T(8,128)(2,1)S(1)} %pad_maximum_fusion), channel_id=1, source_target_pairs={{16,0},{0,16},{17,1},{1,17},{18,2},{2,18},{19,3},{3,19},{20,4},{4,... | collective-permute-start | bytes 493832 | tf_op jit(solution)/shard_map/ppermute | solution.py:265
  5.8 2.7 %collective-permute-start.8 = (bf16[8,128,128]{2,1,0:T(8,128)(2,1)S(1)}, bf16[8,128,128]{2,1,0:T(8,128)(2,1)S(1)}, u32[]{:S(2)}, u32[]{:S(2)}) collective-permute-start(bf16[8,128,128]{2,1,0:T(8,128)(2,1)S(1)} %get-tuple-element.105), channel_id=1, source_target_pairs={{0,8},{1,9},{2,10},{3,11},{4,12},{5,13},{6,14},{7,15},{8,0},{9,1},... | collective-permute-start | bytes 786440 | tf_op jit(solution)/shard_map/ppermute | solution.py:258
  9.3 1.6 %collective-permute-start.20 = (bf16[128,512]{0,1:T(8,128)(2,1)S(1)}, bf16[128,512]{0,1:T(8,128)(2,1)S(1)}, u32[]{:S(2)}, u32[]{:S(2)}) collective-permute-start(bf16[128,512]{0,1:T(8,128)(2,1)S(1)} %bitcast.46), channel_id=1, source_target_pairs={{16,0},{0,16},{17,1},{1,17},{18,2},{2,18},{19,3},{3,19},{20,4},{4,... | collective-permute-start | bytes 393224 | tf_op jit(solution)/shard_map/ppermute | solution.py:265
  13.0 1.3 %shard_map.73 = (bf16[2,256,128]{2,1,0:T(8,128)(2,1)S(1)}, bf16[2,256,128]{2,1,0:T(8,128)(2,1)S(1)}, bf16[2,256,128]{2,1,0:T(8,128)(2,1)S(1)}, bf16[2,256,128]{2...) custom-call(s32[3]{0:T(128)S(1)} %pad_add_fusion.here, ...), custom_call_target="tpu_custom_call" | custom-call | flops 167772160 | tf_op jit(solution)/shard_map/pallas_call | solution.py:217
  14.3 1.6 %collective-permute-start.1 = (bf16[2,256,128]{2,1,0:T(8,128)(2,1)S(1)}, bf16[2,256,128]{2,1,0:T(8,128)(2,1)S(1)}, u32[]{:S(2)}, u32[]{:S(2)}) collective-permute-start(bf16[2,256,128]{2,1,0:T(8,128)(2,1)S(1)} %get-tuple-element.56), channel_id=1, source_target_pairs={{0,2},{1,3},{2,0},{3,1},{4,6},{5,7},{6,4},{7,5},{8,10},{9,11},{10,... | collective-permute-start | bytes 393224 | tf_op jit(solution)/shard_map/ppermute | solution.py:238
  15.9 4.2 %collective-permute-done.8.pair = bf16[8,128,128]{2,1,0:T(8,128)(2,1)S(1)} collective-permute-done((bf16[8,128,128]{2,1,0:T(8,128)(2,1)S(1)}, bf16[8,128,128]{2,1,0:T(8,128)(2,1)S(1)}, u32[]{:S(2)}, u32[]{:S(2)}) %collective-permute-start.8) | collective-permute-done | bytes 262176 | tf_op jit(solution)/shard_map/ppermute | solution.py:258
  20.8 1.3 %shard_map.74 = (bf16[2,256,128]{2,1,0:T(8,128)(2,1)S(1)}, bf16[2,256,128]{2,1,0:T(8,128)(2,1)S(1)}, bf16[2,256,128]{2,1,0:T(8,128)(2,1)S(1)}, bf16[2,256,128]{2...) custom-call(s32[3]{0:T(128)S(1)} %pad_add_fusion.here, ...), custom_call_target="tpu_custom_call" | custom-call | flops 167772160 | tf_op jit(solution)/shard_map/pallas_call | solution.py:217
  22.1 2.4 %collective-permute-start.3 = (bf16[2,256,128]{2,1,0:T(8,128)(2,1)S(1)}, bf16[2,256,128]{2,1,0:T(8,128)(2,1)S(1)}, u32[]{:S(2)}, u32[]{:S(2)}) collective-permute-start(bf16[2,256,128]{2,1,0:T(8,128)(2,1)S(1)} %get-tuple-element.58), channel_id=1, source_target_pairs={{0,6},{1,7},{2,4},{3,5},{4,2},{5,3},{6,0},{7,1},{8,14},{9,15},{10,... | collective-permute-start | bytes 393224 | tf_op jit(solution)/shard_map/ppermute | solution.py:238
  25.9 2.3 %collective-permute-start.11 = (bf16[2,256,128]{2,1,0:T(8,128)(2,1)S(1)}, bf16[2,256,128]{2,1,0:T(8,128)(2,1)S(1)}, u32[]{:S(2)}, u32[]{:S(2)}) collective-permute-start(bf16[2,256,128]{2,1,0:T(8,128)(2,1)S(1)} %get-tuple-element.62), channel_id=1, source_target_pairs={{0,6},{1,7},{2,4},{3,5},{4,2},{5,3},{6,0},{7,1},{8,14},{9,15},{10,... | collective-permute-start | bytes 393224 | tf_op jit(solution)/shard_map/ppermute | solution.py:238
  29.5 2.9 %collective-permute-done.9.refs_9_ = bf16[2,256,128]{2,1,0:T(8,128)(2,1)S(1)} collective-permute-done((bf16[2,256,128]{2,1,0:T(8,128)(2,1)S(1)}, bf16[2,256,128]{2,1,0:T(8,128)(2,1)S(1)}, u32[]{:S(2)}, u32[]{:S(2)}) %collective-permute-start.9) | collective-permute-done | bytes 131104 | tf_op jit(solution)/shard_map/ppermute | solution.py:238
  32.9 1.7 %collective-permute-done.11.refs_11_ = bf16[2,256,128]{2,1,0:T(8,128)(2,1)S(1)} collective-permute-done((bf16[2,256,128]{2,1,0:T(8,128)(2,1)S(1)}, bf16[2,256,128]{2,1,0:T(8,128)(2,1)S(1)}, u32[]{:S(2)}, u32[]{:S(2)}) %collective-permute-start.11) | collective-permute-done | bytes 131104 | tf_op jit(solution)/shard_map/ppermute | solution.py:238
  36.4 1.5 %shard_map.75 = (bf16[256,128]{1,0:T(8,128)(2,1)S(1)}, bf16[256,128]{1,0:T(8,128)(2,1)S(1)}, bf16[256,128]{1,0:T(8,128)(2,1)S(1)}, bf16[256,128]{1,0:T(8,128)(2,...) custom-call(s32[3]{0:T(128)S(1)} %pad_add_fusion.here, ...), custom_call_target="tpu_custom_call" | custom-call | flops 67108864 | tf_op jit(solution)/shard_map/pallas_call | solution.py:217
  39.9 1.5 %collective-permute-start.18 = (bf16[256,128]{1,0:T(8,128)(2,1)S(1)}, bf16[256,128]{1,0:T(8,128)(2,1)S(1)}, u32[]{:S(2)}, u32[]{:S(2)}) collective-permute-start(bf16[256,128]{1,0:T(8,128)(2,1)S(1)} %get-tuple-element.66), channel_id=1, source_target_pairs={{0,6},{1,7},{2,4},{3,5},{4,2},{5,3},{6,0},{7,1},{8,14},{9,15},{10,... | collective-permute-start | bytes 196616 | tf_op jit(solution)/shard_map/ppermute | solution.py:238
  43.7 1.7 %collective-permute-done.18.refs_3_ = bf16[256,128]{1,0:T(8,128)(2,1)S(1)} collective-permute-done((bf16[256,128]{1,0:T(8,128)(2,1)S(1)}, bf16[256,128]{1,0:T(8,128)(2,1)S(1)}, u32[]{:S(2)}, u32[]{:S(2)}) %collective-permute-start.18) | collective-permute-done | bytes 65568 | tf_op jit(solution)/shard_map/ppermute | solution.py:238
  45.5 2.1 %shard_map.76 = (bf16[2,256,128]{2,1,0:T(8,128)(2,1)S(1)}, bf16[2,256,128]{2,1,0:T(8,128)(2,1)S(1)}, bf16[2,256,128]{2,1,0:T(8,128)(2,1)S(1)}, bf16[2,256,128]{2...) custom-call(s32[3]{0:T(128)S(1)} %pad_add_fusion.here, ...), custom_call_target="tpu_custom_call" | custom-call | flops 469762048 | tf_op jit(solution)/shard_map/pallas_call | solution.py:217
  47.7 1.4 %collective-permute-start.22 = (bf16[2,256,128]{2,1,0:T(8,128)(2,1)S(1)}, bf16[2,256,128]{2,1,0:T(8,128)(2,1)S(1)}, u32[]{:S(2)}, u32[]{:S(2)}) collective-permute-start(bf16[2,256,128]{2,1,0:T(8,128)(2,1)S(1)} %get-tuple-element.80), channel_id=1, source_target_pairs={{0,2},{1,3},{2,0},{3,1},{4,6},{5,7},{6,4},{7,5},{8,10},{9,11},{10,... | collective-permute-start | bytes 393224 | tf_op jit(solution)/shard_map/ppermute | solution.py:238
  51.2 1.7 %collective-permute-start.31 = (bf16[256,128]{1,0:T(8,128)(2,1)S(1)}, bf16[256,128]{1,0:T(8,128)(2,1)S(1)}, u32[]{:S(2)}, u32[]{:S(2)}) collective-permute-start(bf16[256,128]{1,0:T(8,128)(2,1)S(1)} %get-tuple-element.86), channel_id=1, source_target_pairs={{0,6},{1,7},{2,4},{3,5},{4,2},{5,3},{6,0},{7,1},{8,14},{9,15},{10,... | collective-permute-start | bytes 196616 | tf_op jit(solution)/shard_map/ppermute | solution.py:238
  53.0 4.7 %collective-permute-done.31.refs_3_ = bf16[256,128]{1,0:T(8,128)(2,1)S(1)} collective-permute-done((bf16[256,128]{1,0:T(8,128)(2,1)S(1)}, bf16[256,128]{1,0:T(8,128)(2,1)S(1)}, u32[]{:S(2)}, u32[]{:S(2)}) %collective-permute-start.31) | collective-permute-done | bytes 65568 | tf_op jit(solution)/shard_map/ppermute | solution.py:238
  57.7 2.1 %shard_map.77 = (bf16[2,256,128]{2,1,0:T(8,128)(2,1)S(1)}, bf16[2,256,128]{2,1,0:T(8,128)(2,1)S(1)}, bf16[2,256,128]{2,1,0:T(8,128)(2,1)S(1)}, bf16[2,256,128]{2...) custom-call(s32[3]{0:T(128)S(1)} %pad_add_fusion.here, ...), custom_call_target="tpu_custom_call" | custom-call | flops 469762048 | tf_op jit(solution)/shard_map/pallas_call | solution.py:217
  61.7 1.6 %collective-permute-start.34 = (bf16[2,256,128]{2,1,0:T(8,128)(2,1)S(1)}, bf16[2,256,128]{2,1,0:T(8,128)(2,1)S(1)}, u32[]{:S(2)}, u32[]{:S(2)}) collective-permute-start(bf16[2,256,128]{2,1,0:T(8,128)(2,1)S(1)} %get-tuple-element.92), channel_id=1, source_target_pairs={{0,6},{1,7},{2,4},{3,5},{4,2},{5,3},{6,0},{7,1},{8,14},{9,15},{10,... | collective-permute-start | bytes 393224 | tf_op jit(solution)/shard_map/ppermute | solution.py:238
  63.9 2.4 %collective-permute-done.32.refs_9_ = bf16[2,256,128]{2,1,0:T(8,128)(2,1)S(1)} collective-permute-done((bf16[2,256,128]{2,1,0:T(8,128)(2,1)S(1)}, bf16[2,256,128]{2,1,0:T(8,128)(2,1)S(1)}, u32[]{:S(2)}, u32[]{:S(2)}) %collective-permute-start.32) | collective-permute-done | bytes 131104 | tf_op jit(solution)/shard_map/ppermute | solution.py:238
  66.8 1.5 %collective-permute-done.34.refs_11_ = bf16[2,256,128]{2,1,0:T(8,128)(2,1)S(1)} collective-permute-done((bf16[2,256,128]{2,1,0:T(8,128)(2,1)S(1)}, bf16[2,256,128]{2,1,0:T(8,128)(2,1)S(1)}, u32[]{:S(2)}, u32[]{:S(2)}) %collective-permute-start.34) | collective-permute-done | bytes 131104 | tf_op jit(solution)/shard_map/ppermute | solution.py:238
  70.2 1.5 %shard_map.78 = (bf16[256,128]{1,0:T(8,128)(2,1)S(1)}, bf16[256,128]{1,0:T(8,128)(2,1)S(1)}, bf16[256,128]{1,0:T(8,128)(2,1)S(1)}, bf16[256,128]{1,0:T(8,128)(2,...) custom-call(s32[3]{0:T(128)S(1)} %pad_add_fusion.here, ...), custom_call_target="tpu_custom_call" | custom-call | flops 67108864 | tf_op jit(solution)/shard_map/pallas_call | solution.py:217
  71.7 1.4 %collective-permute-start.42 = (bf16[256,128]{1,0:T(8,128)(2,1)S(1)}, bf16[256,128]{1,0:T(8,128)(2,1)S(1)}, u32[]{:S(2)}, u32[]{:S(2)}) collective-permute-start(bf16[256,128]{1,0:T(8,128)(2,1)S(1)} %get-tuple-element.100), channel_id=1, source_target_pairs={{0,2},{1,3},{2,0},{3,1},{4,6},{5,7},{6,4},{7,5},{8,10},{9,11},{10,... | collective-permute-start | bytes 196616 | tf_op jit(solution)/shard_map/ppermute | solution.py:238
  76.0 2.0 %collective-permute-done.43.refs_2_ = bf16[256,128]{1,0:T(8,128)(2,1)S(1)} collective-permute-done((bf16[256,128]{1,0:T(8,128)(2,1)S(1)}, bf16[256,128]{1,0:T(8,128)(2,1)S(1)}, u32[]{:S(2)}, u32[]{:S(2)}) %collective-permute-start.43) | collective-permute-done | bytes 65568 | tf_op jit(solution)/shard_map/ppermute | solution.py:238
  79.2 1.6 %shard_map.80 = bf16[1,8,128,128]{3,2,1,0:T(8,128)(2,1)S(1)} custom-call(s32[3]{0:T(128)S(1)} %pad_add_fusion.here, bf16[256,128]{1,0:T(8,128)(2,1)S(1)} %get-tuple-element.99.refs_0_, bf16[256,128]{1,0:T(8,128)(2,1)S(1)} %collective-permute-done.42.refs_1_, bf16[256,128]{1,0:T(8,128)(2,1)S(1)} %collective-permute-done.43.refs_2_, ...), custom_call_target="tpu_custom_call" | custom-call | flops 301989888 | tf_op jit(solution)/shard_map/pallas_call | solution.py:217
  80.8 2.9 %collective-permute-start.45 = (bf16[1,8,128,128]{3,2,1,0:T(8,128)(2,1)S(1)}, bf16[1,8,128,128]{3,2,1,0:T(8,128)(2,1)S(1)}, u32[]{:S(2)}, u32[]{:S(2)}) collective-permute-start(bf16[1,8,128,128]{3,2,1,0:T(8,128)(2,1)S(1)} %shard_map.80), channel_id=1, source_target_pairs={{0,8},{1,9},{2,10},{3,11},{4,12},{5,13},{6,14},{7,15},{8,0},{9,1},... | collective-permute-start | bytes 786440 | tf_op jit(solution)/shard_map/ppermute | solution.py:258
  83.7 1.5 %collective-permute-start.39 = (bf16[256,128]{1,0:T(8,128)(2,1)S(1)}, bf16[256,128]{1,0:T(8,128)(2,1)S(1)}, u32[]{:S(2)}, u32[]{:S(2)}) collective-permute-start(bf16[256,128]{1,0:T(8,128)(2,1)S(1)} %get-tuple-element.94), channel_id=1, source_target_pairs={{0,2},{1,3},{2,0},{3,1},{4,6},{5,7},{6,4},{7,5},{8,10},{9,11},{10,... | collective-permute-start | bytes 196616 | tf_op jit(solution)/shard_map/ppermute | solution.py:238
  85.9 1.3 %collective-permute-start.41 = (bf16[256,128]{1,0:T(8,128)(2,1)S(1)}, bf16[256,128]{1,0:T(8,128)(2,1)S(1)}, u32[]{:S(2)}, u32[]{:S(2)}) collective-permute-start(bf16[256,128]{1,0:T(8,128)(2,1)S(1)} %get-tuple-element.96), channel_id=1, source_target_pairs={{0,6},{1,7},{2,4},{3,5},{4,2},{5,3},{6,0},{7,1},{8,14},{9,15},{10,... | collective-permute-start | bytes 196616 | tf_op jit(solution)/shard_map/ppermute | solution.py:238
  87.2 1.5 %collective-permute-done.39.refs_1_ = bf16[256,128]{1,0:T(8,128)(2,1)S(1)} collective-permute-done((bf16[256,128]{1,0:T(8,128)(2,1)S(1)}, bf16[256,128]{1,0:T(8,128)(2,1)S(1)}, u32[]{:S(2)}, u32[]{:S(2)}) %collective-permute-start.39) | collective-permute-done | bytes 65568 | tf_op jit(solution)/shard_map/ppermute | solution.py:238
  88.7 1.9 %collective-permute-done.40.refs_2_ = bf16[256,128]{1,0:T(8,128)(2,1)S(1)} collective-permute-done((bf16[256,128]{1,0:T(8,128)(2,1)S(1)}, bf16[256,128]{1,0:T(8,128)(2,1)S(1)}, u32[]{:S(2)}, u32[]{:S(2)}) %collective-permute-start.40) | collective-permute-done | bytes 65568 | tf_op jit(solution)/shard_map/ppermute | solution.py:238
  91.4 2.4 %shard_map.79 = bf16[2,8,128,128]{3,2,1,0:T(8,128)(2,1)} custom-call(s32[3]{0:T(128)S(1)} %pad_add_fusion.here, bf16[256,128]{1,0:T(8,128)(2,1)S(1)} %get-tuple-element.93.refs_0_, bf16[256,128]{1,0:T(8,128)(2,1)S(1)} %collective-permute-done.39.refs_1_, bf16[256,128]{1,0:T(8,128)(2,1)S(1)} %collective-permute-done.40.refs_2_, ...), custom_call_target="tpu_custom_call" | custom-call | flops 301989888 | tf_op jit(solution)/shard_map/pallas_call | solution.py:217
  (104 shorter events, 29.8 us)
Async XLA Ops:
  1.6 11.0 %collective-permute-start = (bf16[643,128]{1,0:T(8,128)(2,1)S(1)}, bf16[643,128]{1,0:T(8,128)(2,1)S(1)}, u32[]{:S(2)}, u32[]{:S(2)}) collective-permute-start(bf16[643,128]{1,0:T(8,128)(2,1)S(1)} %pad_maximum_fusion), channel_id=1, source_target_pairs={{16,0},{0,16},{17,1},{1,17},{18,2},{2,18},{19,3},{3,19},{20,4},{4,... | collective-permute-start | bytes 493832 | tf_op jit(solution)/shard_map/ppermute | solution.py:265
  5.8 14.3 %collective-permute-start.8 = (bf16[8,128,128]{2,1,0:T(8,128)(2,1)S(1)}, bf16[8,128,128]{2,1,0:T(8,128)(2,1)S(1)}, u32[]{:S(2)}, u32[]{:S(2)}) collective-permute-start(bf16[8,128,128]{2,1,0:T(8,128)(2,1)S(1)} %get-tuple-element.105), channel_id=1, source_target_pairs={{0,8},{1,9},{2,10},{3,11},{4,12},{5,13},{6,14},{7,15},{8,0},{9,1},... | collective-permute-start | bytes 786440 | tf_op jit(solution)/shard_map/ppermute | solution.py:258
  8.5 13.5 %collective-permute-start.19 = (bf16[128,128]{0,1:T(8,128)(2,1)S(1)}, bf16[128,128]{0,1:T(8,128)(2,1)S(1)}, u32[]{:S(2)}, u32[]{:S(2)}) collective-permute-start(bf16[128,128]{0,1:T(8,128)(2,1)S(1)} %bitcast.50), channel_id=1, source_target_pairs={{16,0},{0,16},{17,1},{1,17},{18,2},{2,18},{19,3},{3,19},{20,4},{4,... | collective-permute-start | bytes 98312 | tf_op jit(solution)/shard_map/ppermute | solution.py:265
  9.3 15.2 %collective-permute-start.20 = (bf16[128,512]{0,1:T(8,128)(2,1)S(1)}, bf16[128,512]{0,1:T(8,128)(2,1)S(1)}, u32[]{:S(2)}, u32[]{:S(2)}) collective-permute-start(bf16[128,512]{0,1:T(8,128)(2,1)S(1)} %bitcast.46), channel_id=1, source_target_pairs={{16,0},{0,16},{17,1},{1,17},{18,2},{2,18},{19,3},{3,19},{20,4},{4,... | collective-permute-start | bytes 393224 | tf_op jit(solution)/shard_map/ppermute | solution.py:265
  11.0 13.5 %collective-permute-start.21 = (bf16[512,128]{0,1:T(8,128)(2,1)S(1)}, bf16[512,128]{0,1:T(8,128)(2,1)S(1)}, u32[]{:S(2)}, u32[]{:S(2)}) collective-permute-start(bf16[512,128]{0,1:T(8,128)(2,1)S(1)} %bitcast.48), channel_id=1, source_target_pairs={{16,0},{0,16},{17,1},{1,17},{18,2},{2,18},{19,3},{3,19},{20,4},{4,... | collective-permute-start | bytes 393224 | tf_op jit(solution)/shard_map/ppermute | solution.py:265
  14.3 10.9 %collective-permute-start.1 = (bf16[2,256,128]{2,1,0:T(8,128)(2,1)S(1)}, bf16[2,256,128]{2,1,0:T(8,128)(2,1)S(1)}, u32[]{:S(2)}, u32[]{:S(2)}) collective-permute-start(bf16[2,256,128]{2,1,0:T(8,128)(2,1)S(1)} %get-tuple-element.56), channel_id=1, source_target_pairs={{0,2},{1,3},{2,0},{3,1},{4,6},{5,7},{6,4},{7,5},{8,10},{9,11},{10,... | collective-permute-start | bytes 393224 | tf_op jit(solution)/shard_map/ppermute | solution.py:238
  20.1 5.8 %collective-permute-start.2 = (bf16[2,256,128]{2,1,0:T(8,128)(2,1)S(1)}, bf16[2,256,128]{2,1,0:T(8,128)(2,1)S(1)}, u32[]{:S(2)}, u32[]{:S(2)}) collective-permute-start(bf16[2,256,128]{2,1,0:T(8,128)(2,1)S(1)} %get-tuple-element.57), channel_id=1, source_target_pairs={{0,4},{1,5},{2,6},{3,7},{4,0},{5,1},{6,2},{7,3},{8,12},{9,13},{10,... | collective-permute-start | bytes 393224 | tf_op jit(solution)/shard_map/ppermute | solution.py:238
  22.1 6.8 %collective-permute-start.3 = (bf16[2,256,128]{2,1,0:T(8,128)(2,1)S(1)}, bf16[2,256,128]{2,1,0:T(8,128)(2,1)S(1)}, u32[]{:S(2)}, u32[]{:S(2)}) collective-permute-start(bf16[2,256,128]{2,1,0:T(8,128)(2,1)S(1)} %get-tuple-element.58), channel_id=1, source_target_pairs={{0,6},{1,7},{2,4},{3,5},{4,2},{5,3},{6,0},{7,1},{8,14},{9,15},{10,... | collective-permute-start | bytes 393224 | tf_op jit(solution)/shard_map/ppermute | solution.py:238
  24.5 7.9 %collective-permute-start.9 = (bf16[2,256,128]{2,1,0:T(8,128)(2,1)S(1)}, bf16[2,256,128]{2,1,0:T(8,128)(2,1)S(1)}, u32[]{:S(2)}, u32[]{:S(2)}) collective-permute-start(bf16[2,256,128]{2,1,0:T(8,128)(2,1)S(1)} %get-tuple-element.60), channel_id=1, source_target_pairs={{0,2},{1,3},{2,0},{3,1},{4,6},{5,7},{6,4},{7,5},{8,10},{9,11},{10,... | collective-permute-start | bytes 393224 | tf_op jit(solution)/shard_map/ppermute | solution.py:238
  25.2 7.2 %collective-permute-start.10 = (bf16[2,256,128]{2,1,0:T(8,128)(2,1)S(1)}, bf16[2,256,128]{2,1,0:T(8,128)(2,1)S(1)}, u32[]{:S(2)}, u32[]{:S(2)}) collective-permute-start(bf16[2,256,128]{2,1,0:T(8,128)(2,1)S(1)} %get-tuple-element.61), channel_id=1, source_target_pairs={{0,4},{1,5},{2,6},{3,7},{4,0},{5,1},{6,2},{7,3},{8,12},{9,13},{10,... | collective-permute-start | bytes 393224 | tf_op jit(solution)/shard_map/ppermute | solution.py:238
  25.9 8.7 %collective-permute-start.11 = (bf16[2,256,128]{2,1,0:T(8,128)(2,1)S(1)}, bf16[2,256,128]{2,1,0:T(8,128)(2,1)S(1)}, u32[]{:S(2)}, u32[]{:S(2)}) collective-permute-start(bf16[2,256,128]{2,1,0:T(8,128)(2,1)S(1)} %get-tuple-element.62), channel_id=1, source_target_pairs={{0,6},{1,7},{2,4},{3,5},{4,2},{5,3},{6,0},{7,1},{8,14},{9,15},{10,... | collective-permute-start | bytes 393224 | tf_op jit(solution)/shard_map/ppermute | solution.py:238
  28.9 5.6 %collective-permute-start.12 = (bf16[2,256,128]{2,1,0:T(8,128)(2,1)S(1)}, bf16[2,256,128]{2,1,0:T(8,128)(2,1)S(1)}, u32[]{:S(2)}, u32[]{:S(2)}) collective-permute-start(bf16[2,256,128]{2,1,0:T(8,128)(2,1)S(1)} %get-tuple-element.59.refs_8_), channel_id=1, source_target_pairs={{0,1},{1,0},{2,3},{3,2},{4,5},{5,4},{6,7},{7,6},{8,9},{9,8},{10,11... | collective-permute-start | bytes 393224 | tf_op jit(solution)/shard_map/ppermute | solution.py:247
  28.9 6.1 %collective-permute-start.5 = (bf16[2,256,128]{2,1,0:T(8,128)(2,1)S(1)}, bf16[2,256,128]{2,1,0:T(8,128)(2,1)S(1)}, u32[]{:S(2)}, u32[]{:S(2)}) collective-permute-start(bf16[2,256,128]{2,1,0:T(8,128)(2,1)S(1)} %collective-permute-done.1.refs_1_), channel_id=1, source_target_pairs={{0,1},{1,0},{2,3},{3,2},{4,5},{5,4},{6,7},{7,6},{8,9},{9,8},{10,11... | collective-permute-start | bytes 393224 | tf_op jit(solution)/shard_map/ppermute | solution.py:247
  37.9 5.7 %collective-permute-start.16 = (bf16[256,128]{1,0:T(8,128)(2,1)S(1)}, bf16[256,128]{1,0:T(8,128)(2,1)S(1)}, u32[]{:S(2)}, u32[]{:S(2)}) collective-permute-start(bf16[256,128]{1,0:T(8,128)(2,1)S(1)} %get-tuple-element.64), channel_id=1, source_target_pairs={{0,2},{1,3},{2,0},{3,1},{4,6},{5,7},{6,4},{7,5},{8,10},{9,11},{10,... | collective-permute-start | bytes 196616 | tf_op jit(solution)/shard_map/ppermute | solution.py:238
  39.9 5.5 %collective-permute-start.18 = (bf16[256,128]{1,0:T(8,128)(2,1)S(1)}, bf16[256,128]{1,0:T(8,128)(2,1)S(1)}, u32[]{:S(2)}, u32[]{:S(2)}) collective-permute-start(bf16[256,128]{1,0:T(8,128)(2,1)S(1)} %get-tuple-element.66), channel_id=1, source_target_pairs={{0,6},{1,7},{2,4},{3,5},{4,2},{5,3},{6,0},{7,1},{8,14},{9,15},{10,... | collective-permute-start | bytes 196616 | tf_op jit(solution)/shard_map/ppermute | solution.py:238
  41.5 9.7 %collective-permute-start.29 = (bf16[256,128]{1,0:T(8,128)(2,1)S(1)}, bf16[256,128]{1,0:T(8,128)(2,1)S(1)}, u32[]{:S(2)}, u32[]{:S(2)}) collective-permute-start(bf16[256,128]{1,0:T(8,128)(2,1)S(1)} %get-tuple-element.84), channel_id=1, source_target_pairs={{0,2},{1,3},{2,0},{3,1},{4,6},{5,7},{6,4},{7,5},{8,10},{9,11},{10,... | collective-permute-start | bytes 196616 | tf_op jit(solution)/shard_map/ppermute | solution.py:238
  42.4 8.8 %collective-permute-start.30 = (bf16[256,128]{1,0:T(8,128)(2,1)S(1)}, bf16[256,128]{1,0:T(8,128)(2,1)S(1)}, u32[]{:S(2)}, u32[]{:S(2)}) collective-permute-start(bf16[256,128]{1,0:T(8,128)(2,1)S(1)} %get-tuple-element.85), channel_id=1, source_target_pairs={{0,4},{1,5},{2,6},{3,7},{4,0},{5,1},{6,2},{7,3},{8,12},{9,13},{10,... | collective-permute-start | bytes 196616 | tf_op jit(solution)/shard_map/ppermute | solution.py:238
  47.7 12.9 %collective-permute-start.22 = (bf16[2,256,128]{2,1,0:T(8,128)(2,1)S(1)}, bf16[2,256,128]{2,1,0:T(8,128)(2,1)S(1)}, u32[]{:S(2)}, u32[]{:S(2)}) collective-permute-start(bf16[2,256,128]{2,1,0:T(8,128)(2,1)S(1)} %get-tuple-element.80), channel_id=1, source_target_pairs={{0,2},{1,3},{2,0},{3,1},{4,6},{5,7},{6,4},{7,5},{8,10},{9,11},{10,... | collective-permute-start | bytes 393224 | tf_op jit(solution)/shard_map/ppermute | solution.py:238
  49.1 12.6 %collective-permute-start.23 = (bf16[2,256,128]{2,1,0:T(8,128)(2,1)S(1)}, bf16[2,256,128]{2,1,0:T(8,128)(2,1)S(1)}, u32[]{:S(2)}, u32[]{:S(2)}) collective-permute-start(bf16[2,256,128]{2,1,0:T(8,128)(2,1)S(1)} %get-tuple-element.81), channel_id=1, source_target_pairs={{0,4},{1,5},{2,6},{3,7},{4,0},{5,1},{6,2},{7,3},{8,12},{9,13},{10,... | collective-permute-start | bytes 393224 | tf_op jit(solution)/shard_map/ppermute | solution.py:238
  49.9 13.4 %collective-permute-start.24 = (bf16[2,256,128]{2,1,0:T(8,128)(2,1)S(1)}, bf16[2,256,128]{2,1,0:T(8,128)(2,1)S(1)}, u32[]{:S(2)}, u32[]{:S(2)}) collective-permute-start(bf16[2,256,128]{2,1,0:T(8,128)(2,1)S(1)} %get-tuple-element.82), channel_id=1, source_target_pairs={{0,6},{1,7},{2,4},{3,5},{4,2},{5,3},{6,0},{7,1},{8,14},{9,15},{10,... | collective-permute-start | bytes 393224 | tf_op jit(solution)/shard_map/ppermute | solution.py:238
  51.2 12.1 %collective-permute-start.25 = (bf16[2,256,128]{2,1,0:T(8,128)(2,1)S(1)}, bf16[2,256,128]{2,1,0:T(8,128)(2,1)S(1)}, u32[]{:S(2)}, u32[]{:S(2)}) collective-permute-start(bf16[2,256,128]{2,1,0:T(8,128)(2,1)S(1)} %get-tuple-element.79.refs_0_), channel_id=1, source_target_pairs={{0,1},{1,0},{2,3},{3,2},{4,5},{5,4},{6,7},{7,6},{8,9},{9,8},{10,11... | collective-permute-start | bytes 393224 | tf_op jit(solution)/shard_map/ppermute | solution.py:247
  51.2 6.4 %collective-permute-start.31 = (bf16[256,128]{1,0:T(8,128)(2,1)S(1)}, bf16[256,128]{1,0:T(8,128)(2,1)S(1)}, u32[]{:S(2)}, u32[]{:S(2)}) collective-permute-start(bf16[256,128]{1,0:T(8,128)(2,1)S(1)} %get-tuple-element.86), channel_id=1, source_target_pairs={{0,6},{1,7},{2,4},{3,5},{4,2},{5,3},{6,0},{7,1},{8,14},{9,15},{10,... | collective-permute-start | bytes 196616 | tf_op jit(solution)/shard_map/ppermute | solution.py:238
  59.8 6.4 %collective-permute-start.32 = (bf16[2,256,128]{2,1,0:T(8,128)(2,1)S(1)}, bf16[2,256,128]{2,1,0:T(8,128)(2,1)S(1)}, u32[]{:S(2)}, u32[]{:S(2)}) collective-permute-start(bf16[2,256,128]{2,1,0:T(8,128)(2,1)S(1)} %get-tuple-element.90), channel_id=1, source_target_pairs={{0,2},{1,3},{2,0},{3,1},{4,6},{5,7},{6,4},{7,5},{8,10},{9,11},{10,... | collective-permute-start | bytes 393224 | tf_op jit(solution)/shard_map/ppermute | solution.py:238
  60.5 6.3 %collective-permute-start.33 = (bf16[2,256,128]{2,1,0:T(8,128)(2,1)S(1)}, bf16[2,256,128]{2,1,0:T(8,128)(2,1)S(1)}, u32[]{:S(2)}, u32[]{:S(2)}) collective-permute-start(bf16[2,256,128]{2,1,0:T(8,128)(2,1)S(1)} %get-tuple-element.91), channel_id=1, source_target_pairs={{0,4},{1,5},{2,6},{3,7},{4,0},{5,1},{6,2},{7,3},{8,12},{9,13},{10,... | collective-permute-start | bytes 393224 | tf_op jit(solution)/shard_map/ppermute | solution.py:238
  61.7 6.6 %collective-permute-start.34 = (bf16[2,256,128]{2,1,0:T(8,128)(2,1)S(1)}, bf16[2,256,128]{2,1,0:T(8,128)(2,1)S(1)}, u32[]{:S(2)}, u32[]{:S(2)}) collective-permute-start(bf16[2,256,128]{2,1,0:T(8,128)(2,1)S(1)} %get-tuple-element.92), channel_id=1, source_target_pairs={{0,6},{1,7},{2,4},{3,5},{4,2},{5,3},{6,0},{7,1},{8,14},{9,15},{10,... | collective-permute-start | bytes 393224 | tf_op jit(solution)/shard_map/ppermute | solution.py:238
  63.4 5.0 %collective-permute-start.35 = (bf16[2,256,128]{2,1,0:T(8,128)(2,1)S(1)}, bf16[2,256,128]{2,1,0:T(8,128)(2,1)S(1)}, u32[]{:S(2)}, u32[]{:S(2)}) collective-permute-start(bf16[2,256,128]{2,1,0:T(8,128)(2,1)S(1)} %get-tuple-element.89.refs_8_), channel_id=1, source_target_pairs={{0,1},{1,0},{2,3},{3,2},{4,5},{5,4},{6,7},{7,6},{8,9},{9,8},{10,11... | collective-permute-start | bytes 393224 | tf_op jit(solution)/shard_map/ppermute | solution.py:247
  63.4 5.5 %collective-permute-start.26 = (bf16[2,256,128]{2,1,0:T(8,128)(2,1)S(1)}, bf16[2,256,128]{2,1,0:T(8,128)(2,1)S(1)}, u32[]{:S(2)}, u32[]{:S(2)}) collective-permute-start(bf16[2,256,128]{2,1,0:T(8,128)(2,1)S(1)} %collective-permute-done.22.refs_1_), channel_id=1, source_target_pairs={{0,1},{1,0},{2,3},{3,2},{4,5},{5,4},{6,7},{7,6},{8,9},{9,8},{10,11... | collective-permute-start | bytes 393224 | tf_op jit(solution)/shard_map/ppermute | solution.py:247
  74.0 5.2 %collective-permute-start.44 = (bf16[256,128]{1,0:T(8,128)(2,1)S(1)}, bf16[256,128]{1,0:T(8,128)(2,1)S(1)}, u32[]{:S(2)}, u32[]{:S(2)}) collective-permute-start(bf16[256,128]{1,0:T(8,128)(2,1)S(1)} %get-tuple-element.102), channel_id=1, source_target_pairs={{0,6},{1,7},{2,4},{3,5},{4,2},{5,3},{6,0},{7,1},{8,14},{9,15},{10,... | collective-permute-start | bytes 196616 | tf_op jit(solution)/shard_map/ppermute | solution.py:238
  80.8 14.0 %collective-permute-start.45 = (bf16[1,8,128,128]{3,2,1,0:T(8,128)(2,1)S(1)}, bf16[1,8,128,128]{3,2,1,0:T(8,128)(2,1)S(1)}, u32[]{:S(2)}, u32[]{:S(2)}) collective-permute-start(bf16[1,8,128,128]{3,2,1,0:T(8,128)(2,1)S(1)} %shard_map.80), channel_id=1, source_target_pairs={{0,8},{1,9},{2,10},{3,11},{4,12},{5,13},{6,14},{7,15},{8,0},{9,1},... | collective-permute-start | bytes 786440 | tf_op jit(solution)/shard_map/ppermute | solution.py:258
  83.7 5.0 %collective-permute-start.39 = (bf16[256,128]{1,0:T(8,128)(2,1)S(1)}, bf16[256,128]{1,0:T(8,128)(2,1)S(1)}, u32[]{:S(2)}, u32[]{:S(2)}) collective-permute-start(bf16[256,128]{1,0:T(8,128)(2,1)S(1)} %get-tuple-element.94), channel_id=1, source_target_pairs={{0,2},{1,3},{2,0},{3,1},{4,6},{5,7},{6,4},{7,5},{8,10},{9,11},{10,... | collective-permute-start | bytes 196616 | tf_op jit(solution)/shard_map/ppermute | solution.py:238
  85.2 5.4 %collective-permute-start.40 = (bf16[256,128]{1,0:T(8,128)(2,1)S(1)}, bf16[256,128]{1,0:T(8,128)(2,1)S(1)}, u32[]{:S(2)}, u32[]{:S(2)}) collective-permute-start(bf16[256,128]{1,0:T(8,128)(2,1)S(1)} %get-tuple-element.95), channel_id=1, source_target_pairs={{0,4},{1,5},{2,6},{3,7},{4,0},{5,1},{6,2},{7,3},{8,12},{9,13},{10,... | collective-permute-start | bytes 196616 | tf_op jit(solution)/shard_map/ppermute | solution.py:238
  85.9 5.5 %collective-permute-start.41 = (bf16[256,128]{1,0:T(8,128)(2,1)S(1)}, bf16[256,128]{1,0:T(8,128)(2,1)S(1)}, u32[]{:S(2)}, u32[]{:S(2)}) collective-permute-start(bf16[256,128]{1,0:T(8,128)(2,1)S(1)} %get-tuple-element.96), channel_id=1, source_target_pairs={{0,6},{1,7},{2,4},{3,5},{4,2},{5,3},{6,0},{7,1},{8,14},{9,15},{10,... | collective-permute-start | bytes 196616 | tf_op jit(solution)/shard_map/ppermute | solution.py:238
  (20 other events, 52.7 us)
